TPU v7x, 512 devices: a whole 4x4x16 slice. The times are simulated.
512 devices in a mesh: seqa: 16 (over z_lo, core), seqb: 8 (over x, z_hi), dp: 4 (over y).
Axes of the slice: x: 4, y: 4, z: 16 (z_hi: 2, z_lo: 8; z = z_hi * 8 + z_lo), core: 2. Of those that a mesh axis runs over, the one named last changes fastest.
Arguments:
- queries: bfloat16 [16384, 128, 64], P(('dp', 'seqa', 'seqb')), parts along dimension 0, may hold values from -6 to 6
- keys: bfloat16 [16384, 128, 64], P(('dp', 'seqa', 'seqb')), parts along dimension 0, may hold values from -6 to 6
- values: bfloat16 [16384, 128, 64], P(('dp', 'seqa', 'seqb')), parts along dimension 0, may hold values from -6 to 6
- doc_bounds: int32 [36], P('dp'), parts along dimension 0, may hold values from 0 to 4096, as said below
- q_gain: float32 [64], replicated, may hold values from 0.25 to 1.75
- k_gain: float32 [64], replicated, may hold values from 0.25 to 1.75
Outputs:
- attended: bfloat16 [16384, 128, 64], P(('dp', 'seqa', 'seqb')), parts along dimension 0
There are 4 independent parts, one for each index of `dp`. A program takes and returns all parts, laid end to end along the dimension named above; an argument that names none is the same for every part. Nothing has to cross between parts.
Inputs may be any that keep to these rules, and one draw needn't show every extreme that they name: doc_bounds[0] is 0, doc_bounds[8] is 4096, and the entries rise strictly.
All inputs are finite; a program needn't handle non-finite values.
Results may differ from a plain program's by a relative error of at most 0.0015.
Values may be sent and summed in bfloat16 or wider, within the bound.
No kernel may reach another device: no remote copies, remote signals or barrier semaphores. Data moves between devices by JAX's collectives and lax.ppermute only.
A program may use at most 64 MiB of HBM per device.

v0:
```python
import jax
import jax.numpy as jnp
from jax import lax
from jax.sharding import PartitionSpec as P

TOK_DEV = 32
DOCS = 8


def for_sending(value):
    return jax.tree.map(lambda a: a.astype(jnp.bfloat16) if a.dtype == jnp.float32 else a, value)


def prepare(block, gain, positions):
    values32 = block.astype(jnp.float32)
    scale = lax.rsqrt(jnp.mean(values32 * values32, axis=-1, keepdims=True) + 1e-06)
    normed = values32 * scale * gain
    half = normed.shape[-1] // 2
    freq = jnp.exp(-jnp.log(10000.0) * jnp.arange(half, dtype=jnp.float32) * 2.0 / normed.shape[-1])
    angle = positions.astype(jnp.float32)[:, None] * freq[None, :]
    first = normed[:, :half]
    second = normed[:, half:]
    cosine = jnp.cos(angle)
    sine = jnp.sin(angle)
    rotated = jnp.concatenate(
        [first * cosine - second * sine, first * sine + second * cosine], axis=-1
    )
    return rotated.astype(jnp.bfloat16)


def attend_head(query_head, key_head, value_head, doc_bounds, q_gain, k_gain):
    length, width = query_head.shape
    places = jnp.arange(length, dtype=jnp.int32)
    doc = jnp.sum((places[:, None] >= doc_bounds[None, 1:DOCS]).astype(jnp.int32), axis=1).astype(
        jnp.int32
    )
    positions = places - doc_bounds[doc]
    qr = prepare(query_head, q_gain, positions)
    kr = prepare(key_head, k_gain, positions)
    block = 8 * TOK_DEV
    count = length // block

    def one_block(items):
        query_rows, query_doc, query_place = items
        scores = jnp.dot(query_rows, kr.T, preferred_element_type=jnp.float32) / jnp.sqrt(
            jnp.float32(width)
        )
        allowed = (query_doc[:, None] == doc[None, :]) & (places[None, :] <= query_place[:, None])
        scores = jnp.where(allowed, scores, jnp.float32(-1e30))
        top = jnp.max(scores, axis=1, keepdims=True)
        expo = jnp.where(allowed, jnp.exp(scores - top), jnp.float32(0.0))
        weights = (expo / jnp.sum(expo, axis=1, keepdims=True)).astype(jnp.bfloat16)
        return jnp.dot(weights, value_head, preferred_element_type=jnp.float32).astype(jnp.bfloat16)

    outputs = lax.map(
        one_block,
        (qr.reshape(count, block, width), doc.reshape(count, block), places.reshape(count, block)),
    )
    return outputs.reshape(length, width)


def body(queries, keys, values, doc_bounds, q_gain, k_gain):
    query_full, key_full, value_full = (
        lax.all_to_all(queries, ("seqa", "seqb"), split_axis=1, concat_axis=0, tiled=True),
        lax.all_to_all(keys, ("seqa", "seqb"), split_axis=1, concat_axis=0, tiled=True),
        lax.all_to_all(values, ("seqa", "seqb"), split_axis=1, concat_axis=0, tiled=True),
    )
    attend_all = jax.vmap(attend_head, in_axes=(1, 1, 1, None, None, None), out_axes=1)
    result = attend_all(query_full, key_full, value_full, doc_bounds, q_gain, k_gain)
    back = jax.tree.map(
        lambda part, own: part.astype(own.dtype),
        lax.all_to_all(
            for_sending(result), ("seqa", "seqb"), split_axis=0, concat_axis=1, tiled=True
        ),
        result,
    )
    return back


def solution(mesh):
    placed = (
        P(("dp", "seqa", "seqb"), None, None),
        P(("dp", "seqa", "seqb"), None, None),
        P(("dp", "seqa", "seqb"), None, None),
        P("dp"),
        P(),
        P(),
    )
    return jax.shard_map(
        body,
        mesh=mesh,
        in_specs=placed,
        out_specs=P(("dp", "seqa", "seqb"), None, None),
        check_vma=False,
    )
```

profile of v0, /device:TPU:1, one launch (start us, length us, event | category | flops | bytes accessed | tf_op | source)
XLA Modules:
  0.0 308.2 jit_solution(3583680308432293283)
XLA Ops:
  0.0 2.5 copy.59
  3.9 20.4 %all-to-all-start = ((bf16[128,2,1024]{2,1,0:T(2,128)(2,1)}), bf16[128,2,1024]{2,1,0:T(2,128)(2,1)S(1)}, u32[]{:S(2)}, u32[]{:S(2)}) async-start(bf16[128,2,1024]{2,1,0:T(2,128)(2,1)} %reshape.490), calls=%async_computation | async-start | bytes 1048576 | tf_op jit(solution)/shard_map/all_to_all | solution.py:64
  27.5 31.3 %all-to-all-done = bf16[128,2,1024]{2,1,0:T(2,128)(2,1)S(1)} async-done(((bf16[128,2,1024]{2,1,0:T(2,128)(2,1)}), bf16[128,2,1024]{2,1,0:T(2,128)(2,1)S(1)}, u32[]{:S(2)}, u32[]{:S(2)}) %all-to-all-start) | async-done | bytes 524320 | tf_op jit(solution)/shard_map/all_to_all | solution.py:64
  58.8 6.4 %all-to-all-start.1 = ((bf16[128,2,1024]{2,1,0:T(2,128)(2,1)}), bf16[128,2,1024]{2,1,0:T(2,128)(2,1)}, u32[]{:S(2)}, u32[]{:S(2)}) async-start(bf16[128,2,1024]{2,1,0:T(2,128)(2,1)} %reshape.492), calls=%async_computation.1 | async-start | bytes 1048576 | tf_op jit(solution)/shard_map/all_to_all | solution.py:65
  69.1 4.6 %compare_select_fusion.1 = (s32[4096,1]{0,1:T(1,128)S(1)}, s32[4096,1]{0,1:T(1,128)S(1)}) fusion(s32[]{:T(128)} %bitcast.7, s32[]{:T(128)} %bitcast.8, s32[]{:T(128)} %bitcast.9, s32[]{:T(128)} %bitcast.10, s32[]{:T(128)} %bitcast.11, s32[]{:T(128)} %bitcast.13, s32[]{:T(128)} %bitcast.12, s32[4096,1]{0,1:T(1,128)S(1)} %bitcast.90), kind=kLoop, calls=%fused_computation.49 | loop fusion | flops 61440 | bytes 49180 | tf_op jit(solution)/shard_map/vmap()/gather | solution.py:37
  76.7 20.9 %all-to-all-done.1 = bf16[128,2,1024]{2,1,0:T(2,128)(2,1)} async-done(((bf16[128,2,1024]{2,1,0:T(2,128)(2,1)}), bf16[128,2,1024]{2,1,0:T(2,128)(2,1)}, u32[]{:S(2)}, u32[]{:S(2)}) %all-to-all-start.1) | async-done | bytes 524320 | tf_op jit(solution)/shard_map/all_to_all | solution.py:65
  97.5 6.6 %all-to-all-start.2 = ((bf16[128,2,1024]{2,1,0:T(2,128)(2,1)}), bf16[128,2,1024]{2,1,0:T(2,128)(2,1)}, u32[]{:S(2)}, u32[]{:S(2)}) async-start(bf16[128,2,1024]{2,1,0:T(2,128)(2,1)} %reshape.494), calls=%async_computation.2 | async-start | bytes 1048576 | tf_op jit(solution)/shard_map/all_to_all | solution.py:66
  112.4 2.4 fusion.28
  117.7 19.6 %all-to-all-done.2 = bf16[128,2,1024]{2,1,0:T(2,128)(2,1)} async-done(((bf16[128,2,1024]{2,1,0:T(2,128)(2,1)}), bf16[128,2,1024]{2,1,0:T(2,128)(2,1)}, u32[]{:S(2)}, u32[]{:S(2)}) %all-to-all-start.2) | async-done | bytes 524320 | tf_op jit(solution)/shard_map/all_to_all | solution.py:66
  139.6 99.7 %while.11 = (s32[]{:T(128)}, bf16[16,1,256,64]{2,3,1,0:T(8,128)(2,1)}, s32[16,256]{1,0:T(8,128)S(1)}, s32[4096]{0:T(1024)S(1)}, s32[16,256]{1,0:T(8,128)S(1)}, /...) while((s32[]{:T(128)}, ...), condition=%wide.region_6.7_spmd.clone, body=%wide.region_3.6_spmd.clone.sunk | while | flops 288374272 | bytes 13794917 | solution.py:55
  139.6 2.5 fusion.39
  145.9 2.5 fusion.39
  149.8 2.3 fusion.41
  152.1 2.5 fusion.39
  158.3 2.5 fusion.39
  162.2 2.3 fusion.41
  164.6 2.5 fusion.39
  170.8 2.5 fusion.39
  174.7 2.3 fusion.41
  177.0 2.5 fusion.39
  183.3 2.5 fusion.39
  187.2 2.3 fusion.41
  189.5 2.5 fusion.39
  195.7 2.5 fusion.39
  202.0 2.5 fusion.39
  208.2 2.5 fusion.39
  214.4 2.5 fusion.39
  220.7 2.5 fusion.39
  226.9 2.5 fusion.39
  233.1 2.5 fusion.39
  241.9 22.6 %reduce.16 = bf16[4096,64]{1,0:T(8,128)(2,1)S(1)} reduce(bf16[4096,1,64]{2,1,0:T(2,128)(2,1)S(1)} %reshape.484, bf16[]{:T(256)} %broadcast.313), dimensions={1}, to_apply=%reshape.484.reduce_sub_computation | reduce | bytes 1048578 | tf_op jit(solution)/shard_map/vmap()/transpose;vmap()/reshape;vmap()/transpose | solution.py:69
  265.1 39.9 %all_to_all.51 = bf16[128,2,1024]{2,1,0:T(2,128)(2,1)S(1)} all-to-all(bf16[128,2,1024]{2,1,0:T(2,128)(2,1)S(1)} %reshape.496), channel_id=1, replica_groups=mesh['seqa'=16,'seqb'=8,'dp'=4] {'seqa','seqb'}, dimensions={0} | all-to-all | bytes 1048576 | tf_op jit(solution)/shard_map/all_to_all | solution.py:72
  (98 shorter events, 80.8 us)
Async XLA Ops:
  0.0 24.3 %copy-start.2 = (s32[9]{0:T(128)S(1)}, s32[9]{0:T(128)}, u32[]{:S(2)}) copy-start(s32[9]{0:T(128)} %param.11) | copy-start | bytes 112
  0.0 24.4 %copy-start = (bf16[32,128,64]{1,2,0:T(8,128)(2,1)S(1)}, bf16[32,128,64]{1,2,0:T(8,128)(2,1)}, u32[]{:S(2)}) copy-start(bf16[32,128,64]{1,2,0:T(8,128)(2,1)} %param.9) | copy-start | bytes 1572868
  0.0 65.4 %copy-start.1 = (bf16[32,128,64]{1,2,0:T(8,128)(2,1)S(1)}, bf16[32,128,64]{1,2,0:T(8,128)(2,1)}, u32[]{:S(2)}) copy-start(bf16[32,128,64]{1,2,0:T(8,128)(2,1)} %param.10) | copy-start | bytes 1572868
  3.9 54.9 %all-to-all-start = ((bf16[128,2,1024]{2,1,0:T(2,128)(2,1)}), bf16[128,2,1024]{2,1,0:T(2,128)(2,1)S(1)}, u32[]{:S(2)}, u32[]{:S(2)}) async-start(bf16[128,2,1024]{2,1,0:T(2,128)(2,1)} %reshape.490), calls=%async_computation | async-start | bytes 1048576 | tf_op jit(solution)/shard_map/all_to_all | solution.py:64
  58.8 38.7 %all-to-all-start.1 = ((bf16[128,2,1024]{2,1,0:T(2,128)(2,1)}), bf16[128,2,1024]{2,1,0:T(2,128)(2,1)}, u32[]{:S(2)}, u32[]{:S(2)}) async-start(bf16[128,2,1024]{2,1,0:T(2,128)(2,1)} %reshape.492), calls=%async_computation.1 | async-start | bytes 1048576 | tf_op jit(solution)/shard_map/all_to_all | solution.py:65
  97.5 39.8 %all-to-all-start.2 = ((bf16[128,2,1024]{2,1,0:T(2,128)(2,1)}), bf16[128,2,1024]{2,1,0:T(2,128)(2,1)}, u32[]{:S(2)}, u32[]{:S(2)}) async-start(bf16[128,2,1024]{2,1,0:T(2,128)(2,1)} %reshape.494), calls=%async_computation.2 | async-start | bytes 1048576 | tf_op jit(solution)/shard_map/all_to_all | solution.py:66
  108.1 3.9 %copy-start.3 = (f32[64]{0:T(128)S(1)}, f32[64]{0:T(128)}, u32[]{:S(2)}) copy-start(f32[64]{0:T(128)} %param.13) | copy-start | bytes 772
  108.1 4.0 %copy-start.4 = (f32[64]{0:T(128)S(1)}, f32[64]{0:T(128)}, u32[]{:S(2)}) copy-start(f32[64]{0:T(128)} %param.12) | copy-start | bytes 772
where the time goes:
time: 309 us; the launch traced here: 308 us
  matrix products  77.5 us (25%)
  waiting for transfers between devices  71.8 us (23%)
  other arithmetic  57.5 us (19%)
  blocking collectives  39.9 us (13%)
  starting transfers between devices  33.4 us (11%)
  local copies, waits for them, and re-layouts  27.8 us (9%)
    dot_general x16, matrix products, one_block(): jnp.dot(query_rows, kr.T, preferred_element_type=jnp.float32)  40.5 us
    all_to_all x1, blocking collectives, body(): lax.all_to_all(for_sending(result), ('seqa', 'seqb'), split_axis=0, conca...  39.9 us
    dot_general x16, matrix products, one_block(): jnp.dot(weights, value_head, preferred_element_type=jnp.float32)  37 us
    all_to_all x1, waiting for transfers between devices, body(): lax.all_to_all(queries, ('seqa', 'seqb'), split_axis=1, concat_axis=0, ti...  31.3 us
    transpose x1, other arithmetic, body(): attend_all(query_full, key_full, value_full, doc_bounds, q_gain, k_gain)  22.6 us
    reduce_sum x16, other arithmetic, one_block(): weights = (expo / jnp.sum(expo, axis=1, keepdims=True)).astype(jnp.bfloat16)  22.1 us
    all_to_all x1, waiting for transfers between devices, body(): lax.all_to_all(keys, ('seqa', 'seqb'), split_axis=1, concat_axis=0, tiled...  20.9 us
    all_to_all x1, starting transfers between devices, body(): lax.all_to_all(queries, ('seqa', 'seqb'), split_axis=1, concat_axis=0, ti...  20.4 us
  transfers between devices with their start and end apart: 3, of which 3 were waited for; matrix products, arithmetic and copies ran while one was open for 9% of the time, Pallas kernels for 0%

commit v1 on v0

v1 whole, which is shorter than its diff:
```python
import functools

import jax
import jax.numpy as jnp
from jax import lax
from jax.experimental import pallas as pl
from jax.experimental.pallas import tpu as pltpu
from jax.sharding import PartitionSpec as P

AXES = ("seqa", "seqb")
TOK = 32
HALF_TOK = 16
HD = 64
HEADS = 128
DOCS = 8
SEQ = 4096
BLK = 256
PAIRS = BLK // 2
NBLK = SEQ // BLK
SRC = BLK // TOK
NT = (((1,), (1,)), ((), ()))
NN = (((1,), (0,)), ((), ()))
SCALE = 1.4426950408889634 / 8.0
FIRST = -9.210340371976184


def dot(a, b, dims):
    return lax.dot_general(a, b, dims, preferred_element_type=jnp.float32)


def starts_of(token, bounds_ref):
    start = jnp.zeros_like(token)
    for d in range(1, DOCS):
        start = jnp.where(token >= bounds_ref[d], bounds_ref[d], start)
    return start


def identity(n):
    return (
        lax.broadcasted_iota(jnp.int32, (n, n), 0) == lax.broadcasted_iota(jnp.int32, (n, n), 1)
    ).astype(jnp.float32).astype(jnp.bfloat16)


def interleave():
    row = lax.broadcasted_iota(jnp.int32, (256, 256), 0)
    col = lax.broadcasted_iota(jnp.int32, (256, 256), 1)
    return (col == (row % 16) * 16 + row // 16).astype(jnp.float32).astype(jnp.bfloat16)


def send_kernel(base_ref, bounds_ref, q_ref, k_ref, v_ref, qg_ref, kg_ref, o_ref, rot, turned):
    lane = lax.broadcasted_iota(jnp.int32, (HD // 2, 128), 1)
    token = base_ref[0] + lane
    place = (token - starts_of(token, bounds_ref)).astype(jnp.float32)
    index = lax.broadcasted_iota(jnp.int32, (HD // 2, 128), 0).astype(jnp.float32)
    angle = place * jnp.exp(jnp.float32(FIRST) * index * 2.0 / HD)
    cosine = jnp.cos(angle)
    sine = jnp.sin(angle)
    gains = [jnp.transpose(jnp.broadcast_to(g[...], (HEADS, HD))) for g in (qg_ref, kg_ref)]
    for t in range(TOK):
        c = jnp.broadcast_to(cosine[:, t : t + 1], (HD // 2, HEADS))
        s = jnp.broadcast_to(sine[:, t : t + 1], (HD // 2, HEADS))
        for n, (x_ref, gain) in enumerate(zip((q_ref, k_ref), gains)):
            x = x_ref[t].astype(jnp.float32)
            scale = lax.rsqrt(jnp.mean(x * x, axis=0, keepdims=True) + 1e-06)
            x = x * scale * gain
            a, b = x[: HD // 2], x[HD // 2 :]
            row = pl.ds((t // HALF_TOK) * HD, HD)
            rot[n, t % HALF_TOK, row, :] = jnp.concatenate([a * c - b * s, a * s + b * c], axis=0).astype(
                jnp.bfloat16
            )
    for t in range(TOK):
        rot[2, t % HALF_TOK, pl.ds((t // HALF_TOK) * HD, HD), :] = v_ref[t]
    eye = identity(HEADS)
    for n in range(3):
        for r in range(0, HALF_TOK, 2):
            both = dot(eye, rot[n, r : r + 2].reshape(256, HEADS), NT).astype(jnp.bfloat16)
            turned[n, r] = both[:, :128]
            turned[n, r + 1] = both[:, 128:]
    mix = interleave()
    for n in range(3):
        for h in range(0, HEADS, 16):
            part = turned[n, :, h : h + 16, :].reshape(256, 128)
            o_ref[h : h + 16, 16 * n : 16 * n + 16, :] = (
                dot(mix, part, NN).astype(jnp.bfloat16).reshape(16, 16, 128)
            )


def attend_kernel(bounds_ref, x_ref, o_ref, vt, expo):
    eye = identity(128)
    for j in range(NBLK):
        v2 = x_ref[SRC * j : SRC * j + SRC, 32:48, :].reshape(PAIRS, 128)
        vt[j] = dot(eye, v2, NT).astype(jnp.bfloat16)
    low = lax.broadcasted_iota(jnp.int32, (PAIRS, 128), 1) < HD
    lane = lax.broadcasted_iota(jnp.int32, (1, BLK), 1)
    pair = lane % PAIRS
    q_off = (pair // 16) * 32 + pair % 16 + (lane // PAIRS) * 16
    row = lax.broadcasted_iota(jnp.int32, (PAIRS, BLK), 0)
    k_off = (row // 16) * 32 + row % 16

    def query_block(i, _):
        q2 = x_ref[pl.ds(SRC * i, SRC), 0:16, :].reshape(PAIRS, 128).astype(jnp.float32)
        swap = pltpu.roll(q2, HD, 1)
        zero = jnp.zeros_like(q2)
        rhs_lo = jnp.concatenate([jnp.where(low, q2, zero), jnp.where(low, swap, zero)], axis=0).astype(jnp.bfloat16)
        rhs_hi = jnp.concatenate([jnp.where(low, zero, swap), jnp.where(low, zero, q2)], axis=0).astype(jnp.bfloat16)
        q_tok = BLK * i + q_off
        q_start = starts_of(q_tok, bounds_ref)
        first = BLK * i
        start = jnp.int32(0)
        for d in range(1, DOCS):
            start = jnp.where(first >= bounds_ref[d], bounds_ref[d], start)
        j0 = start // BLK

        def scores(j, total):
            k2 = x_ref[pl.ds(SRC * j, SRC), 16:32, :].reshape(PAIRS, 128)
            for n, rhs in enumerate((rhs_lo, rhs_hi)):
                s = dot(k2, rhs, NT)
                k_tok = BLK * j + 16 * n + k_off
                allowed = (k_tok <= q_tok) & (k_tok >= q_start)
                e = jnp.where(allowed, jnp.exp2(s * jnp.float32(SCALE)), jnp.float32(0.0))
                expo[j - j0, n] = e
                total = total + jnp.sum(e, axis=0, keepdims=True)
            return total

        total = lax.fori_loop(j0, i + 1, scores, jnp.zeros((1, BLK), jnp.float32))
        inverse = 1.0 / total

        def weigh(j, out):
            for n in range(2):
                w = (expo[j - j0, n] * inverse).astype(jnp.bfloat16)
                out = out + dot(vt[j, HD * n : HD * n + HD, :], w, NN)
            return out

        out = lax.fori_loop(j0, i + 1, weigh, jnp.zeros((HD, BLK), jnp.float32))
        both = jnp.concatenate([out[:, :PAIRS], out[:, PAIRS:]], axis=0)
        o_ref[pl.ds(SRC * i, SRC)] = jnp.transpose(both).astype(jnp.bfloat16).reshape(SRC, 16, 128)
        return 0

    lax.fori_loop(0, NBLK, query_block, 0)


def take_kernel(x_ref, o_ref, turned):
    mix = interleave()
    for h in range(0, HEADS, 16):
        part = x_ref[h : h + 16].reshape(256, 128)
        turned[:, h : h + 16, :] = dot(mix, part, NN).astype(jnp.bfloat16).reshape(16, 16, 128)
    eye = identity(128)
    for r in range(HALF_TOK):
        both = dot(eye, turned[r], NT).astype(jnp.bfloat16)
        o_ref[r] = both[:HD]
        o_ref[r + HALF_TOK] = both[HD:]


SMEM = pl.BlockSpec(memory_space=pltpu.SMEM)
VMEM = pl.BlockSpec(memory_space=pltpu.VMEM)


def body(queries, keys, values, doc_bounds, q_gain, k_gain):
    group = lax.axis_size("seqa") * lax.axis_size("seqb")
    index = lax.axis_index("seqa") * lax.axis_size("seqb") + lax.axis_index("seqb")
    base = (index * TOK).astype(jnp.int32).reshape(1)
    turn = lambda x: jnp.transpose(x, (0, 2, 1))
    packed = pl.pallas_call(
        send_kernel,
        out_shape=jax.ShapeDtypeStruct((HEADS, 48, 128), jnp.bfloat16),
        in_specs=[SMEM, SMEM, VMEM, VMEM, VMEM, VMEM, VMEM],
        out_specs=VMEM,
        scratch_shapes=[
            pltpu.VMEM((3, HALF_TOK, 128, HEADS), jnp.bfloat16),
            pltpu.VMEM((3, HALF_TOK, HEADS, 128), jnp.bfloat16),
        ],
        compiler_params=pltpu.CompilerParams(vmem_limit_bytes=32 << 20),
        name="send_side",
    )(base, doc_bounds, turn(queries), turn(keys), turn(values), q_gain.reshape(1, HD), k_gain.reshape(1, HD))
    mine = lax.all_to_all(packed, AXES, split_axis=0, concat_axis=0, tiled=True)
    result = pl.pallas_call(
        attend_kernel,
        out_shape=jax.ShapeDtypeStruct((group, HALF_TOK, 128), jnp.bfloat16),
        in_specs=[SMEM, VMEM],
        out_specs=VMEM,
        scratch_shapes=[
            pltpu.VMEM((NBLK, 128, PAIRS), jnp.bfloat16),
            pltpu.VMEM((NBLK, 2, PAIRS, BLK), jnp.float32),
        ],
        compiler_params=pltpu.CompilerParams(vmem_limit_bytes=32 << 20),
        name="attend",
    )(doc_bounds, mine)
    back = lax.all_to_all(result, AXES, split_axis=0, concat_axis=0, tiled=True)
    out = pl.pallas_call(
        take_kernel,
        out_shape=jax.ShapeDtypeStruct((TOK, HD, HEADS), jnp.bfloat16),
        in_specs=[VMEM],
        out_specs=VMEM,
        scratch_shapes=[pltpu.VMEM((HALF_TOK, HEADS, 128), jnp.bfloat16)],
        compiler_params=pltpu.CompilerParams(vmem_limit_bytes=32 << 20),
        name="take_side",
    )(back)
    return turn(out)


def solution(mesh):
    tokens = P(("dp", "seqa", "seqb"), None, None)
    return jax.shard_map(
        body,
        mesh=mesh,
        in_specs=(tokens, tokens, tokens, P("dp"), P(), P()),
        out_specs=tokens,
        check_vma=False,
    )
```

time: 309 us -> 176 us (0.57)
  the two profiles are of different devices: /device:TPU:1 before, /device:TPU:25 now
where the time goes in v1:
time: 176 us; the launch traced here: 174 us
  blocking collectives  139 us (79%)
  Pallas kernels  30.3 us (17%)
  local copies, waits for them, and re-layouts  5.09 us (3%)
    all_to_all x1, blocking collectives, body(): mine = lax.all_to_all(packed, AXES, split_axis=0, concat_axis=0, tiled=True)  94.6 us
    all_to_all x1, blocking collectives, body(): back = lax.all_to_all(result, AXES, split_axis=0, concat_axis=0, tiled=True)  44.4 us
    pallas_call x1, Pallas kernels, body(): pl.pallas_call(attend_kernel, out_shape=jax.ShapeDtypeStruct((group, HALF...  26 us
    unnamed x14, local copies, waits for them, and re-layouts  5.09 us

profile of v1, /device:TPU:25, one launch (start us, length us, event | category | flops | bytes accessed | tf_op | source)
XLA Modules:
  0.0 174.4 jit_solution(2979835028376016414)
XLA Ops:
  0.0 0.0 copy-start
  0.0 1.0 copy-done
  1.0 0.0 copy-start.1
  1.0 1.0 copy-done.1
  2.1 0.0 copy-start.2
  2.1 1.0 copy-done.2
  3.1 0.0 copy-start.3
  3.1 0.7 copy-done.3
  3.8 0.0 copy-start.5
  3.8 0.7 copy-done.5
  4.4 0.0 copy-start.6
  4.4 0.7 copy-done.6
  5.1 2.7 %send_side.1 = bf16[128,48,128]{2,1,0:T(8,128)(2,1)S(1)} custom-call(s32[1]{0:T(128)} %bitcast.base_ref, s32[9]{0:T(128)S(1)} %copy-done.3, bf16[32,64,128]{2,1,0:T(8,128)(2,1)S(1)} %bitcast.7, bf16[32,64,128]{2,1,0:T(8,128)(2,1)S(1)} %bitcast.8, bf16[32,64,128]{2,1,0:T(8,128)(2,1)S(1)} %bitcast.9, f32[1,64]{1,0:T(1,128)S(1)} %bitcast.10, f32[1,64]{1,0:T(1,128)S(1)} %bitcast.11), custom_call_target="tpu_custom_call" | custom-call | tf_op jit(solution)/shard_map/send_side/pallas_call | solution.py:163
  7.8 0.0 copy-start.4
  7.8 94.6 %all_to_all.10.x_ref = bf16[128,48,128]{2,1,0:T(8,128)(2,1)S(1)} all-to-all(bf16[128,48,128]{2,1,0:T(8,128)(2,1)S(1)} %send_side.1), channel_id=1, replica_groups=mesh['seqa'=16,'seqb'=8,'dp'=4] {'seqa','seqb'}, dimensions={0} | all-to-all | bytes 3145728 | tf_op jit(solution)/shard_map/all_to_all | solution.py:175
  102.4 0.0 copy-done.4
  102.4 26.0 %attend.1 = bf16[128,16,128]{2,1,0:T(8,128)(2,1)S(1)} custom-call(s32[9]{0:T(128)S(1)} %copy-done.4, bf16[128,48,128]{2,1,0:T(8,128)(2,1)S(1)} %all_to_all.10.x_ref), custom_call_target="tpu_custom_call" | custom-call | tf_op jit(solution)/shard_map/attend/pallas_call | solution.py:176
  128.4 44.4 %all_to_all.11.x_ref = bf16[128,16,128]{2,1,0:T(8,128)(2,1)S(1)} all-to-all(bf16[128,16,128]{2,1,0:T(8,128)(2,1)S(1)} %attend.1), channel_id=1, replica_groups=mesh['seqa'=16,'seqb'=8,'dp'=4] {'seqa','seqb'}, dimensions={0} | all-to-all | bytes 1048576 | tf_op jit(solution)/shard_map/all_to_all | solution.py:188
  172.8 1.6 take_side.1
Async XLA Ops:
  0.0 1.0 copy-start
  1.0 1.0 copy-start.1
  2.1 1.0 copy-start.2
  3.1 0.7 copy-start.3
  3.8 0.7 copy-start.5
  4.4 0.7 copy-start.6
  7.8 94.6 %copy-start.4 = (s32[9]{0:T(128)S(1)}, s32[9]{0:T(128)}, u32[]{:S(2)}) copy-start(s32[9]{0:T(128)} %bounds_ref.3) | copy-start | bytes 112

commit v2 on v0

v2 whole, which is shorter than its diff:
```python
import jax
import jax.numpy as jnp
from jax import lax
from jax.experimental import pallas as pl
from jax.experimental.pallas import tpu as pltpu
from jax.sharding import PartitionSpec as P

AXES = ("seqa", "seqb")
TOK = 32
ROWS = 16
HD = 64
HEADS = 128
DOCS = 8
SEQ = 4096
BLK = 256
PAIRS = BLK // 2
NBLK = SEQ // BLK
SRC = BLK // TOK
UNROLL = 4
GROUP = 8
FAR = (NBLK - 2) * (NBLK - 1) // 2 + UNROLL
NT = (((1,), (1,)), ((), ()))
NN = (((1,), (0,)), ((), ()))
SCALE = 1.4426950408889634 / 8.0
FIRST = -9.210340371976184


def dot(a, b, dims=NN):
    return lax.dot_general(a, b, dims, preferred_element_type=jnp.float32)


def starts_of(token, bounds_ref):
    start = jnp.zeros_like(token)
    for d in range(1, DOCS):
        start = jnp.where(token >= bounds_ref[d], bounds_ref[d], start)
    return start


def identity(n):
    row = lax.broadcasted_iota(jnp.int32, (n, n), 0)
    col = lax.broadcasted_iota(jnp.int32, (n, n), 1)
    return (row == col).astype(jnp.float32).astype(jnp.bfloat16)


def interleave():
    row = lax.broadcasted_iota(jnp.int32, (256, 256), 0)
    col = lax.broadcasted_iota(jnp.int32, (256, 256), 1)
    return (col == (row % 16) * 16 + row // 16).astype(jnp.float32).astype(jnp.bfloat16)


def send_kernel(
    base_ref, bounds_hbm, q_hbm, k_hbm, v_hbm, qg_hbm, kg_hbm, o_hbm, bounds_ref, x_ref, g_ref, rot, turned, packed, sems, out_sems
):
    arriving = [
        pltpu.make_async_copy(source, target, sems.at[n])
        for n, (source, target) in enumerate(
            (
                (bounds_hbm, bounds_ref),
                (qg_hbm, g_ref.at[0]),
                (kg_hbm, g_ref.at[1]),
                (q_hbm, x_ref.at[0]),
                (k_hbm, x_ref.at[1]),
                (v_hbm, x_ref.at[2]),
            )
        )
    ]
    for c in arriving:
        c.start()
    for c in arriving[:3]:
        c.wait()
    lane = lax.broadcasted_iota(jnp.int32, (HD // 2, 128), 1)
    token = base_ref[0] + lane
    place = (token - starts_of(token, bounds_ref)).astype(jnp.float32)
    index = lax.broadcasted_iota(jnp.int32, (HD // 2, 128), 0).astype(jnp.float32)
    angle = place * jnp.exp(jnp.float32(FIRST) * index * 2.0 / HD)
    cosine = jnp.cos(angle)
    sine = jnp.sin(angle)
    gains = [jnp.transpose(jnp.broadcast_to(g_ref[n], (HEADS, HD))) for n in range(2)]
    eye = identity(HEADS)
    mix = interleave()
    for c in arriving[3:]:
        c.wait()

    def turn(n, r, rows):
        both = dot(eye, rows, NT).astype(jnp.bfloat16)
        turned[n, r] = both[:, :128]
        turned[n, r + 1] = both[:, 128:]

    leaving = []

    def leave(heads, rows):
        copy = pltpu.make_async_copy(packed.at[heads, rows], o_hbm.at[heads, rows], out_sems.at[len(leaving)])
        copy.start()
        leaving.append(copy)

    for r in range(0, ROWS, 2):
        turn(2, r, jnp.concatenate([x_ref[2, t] for t in (r, r + ROWS, r + 1, r + 1 + ROWS)], axis=0))
    for h in range(0, HEADS, 32):
        part = jnp.concatenate([turned[2, :, h + m : h + m + 16, :].reshape(256, 128) for m in (0, 16)], axis=1)
        both = dot(mix, part).astype(jnp.bfloat16)
        for m in range(2):
            packed[h + 16 * m : h + 16 * m + 16, 32:48, :] = both[:, 128 * m : 128 * m + 128].reshape(16, 16, 128)
    leave(pl.ds(0, HEADS), pl.ds(32, 16))
    for r in range(0, ROWS, 2):
        for t in (r, r + ROWS, r + 1, r + 1 + ROWS):
            c = jnp.broadcast_to(cosine[:, t : t + 1], (HD // 2, HEADS))
            s = jnp.broadcast_to(sine[:, t : t + 1], (HD // 2, HEADS))
            for n in range(2):
                x = x_ref[n, t].astype(jnp.float32)
                scale = lax.rsqrt(jnp.mean(x * x, axis=0, keepdims=True) + 1e-06)
                x = x * scale * gains[n]
                a, b = x[: HD // 2], x[HD // 2 :]
                y = jnp.concatenate([a * c - b * s, a * s + b * c], axis=0)
                rot[n, t % ROWS, pl.ds((t // ROWS) * HD, HD), :] = y.astype(jnp.bfloat16)
        for n in range(2):
            turn(n, r, rot[n, r : r + 2].reshape(256, HEADS))
    for h in range(0, HEADS, 16):
        part = jnp.concatenate([turned[n, :, h : h + 16, :].reshape(256, 128) for n in range(2)], axis=1)
        both = dot(mix, part).astype(jnp.bfloat16)
        for n in range(2):
            packed[h : h + 16, 16 * n : 16 * n + 16, :] = both[:, 128 * n : 128 * n + 128].reshape(16, 16, 128)
        if h % 32 == 16:
            leave(pl.ds(h - 16, 32), pl.ds(0, 32))
    for c in leaving:
        c.wait()


def attend_kernel(bounds_ref, x_ref, o_ref, qt, vt, starts, near, far, total, summed, item_i, item_j):
    lane = lax.broadcasted_iota(jnp.int32, (1, BLK), 1)
    pair = lane % PAIRS
    q_off = (pair // 16) * 32 + pair % 16 + (lane // PAIRS) * 16
    row = lax.broadcasted_iota(jnp.int32, (2 * PAIRS, BLK), 0)
    k_off = ((row % PAIRS) // 16) * 32 + row % 16 + (row // PAIRS) * 16
    below = k_off <= q_off

    def list_block(i, n):
        def add(j, n):
            item_i[n] = i
            item_j[n] = j
            return n + 1

        return lax.fori_loop(starts_of(BLK * i, bounds_ref) // BLK, i - 1, add, n)

    n_far = lax.fori_loop(2, NBLK, list_block, jnp.int32(0))
    for u in range(UNROLL - 1):
        item_i[n_far + u] = NBLK
        item_j[n_far + u] = 0
    trips = (n_far + UNROLL - 1) // UNROLL
    zero = jnp.zeros((HD, BLK), jnp.bfloat16)

    def wide(x):
        t = jnp.transpose(x.astype(jnp.float32)).astype(jnp.bfloat16)
        return jnp.concatenate([t[:HD], t[HD:]], axis=1)

    def scores(j, q, allowed):
        k2 = x_ref[pl.ds(SRC * j, SRC), 16:32, :].reshape(PAIRS, 128)
        low = dot(k2, jnp.concatenate([q, zero], axis=0))
        high = dot(k2, jnp.concatenate([zero, q], axis=0))
        s = jnp.concatenate([low, high], axis=0)
        return jnp.where(allowed, jnp.exp2(s * jnp.float32(SCALE)), jnp.float32(0.0))

    def partial_sum(e):
        return jnp.sum(e.reshape(BLK // 8, 8, BLK), axis=0)

    def near_scores(g, _):
        for u in range(GROUP):
            i = GROUP * g + u
            q = wide(x_ref[pl.ds(SRC * i, SRC), 0:16, :].reshape(PAIRS, 128))
            qt[i] = q
            vt[i] = wide(x_ref[pl.ds(SRC * i, SRC), 32:48, :].reshape(PAIRS, 128))
            start = starts_of(BLK * i + q_off, bounds_ref)
            starts[i] = start
            e1 = scores(i, q, below & (k_off >= start - BLK * i))
            e0 = scores(jnp.maximum(i - 1, 0), q, k_off >= start - BLK * (i - 1))
            near[i, 0] = e0
            near[i, 1] = e1
            total[i] = partial_sum(e0) + partial_sum(e1)
        return 0

    lax.fori_loop(0, NBLK // GROUP, near_scores, 0)

    def far_scores(w, _):
        for u in range(UNROLL):
            n = UNROLL * w + u
            i, j = item_i[n], item_j[n]
            e = scores(j, qt[i], k_off >= starts[i] - BLK * j)
            far[n] = e
            total[i] += partial_sum(e)
        return 0

    lax.fori_loop(0, trips, far_scores, 0)

    def near_values(g, _):
        for u in range(GROUP):
            i = GROUP * g + u
            inverse = 1.0 / jnp.sum(total[i], axis=0, keepdims=True)
            total[i] = jnp.broadcast_to(inverse, (8, BLK))
            w = jnp.concatenate([(near[i, n] * inverse).astype(jnp.bfloat16) for n in range(2)], axis=0)
            summed[i] = dot(jnp.concatenate([vt[jnp.maximum(i - 1, 0)], vt[i]], axis=1), w)
        return 0

    lax.fori_loop(0, NBLK // GROUP, near_values, 0)

    def far_values(w, _):
        for u in range(UNROLL):
            n = UNROLL * w + u
            i, j = item_i[n], item_j[n]
            summed[i] += dot(vt[j], (far[n] * total[i][0:1]).astype(jnp.bfloat16))
        return 0

    lax.fori_loop(0, trips, far_values, 0)

    def finish(g, _):
        for u in range(GROUP):
            i = GROUP * g + u
            out = summed[i]
            both = jnp.transpose(jnp.concatenate([out[:, :PAIRS], out[:, PAIRS:]], axis=0))
            o_ref[pl.ds(SRC * i, SRC)] = both.astype(jnp.bfloat16).reshape(SRC, 16, 128)
        return 0

    lax.fori_loop(0, NBLK // GROUP, finish, 0)


def take_kernel(x_ref, o_hbm, turned, out, sems):
    mix = interleave()
    eye = identity(128)
    for h in range(0, HEADS, 32):
        part = jnp.concatenate([x_ref[h + m : h + m + 16].reshape(256, 128) for m in (0, 16)], axis=1)
        both = dot(mix, part).astype(jnp.bfloat16)
        for m in range(2):
            turned[:, h + 16 * m : h + 16 * m + 16, :] = both[:, 128 * m : 128 * m + 128].reshape(16, 16, 128)
    copies = []
    for r in range(0, ROWS, 2):
        both = dot(eye, turned[r : r + 2].reshape(256, 128), NT).astype(jnp.bfloat16)
        for m in range(2):
            out[r + m] = both[:HD, 128 * m : 128 * m + 128]
            out[r + m + ROWS] = both[HD:, 128 * m : 128 * m + 128]
        if r % 8 == 6:
            for first in (r - 6, r - 6 + ROWS):
                copy = pltpu.make_async_copy(
                    out.at[pl.ds(first, 8)], o_hbm.at[pl.ds(first, 8)], sems.at[len(copies)]
                )
                copy.start()
                copies.append(copy)
    for copy in copies:
        copy.wait()


SMEM = pl.BlockSpec(memory_space=pltpu.SMEM)
VMEM = pl.BlockSpec(memory_space=pltpu.VMEM)
HBM = pl.BlockSpec(memory_space=pltpu.HBM)


def send_call(base, doc_bounds, q, k, v, q_gain, k_gain):
    return pl.pallas_call(
        send_kernel,
        out_shape=jax.ShapeDtypeStruct((HEADS, 48, 128), jnp.bfloat16),
        in_specs=[SMEM] + [HBM] * 6,
        out_specs=HBM,
        scratch_shapes=[
            pltpu.SMEM((DOCS + 1,), jnp.int32),
            pltpu.VMEM((3, TOK, HD, HEADS), jnp.bfloat16),
            pltpu.VMEM((2, 1, HD), jnp.float32),
            pltpu.VMEM((2, ROWS, 128, HEADS), jnp.bfloat16),
            pltpu.VMEM((3, ROWS, HEADS, 128), jnp.bfloat16),
            pltpu.VMEM((HEADS, 48, 128), jnp.bfloat16),
            pltpu.SemaphoreType.DMA((6,)),
            pltpu.SemaphoreType.DMA((5,)),
        ],
        compiler_params=pltpu.CompilerParams(vmem_limit_bytes=60 << 20),
        name="send_side",
    )(base, doc_bounds, q, k, v, q_gain.reshape(1, HD), k_gain.reshape(1, HD))


def attend_call(doc_bounds, mine):
    return pl.pallas_call(
        attend_kernel,
        out_shape=jax.ShapeDtypeStruct((SEQ // TOK, ROWS, 128), jnp.bfloat16),
        in_specs=[SMEM, VMEM],
        out_specs=VMEM,
        scratch_shapes=[
            pltpu.VMEM((NBLK + 1, HD, BLK), jnp.bfloat16),
            pltpu.VMEM((NBLK, HD, BLK), jnp.bfloat16),
            pltpu.VMEM((NBLK + 1, 1, BLK), jnp.int32),
            pltpu.VMEM((NBLK, 2, BLK, BLK), jnp.float32),
            pltpu.VMEM((FAR, BLK, BLK), jnp.float32),
            pltpu.VMEM((NBLK + 1, 8, BLK), jnp.float32),
            pltpu.VMEM((NBLK + 1, HD, BLK), jnp.float32),
            pltpu.SMEM((FAR,), jnp.int32),
            pltpu.SMEM((FAR,), jnp.int32),
        ],
        compiler_params=pltpu.CompilerParams(vmem_limit_bytes=40 << 20),
        name="attend",
    )(doc_bounds, mine)


def take_call(back):
    return pl.pallas_call(
        take_kernel,
        out_shape=jax.ShapeDtypeStruct((TOK, HD, HEADS), jnp.bfloat16),
        in_specs=[VMEM],
        out_specs=HBM,
        scratch_shapes=[
            pltpu.VMEM((ROWS, HEADS, 128), jnp.bfloat16),
            pltpu.VMEM((TOK, HD, HEADS), jnp.bfloat16),
            pltpu.SemaphoreType.DMA((4,)),
        ],
        compiler_params=pltpu.CompilerParams(vmem_limit_bytes=32 << 20),
        name="take_side",
    )(back)


def body(queries, keys, values, doc_bounds, q_gain, k_gain):
    index = lax.axis_index("seqa") * lax.axis_size("seqb") + lax.axis_index("seqb")
    base = (index * TOK).astype(jnp.int32).reshape(1)
    inputs = [jnp.transpose(x, (0, 2, 1)) for x in (queries, keys, values)]
    packed = send_call(base, doc_bounds, *inputs, q_gain, k_gain)
    mine = lax.all_to_all(packed, AXES, split_axis=0, concat_axis=0, tiled=True)
    result = attend_call(doc_bounds, mine)
    back = lax.all_to_all(result, AXES, split_axis=0, concat_axis=0, tiled=True)
    return jnp.transpose(take_call(back), (0, 2, 1))


def solution(mesh):
    tokens = P(("dp", "seqa", "seqb"), None, None)
    return jax.shard_map(
        body,
        mesh=mesh,
        in_specs=(tokens, tokens, tokens, P("dp"), P(), P()),
        out_specs=tokens,
        check_vma=False,
    )
```

time: 309 us -> 154 us (0.50)
  blocking collectives: 39.9 us -> 140 us
  matrix products: 77.5 us -> 0 us
  waiting for transfers between devices: 71.8 us -> 0 us
  other arithmetic: 57.5 us -> 0 us
  starting transfers between devices: 33.4 us -> 0 us
  local copies, waits for them, and re-layouts: 27.8 us -> 0.01 us
  Pallas kernels: 0 us -> 14.1 us
    all_to_all x1 -> x2, blocking collectives: 39.9 us -> 140 us  [the longest x1 94.6 us: body(): mine = lax.all_to_all(packed, AXES, split_axis=0, concat_axis=0, tiled=True)]
    dot_general x32 -> x0, matrix products: 77.5 us -> none  [the longest x16 40.5 us: one_block(): jnp.dot(query_rows, kr.T, preferred_element_type=jnp.float32)]
    all_to_all x3 -> x0, waiting for transfers between devices: 71.8 us -> none  [the longest x1 31.3 us: body(): lax.all_to_all(queries, ('seqa', 'seqb'), split_axis=1, concat_axis=0, ti...]
    all_to_all x3 -> x0, starting transfers between devices: 33.4 us -> none  [the longest x1 20.4 us: body(): lax.all_to_all(queries, ('seqa', 'seqb'), split_axis=1, concat_axis=0, ti...]
    reduce_sum x19 -> x0, other arithmetic: 23.5 us -> none  [the longest x16 22.1 us: one_block(): weights = (expo / jnp.sum(expo, axis=1, keepdims=True)).astype(jnp.bfloat16)]
    transpose x1 -> x0, other arithmetic: 22.6 us -> none  [body(): attend_all(query_full, key_full, value_full, doc_bounds, q_gain, k_gain)]
    unnamed x25 -> x2, local copies, waits for them, and re-layouts: 18.5 us -> 0.01 us
    pallas_call x0 -> x3, Pallas kernels: none -> 14.1 us  [the longest x1 8.77 us: attend_call(): pl.pallas_call(attend_kernel, out_shape=jax.ShapeDtypeStruct((SEQ // TOK,...]
  transfers between devices with their start and end apart: 3 -> 0, of which waited for: 3 -> 0; matrix products, arithmetic and copies ran while one was open for 9% -> 0% of each run, Pallas kernels for 0% -> 0%
where the time goes in v2:
time: 154 us
  blocking collectives  140 us (91%)
  Pallas kernels  14.1 us (9%)
    all_to_all x1, blocking collectives, body(): mine = lax.all_to_all(packed, AXES, split_axis=0, concat_axis=0, tiled=True)  94.6 us
    all_to_all x1, blocking collectives, body(): back = lax.all_to_all(result, AXES, split_axis=0, concat_axis=0, tiled=True)  45.5 us
    pallas_call x1, Pallas kernels, attend_call(): pl.pallas_call(attend_kernel, out_shape=jax.ShapeDtypeStruct((SEQ // TOK,...  8.77 us
    pallas_call x1, Pallas kernels, send_call(): pl.pallas_call(send_kernel, out_shape=jax.ShapeDtypeStruct((HEADS, 48, 12...  4.06 us

profile of v2, /device:TPU:1, one launch (start us, length us, event | category | flops | bytes accessed | tf_op | source)
XLA Modules:
  0.0 154.3 jit_solution(5495368583652043528)
XLA Ops:
  0.0 4.1 %send_side.1 = bf16[128,48,128]{2,1,0:T(8,128)(2,1)} custom-call(s32[1]{0:T(128)} %bitcast.base_ref, s32[9]{0:T(128)} %bounds_ref.1, bf16[32,64,128]{2,1,0:T(8,128)(2,1)} %bitcast.7, bf16[32,64,128]{2,1,0:T(8,128)(2,1)} %bitcast.8, bf16[32,64,128]{2,1,0:T(8,128)(2,1)} %bitcast.9, f32[1,64]{1,0:T(1,128)} %bitcast.10, f32[1,64]{1,0:T(1,128)} %bitcast.11), custom_call_target="tpu_custom_call" | custom-call | tf_op jit(solution)/shard_map/send_side/pallas_call | solution.py:255
  4.1 0.0 copy-start
  4.1 94.6 %all_to_all.10.x_ref = bf16[128,48,128]{2,1,0:T(8,128)(2,1)S(1)} all-to-all(bf16[128,48,128]{2,1,0:T(8,128)(2,1)} %send_side.1), channel_id=1, replica_groups=mesh['seqa'=16,'seqb'=8,'dp'=4] {'seqa','seqb'}, dimensions={0} | all-to-all | bytes 3145728 | tf_op jit(solution)/shard_map/all_to_all | solution.py:318
  98.7 0.0 copy-done
  98.7 8.8 %attend.1 = bf16[128,16,128]{2,1,0:T(8,128)(2,1)S(1)} custom-call(s32[9]{0:T(128)S(1)} %copy-done, bf16[128,48,128]{2,1,0:T(8,128)(2,1)S(1)} %all_to_all.10.x_ref), custom_call_target="tpu_custom_call" | custom-call | tf_op jit(solution)/shard_map/attend/pallas_call | solution.py:276
  107.5 45.5 %all_to_all.11.x_ref = bf16[128,16,128]{2,1,0:T(8,128)(2,1)S(1)} all-to-all(bf16[128,16,128]{2,1,0:T(8,128)(2,1)S(1)} %attend.1), channel_id=1, replica_groups=mesh['seqa'=16,'seqb'=8,'dp'=4] {'seqa','seqb'}, dimensions={0} | all-to-all | bytes 1048576 | tf_op jit(solution)/shard_map/all_to_all | solution.py:320
  153.0 1.3 take_side.1
Async XLA Ops:
  4.1 94.6 %copy-start = (s32[9]{0:T(128)S(1)}, s32[9]{0:T(128)}, u32[]{:S(2)}) copy-start(s32[9]{0:T(128)} %bounds_ref.1) | copy-start | bytes 112

commit v3 on v2

--- a/solution.py
+++ b/solution.py
@@ -16,11 +16,12 @@
 PAIRS = BLK // 2
 NBLK = SEQ // BLK
 SRC = BLK // TOK
-UNROLL = 4
-GROUP = 8
+UNROLL = 8
+GROUP = 16
 FAR = (NBLK - 2) * (NBLK - 1) // 2 + UNROLL
 NT = (((1,), (1,)), ((), ()))
 NN = (((1,), (0,)), ((), ()))
+BIG = 32768.0
 SCALE = 1.4426950408889634 / 8.0
 FIRST = -9.210340371976184
 
@@ -49,7 +50,7 @@
 
 
 def send_kernel(
-    base_ref, bounds_hbm, q_hbm, k_hbm, v_hbm, qg_hbm, kg_hbm, o_hbm, bounds_ref, x_ref, g_ref, rot, turned, packed, sems, out_sems
+    base_ref, bounds_hbm, q_hbm, k_hbm, v_hbm, qg_hbm, kg_hbm, o_ref, bounds_ref, x_ref, g_ref, rot, turned, sems
 ):
     arriving = [
         pltpu.make_async_copy(source, target, sems.at[n])
@@ -59,8 +60,8 @@
                 (qg_hbm, g_ref.at[0]),
                 (kg_hbm, g_ref.at[1]),
                 (q_hbm, x_ref.at[0]),
+                (v_hbm, x_ref.at[2]),
                 (k_hbm, x_ref.at[1]),
-                (v_hbm, x_ref.at[2]),
             )
         )
     ]
@@ -75,63 +76,66 @@
     angle = place * jnp.exp(jnp.float32(FIRST) * index * 2.0 / HD)
     cosine = jnp.cos(angle)
     sine = jnp.sin(angle)
-    gains = [jnp.transpose(jnp.broadcast_to(g_ref[n], (HEADS, HD))) for n in range(2)]
     eye = identity(HEADS)
     mix = interleave()
-    for c in arriving[3:]:
-        c.wait()
 
     def turn(n, r, rows):
         both = dot(eye, rows, NT).astype(jnp.bfloat16)
         turned[n, r] = both[:, :128]
         turned[n, r + 1] = both[:, 128:]
 
-    leaving = []
-
-    def leave(heads, rows):
-        copy = pltpu.make_async_copy(packed.at[heads, rows], o_hbm.at[heads, rows], out_sems.at[len(leaving)])
-        copy.start()
-        leaving.append(copy)
-
-    for r in range(0, ROWS, 2):
-        turn(2, r, jnp.concatenate([x_ref[2, t] for t in (r, r + ROWS, r + 1, r + 1 + ROWS)], axis=0))
-    for h in range(0, HEADS, 32):
-        part = jnp.concatenate([turned[2, :, h + m : h + m + 16, :].reshape(256, 128) for m in (0, 16)], axis=1)
-        both = dot(mix, part).astype(jnp.bfloat16)
-        for m in range(2):
-            packed[h + 16 * m : h + 16 * m + 16, 32:48, :] = both[:, 128 * m : 128 * m + 128].reshape(16, 16, 128)
-    leave(pl.ds(0, HEADS), pl.ds(32, 16))
-    for r in range(0, ROWS, 2):
-        for t in (r, r + ROWS, r + 1, r + 1 + ROWS):
-            c = jnp.broadcast_to(cosine[:, t : t + 1], (HD // 2, HEADS))
-            s = jnp.broadcast_to(sine[:, t : t + 1], (HD // 2, HEADS))
-            for n in range(2):
+    def rotate(n):
+        gain = jnp.transpose(jnp.broadcast_to(g_ref[n], (HEADS, HD)))
+        for r in range(0, ROWS, 2):
+            for t in (r, r + ROWS, r + 1, r + 1 + ROWS):
+                c = jnp.broadcast_to(cosine[:, t : t + 1], (HD // 2, HEADS))
+                s = jnp.broadcast_to(sine[:, t : t + 1], (HD // 2, HEADS))
                 x = x_ref[n, t].astype(jnp.float32)
                 scale = lax.rsqrt(jnp.mean(x * x, axis=0, keepdims=True) + 1e-06)
-                x = x * scale * gains[n]
+                x = x * scale * gain
                 a, b = x[: HD // 2], x[HD // 2 :]
                 y = jnp.concatenate([a * c - b * s, a * s + b * c], axis=0)
                 rot[n, t % ROWS, pl.ds((t // ROWS) * HD, HD), :] = y.astype(jnp.bfloat16)
-        for n in range(2):
             turn(n, r, rot[n, r : r + 2].reshape(256, HEADS))
-    for h in range(0, HEADS, 16):
-        part = jnp.concatenate([turned[n, :, h : h + 16, :].reshape(256, 128) for n in range(2)], axis=1)
-        both = dot(mix, part).astype(jnp.bfloat16)
-        for n in range(2):
-            packed[h : h + 16, 16 * n : 16 * n + 16, :] = both[:, 128 * n : 128 * n + 128].reshape(16, 16, 128)
-        if h % 32 == 16:
-            leave(pl.ds(h - 16, 32), pl.ds(0, 32))
-    for c in leaving:
-        c.wait()
-
-
-def attend_kernel(bounds_ref, x_ref, o_ref, qt, vt, starts, near, far, total, summed, item_i, item_j):
-    lane = lax.broadcasted_iota(jnp.int32, (1, BLK), 1)
-    pair = lane % PAIRS
-    q_off = (pair // 16) * 32 + pair % 16 + (lane // PAIRS) * 16
-    row = lax.broadcasted_iota(jnp.int32, (2 * PAIRS, BLK), 0)
-    k_off = ((row % PAIRS) // 16) * 32 + row % 16 + (row // PAIRS) * 16
-    below = k_off <= q_off
+
+    def spread(n):
+        for h in range(0, HEADS, 32):
+            part = jnp.concatenate([turned[n, :, h + m : h + m + 16, :].reshape(256, 128) for m in (0, 16)], axis=1)
+            both = dot(mix, part).astype(jnp.bfloat16)
+            for m in range(2):
+                heads = slice(h + 16 * m, h + 16 * m + 16)
+                o_ref[heads, 16 * n : 16 * n + 16, :] = both[:, 128 * m : 128 * m + 128].reshape(16, 16, 128)
+
+    arriving[3].wait()
+    arriving[4].wait()
+    for r in range(0, ROWS, 2):
+        turn(2, r, jnp.concatenate([x_ref[2, t] for t in (r, r + ROWS, r + 1, r + 1 + ROWS)], axis=0))
+    spread(2)
+    rotate(0)
+    arriving[5].wait()
+    spread(0)
+    rotate(1)
+    spread(1)
+
+
+def attend_kernel(bounds_ref, x_ref, o_ref, qt, kf, vt, near, far, total, summed, item_i, item_j):
+    def offsets(shape, axis):
+        n = lax.broadcasted_iota(jnp.int32, shape, axis)
+        return ((n % PAIRS) // 16) * 32 + n % 16 + (n // PAIRS) * 16
+
+    below = offsets((BLK, BLK), 0) <= offsets((BLK, BLK), 1)
+    q_off = offsets((16, BLK), 1)
+    k_off = offsets((BLK, 128), 0)
+
+    def bounds_along(shape, axis):
+        n = lax.broadcasted_iota(jnp.int32, shape, axis)
+        out = jnp.full(shape, SEQ, jnp.int32)
+        for d in range(1, DOCS):
+            out = jnp.where(n == d, bounds_ref[d], out)
+        return out
+
+    q_bounds = bounds_along((16, BLK), 0)
+    k_bounds = bounds_along((1, 128), 1)
 
     def list_block(i, n):
         def add(j, n):
@@ -147,43 +151,46 @@
         item_j[n_far + u] = 0
     trips = (n_far + UNROLL - 1) // UNROLL
     zero = jnp.zeros((HD, BLK), jnp.bfloat16)
+    rest = jnp.zeros((128 - 16, BLK), jnp.bfloat16)
 
     def wide(x):
         t = jnp.transpose(x.astype(jnp.float32)).astype(jnp.bfloat16)
         return jnp.concatenate([t[:HD], t[HD:]], axis=1)
 
-    def scores(j, q, allowed):
+    def scores(j, q, flags):
         k2 = x_ref[pl.ds(SRC * j, SRC), 16:32, :].reshape(PAIRS, 128)
-        low = dot(k2, jnp.concatenate([q, zero], axis=0))
-        high = dot(k2, jnp.concatenate([zero, q], axis=0))
-        s = jnp.concatenate([low, high], axis=0)
-        return jnp.where(allowed, jnp.exp2(s * jnp.float32(SCALE)), jnp.float32(0.0))
+        low = dot(jnp.concatenate([k2, kf[j, :PAIRS]], axis=1), jnp.concatenate([q, zero, flags, rest], axis=0))
+        high = dot(jnp.concatenate([k2, kf[j, PAIRS:]], axis=1), jnp.concatenate([zero, q, flags, rest], axis=0))
+        return jnp.exp2(jnp.concatenate([low, high], axis=0) * jnp.float32(SCALE))
+
+    def flags_of(i):
+        return jnp.where(BLK * i + q_off >= q_bounds, jnp.float32(-BIG), jnp.float32(0.0)).astype(jnp.bfloat16)
 
     def partial_sum(e):
         return jnp.sum(e.reshape(BLK // 8, 8, BLK), axis=0)
 
-    def near_scores(g, _):
-        for u in range(GROUP):
-            i = GROUP * g + u
+    def near_scores():
+        for i in range(NBLK):
             q = wide(x_ref[pl.ds(SRC * i, SRC), 0:16, :].reshape(PAIRS, 128))
             qt[i] = q
             vt[i] = wide(x_ref[pl.ds(SRC * i, SRC), 32:48, :].reshape(PAIRS, 128))
-            start = starts_of(BLK * i + q_off, bounds_ref)
-            starts[i] = start
-            e1 = scores(i, q, below & (k_off >= start - BLK * i))
-            e0 = scores(jnp.maximum(i - 1, 0), q, k_off >= start - BLK * (i - 1))
+            flags = flags_of(i)
+            kf[i] = jnp.where(BLK * i + k_off < k_bounds, jnp.float32(1.0), jnp.float32(0.0)).astype(jnp.bfloat16)
+            e1 = jnp.where(below, scores(i, q, flags), jnp.float32(0.0))
+            e0 = scores(max(i - 1, 0), q, flags)
+            if i == 0:
+                e0 = jnp.zeros_like(e0)
             near[i, 0] = e0
             near[i, 1] = e1
             total[i] = partial_sum(e0) + partial_sum(e1)
-        return 0
-
-    lax.fori_loop(0, NBLK // GROUP, near_scores, 0)
+
+    near_scores()
 
     def far_scores(w, _):
         for u in range(UNROLL):
             n = UNROLL * w + u
             i, j = item_i[n], item_j[n]
-            e = scores(j, qt[i], k_off >= starts[i] - BLK * j)
+            e = scores(j, qt[i], flags_of(i))
             far[n] = e
             total[i] += partial_sum(e)
         return 0
@@ -251,25 +258,27 @@
 HBM = pl.BlockSpec(memory_space=pltpu.HBM)
 
 
+def in_hbm(x):
+    return pltpu.with_memory_space_constraint(x, pltpu.HBM)
+
+
 def send_call(base, doc_bounds, q, k, v, q_gain, k_gain):
     return pl.pallas_call(
         send_kernel,
         out_shape=jax.ShapeDtypeStruct((HEADS, 48, 128), jnp.bfloat16),
         in_specs=[SMEM] + [HBM] * 6,
-        out_specs=HBM,
+        out_specs=VMEM,
         scratch_shapes=[
             pltpu.SMEM((DOCS + 1,), jnp.int32),
             pltpu.VMEM((3, TOK, HD, HEADS), jnp.bfloat16),
             pltpu.VMEM((2, 1, HD), jnp.float32),
             pltpu.VMEM((2, ROWS, 128, HEADS), jnp.bfloat16),
             pltpu.VMEM((3, ROWS, HEADS, 128), jnp.bfloat16),
-            pltpu.VMEM((HEADS, 48, 128), jnp.bfloat16),
             pltpu.SemaphoreType.DMA((6,)),
-            pltpu.SemaphoreType.DMA((5,)),
         ],
-        compiler_params=pltpu.CompilerParams(vmem_limit_bytes=60 << 20),
+        compiler_params=pltpu.CompilerParams(vmem_limit_bytes=32 << 20),
         name="send_side",
-    )(base, doc_bounds, q, k, v, q_gain.reshape(1, HD), k_gain.reshape(1, HD))
+    )(base, *(in_hbm(x) for x in (doc_bounds, q, k, v, q_gain.reshape(1, HD), k_gain.reshape(1, HD))))
 
 
 def attend_call(doc_bounds, mine):
@@ -280,8 +289,8 @@
         out_specs=VMEM,
         scratch_shapes=[
             pltpu.VMEM((NBLK + 1, HD, BLK), jnp.bfloat16),
+            pltpu.VMEM((NBLK, BLK, 128), jnp.bfloat16),
             pltpu.VMEM((NBLK, HD, BLK), jnp.bfloat16),
-            pltpu.VMEM((NBLK + 1, 1, BLK), jnp.int32),
             pltpu.VMEM((NBLK, 2, BLK, BLK), jnp.float32),
             pltpu.VMEM((FAR, BLK, BLK), jnp.float32),
             pltpu.VMEM((NBLK + 1, 8, BLK), jnp.float32),
@@ -289,7 +298,7 @@
             pltpu.SMEM((FAR,), jnp.int32),
             pltpu.SMEM((FAR,), jnp.int32),
         ],
-        compiler_params=pltpu.CompilerParams(vmem_limit_bytes=40 << 20),
+        compiler_params=pltpu.CompilerParams(vmem_limit_bytes=44 << 20),
         name="attend",
     )(doc_bounds, mine)
 

time: 154 us -> 151 us (0.981)
  Pallas kernels: 14.1 us -> 11.7 us
where the time goes in v3:
time: 151 us; the launch traced here: 152 us
  blocking collectives  140 us (93%)
  Pallas kernels  11.7 us (8%)
    all_to_all x1, blocking collectives, body(): mine = lax.all_to_all(packed, AXES, split_axis=0, concat_axis=0, tiled=True)  95.4 us
    all_to_all x1, blocking collectives, body(): back = lax.all_to_all(result, AXES, split_axis=0, concat_axis=0, tiled=True)  44.4 us
    pallas_call x1, Pallas kernels, attend_call(): pl.pallas_call(attend_kernel, out_shape=jax.ShapeDtypeStruct((SEQ // TOK,...  7.28 us
    pallas_call x1, Pallas kernels, send_call(): pl.pallas_call(send_kernel, out_shape=jax.ShapeDtypeStruct((HEADS, 48, 12...  3.1 us

profile of v3, /device:TPU:1, one launch (start us, length us, event | category | flops | bytes accessed | tf_op | source)
XLA Modules:
  0.0 151.5 jit_solution(13224114884797774269)
XLA Ops:
  0.0 3.1 %send_side.1 = bf16[128,48,128]{2,1,0:T(8,128)(2,1)S(1)} custom-call(s32[1]{0:T(128)} %bitcast.base_ref, s32[9]{0:T(128)} %bounds_ref.1, bf16[32,64,128]{2,1,0:T(8,128)(2,1)} %bitcast.7, bf16[32,64,128]{2,1,0:T(8,128)(2,1)} %bitcast.8, bf16[32,64,128]{2,1,0:T(8,128)(2,1)} %bitcast.9, f32[1,64]{1,0:T(1,128)} %bitcast.10, f32[1,64]{1,0:T(1,128)} %bitcast.11), custom_call_target="tpu_custom_call" | custom-call | tf_op jit(solution)/shard_map/send_side/pallas_call | solution.py:266
  3.1 0.0 copy-start
  3.1 95.4 %all_to_all.10.x_ref = bf16[128,48,128]{2,1,0:T(8,128)(2,1)S(1)} all-to-all(bf16[128,48,128]{2,1,0:T(8,128)(2,1)S(1)} %send_side.1), channel_id=1, replica_groups=mesh['seqa'=16,'seqb'=8,'dp'=4] {'seqa','seqb'}, dimensions={0} | all-to-all | bytes 3145728 | tf_op jit(solution)/shard_map/all_to_all | solution.py:327
  98.5 0.0 copy-done
  98.5 7.3 %attend.1 = bf16[128,16,128]{2,1,0:T(8,128)(2,1)S(1)} custom-call(s32[9]{0:T(128)S(1)} %copy-done, bf16[128,48,128]{2,1,0:T(8,128)(2,1)S(1)} %all_to_all.10.x_ref), custom_call_target="tpu_custom_call" | custom-call | tf_op jit(solution)/shard_map/attend/pallas_call | solution.py:285
  105.8 44.4 %all_to_all.11.x_ref = bf16[128,16,128]{2,1,0:T(8,128)(2,1)S(1)} all-to-all(bf16[128,16,128]{2,1,0:T(8,128)(2,1)S(1)} %attend.1), channel_id=1, replica_groups=mesh['seqa'=16,'seqb'=8,'dp'=4] {'seqa','seqb'}, dimensions={0} | all-to-all | bytes 1048576 | tf_op jit(solution)/shard_map/all_to_all | solution.py:329
  150.2 1.3 take_side.1
Async XLA Ops:
  3.1 95.4 %copy-start = (s32[9]{0:T(128)S(1)}, s32[9]{0:T(128)}, u32[]{:S(2)}) copy-start(s32[9]{0:T(128)} %bounds_ref.1) | copy-start | bytes 112

commit v4 on v3

--- a/solution.py
+++ b/solution.py
@@ -30,10 +30,10 @@
     return lax.dot_general(a, b, dims, preferred_element_type=jnp.float32)
 
 
-def starts_of(token, bounds_ref):
+def starts_of(token, bound):
     start = jnp.zeros_like(token)
     for d in range(1, DOCS):
-        start = jnp.where(token >= bounds_ref[d], bounds_ref[d], start)
+        start = jnp.where(token >= bound(d), bound(d), start)
     return start
 
 
@@ -50,7 +50,7 @@
 
 
 def send_kernel(
-    base_ref, bounds_hbm, q_hbm, k_hbm, v_hbm, qg_hbm, kg_hbm, o_ref, bounds_ref, x_ref, g_ref, rot, turned, sems
+    bounds_hbm, q_hbm, k_hbm, v_hbm, qg_hbm, kg_hbm, o_ref, bounds_ref, x_ref, g_ref, rot, turned, sems
 ):
     arriving = [
         pltpu.make_async_copy(source, target, sems.at[n])
@@ -70,8 +70,10 @@
     for c in arriving[:3]:
         c.wait()
     lane = lax.broadcasted_iota(jnp.int32, (HD // 2, 128), 1)
-    token = base_ref[0] + lane
-    place = (token - starts_of(token, bounds_ref)).astype(jnp.float32)
+    index = lax.axis_index("seqa") * lax.axis_size("seqb") + lax.axis_index("seqb")
+    token = index * TOK + lane
+    start = starts_of(token, lambda d: bounds_ref[:, d : d + 1])
+    place = (token - start).astype(jnp.float32)
     index = lax.broadcasted_iota(jnp.int32, (HD // 2, 128), 0).astype(jnp.float32)
     angle = place * jnp.exp(jnp.float32(FIRST) * index * 2.0 / HD)
     cosine = jnp.cos(angle)
@@ -118,7 +120,10 @@
     spread(1)
 
 
-def attend_kernel(bounds_ref, x_ref, o_ref, qt, kf, vt, near, far, total, summed, item_i, item_j):
+def attend_kernel(bounds_ref, x_ref, o_ref, qt, kf, vt, near, far, total, summed, items, scalars, sem):
+    copy = pltpu.make_async_copy(bounds_ref, scalars, sem)
+    copy.start()
+
     def offsets(shape, axis):
         n = lax.broadcasted_iota(jnp.int32, shape, axis)
         return ((n % PAIRS) // 16) * 32 + n % 16 + (n // PAIRS) * 16
@@ -131,25 +136,12 @@
         n = lax.broadcasted_iota(jnp.int32, shape, axis)
         out = jnp.full(shape, SEQ, jnp.int32)
         for d in range(1, DOCS):
-            out = jnp.where(n == d, bounds_ref[d], out)
+            out = jnp.where(n == d, bounds_ref[:, d : d + 1], out)
         return out
 
     q_bounds = bounds_along((16, BLK), 0)
     k_bounds = bounds_along((1, 128), 1)
 
-    def list_block(i, n):
-        def add(j, n):
-            item_i[n] = i
-            item_j[n] = j
-            return n + 1
-
-        return lax.fori_loop(starts_of(BLK * i, bounds_ref) // BLK, i - 1, add, n)
-
-    n_far = lax.fori_loop(2, NBLK, list_block, jnp.int32(0))
-    for u in range(UNROLL - 1):
-        item_i[n_far + u] = NBLK
-        item_j[n_far + u] = 0
-    trips = (n_far + UNROLL - 1) // UNROLL
     zero = jnp.zeros((HD, BLK), jnp.bfloat16)
     rest = jnp.zeros((128 - 16, BLK), jnp.bfloat16)
 
@@ -169,8 +161,8 @@
     def partial_sum(e):
         return jnp.sum(e.reshape(BLK // 8, 8, BLK), axis=0)
 
-    def near_scores():
-        for i in range(NBLK):
+    def near_scores(blocks):
+        for i in blocks:
             q = wide(x_ref[pl.ds(SRC * i, SRC), 0:16, :].reshape(PAIRS, 128))
             qt[i] = q
             vt[i] = wide(x_ref[pl.ds(SRC * i, SRC), 32:48, :].reshape(PAIRS, 128))
@@ -184,12 +176,23 @@
             near[i, 1] = e1
             total[i] = partial_sum(e0) + partial_sum(e1)
 
-    near_scores()
+    near_scores(range(3))
+    copy.wait()
+    n_far = jnp.int32(0)
+    for i in range(2, NBLK):
+        start = starts_of(jnp.int32(BLK * i), lambda d: scalars[0, d])
+        for j in range(i - 2, -1, -1):
+            items[n_far] = NBLK * i + j
+            n_far += (start < BLK * (j + 1)).astype(jnp.int32)
+    near_scores(range(3, NBLK))
+    for u in range(UNROLL - 1):
+        items[n_far + u] = NBLK * NBLK
+    trips = (n_far + UNROLL - 1) // UNROLL
 
     def far_scores(w, _):
         for u in range(UNROLL):
             n = UNROLL * w + u
-            i, j = item_i[n], item_j[n]
+            i, j = items[n] >> 4, items[n] & 15
             e = scores(j, qt[i], flags_of(i))
             far[n] = e
             total[i] += partial_sum(e)
@@ -197,35 +200,25 @@
 
     lax.fori_loop(0, trips, far_scores, 0)
 
-    def near_values(g, _):
-        for u in range(GROUP):
-            i = GROUP * g + u
-            inverse = 1.0 / jnp.sum(total[i], axis=0, keepdims=True)
-            total[i] = jnp.broadcast_to(inverse, (8, BLK))
-            w = jnp.concatenate([(near[i, n] * inverse).astype(jnp.bfloat16) for n in range(2)], axis=0)
-            summed[i] = dot(jnp.concatenate([vt[jnp.maximum(i - 1, 0)], vt[i]], axis=1), w)
-        return 0
-
-    lax.fori_loop(0, NBLK // GROUP, near_values, 0)
+    for i in range(NBLK):
+        inverse = 1.0 / jnp.sum(total[i], axis=0, keepdims=True)
+        total[i] = jnp.broadcast_to(inverse, (8, BLK))
+        summed[i] = jnp.zeros((HD, BLK), jnp.float32)
 
     def far_values(w, _):
         for u in range(UNROLL):
             n = UNROLL * w + u
-            i, j = item_i[n], item_j[n]
+            i, j = items[n] >> 4, items[n] & 15
             summed[i] += dot(vt[j], (far[n] * total[i][0:1]).astype(jnp.bfloat16))
         return 0
 
     lax.fori_loop(0, trips, far_values, 0)
 
-    def finish(g, _):
-        for u in range(GROUP):
-            i = GROUP * g + u
-            out = summed[i]
-            both = jnp.transpose(jnp.concatenate([out[:, :PAIRS], out[:, PAIRS:]], axis=0))
-            o_ref[pl.ds(SRC * i, SRC)] = both.astype(jnp.bfloat16).reshape(SRC, 16, 128)
-        return 0
-
-    lax.fori_loop(0, NBLK // GROUP, finish, 0)
+    for i in range(NBLK):
+        w = jnp.concatenate([(near[i, n] * total[i][0:1]).astype(jnp.bfloat16) for n in range(2)], axis=0)
+        out = dot(jnp.concatenate([vt[max(i - 1, 0)], vt[i]], axis=1), w) + summed[i]
+        both = jnp.transpose(jnp.concatenate([out[:, :PAIRS], out[:, PAIRS:]], axis=0))
+        o_ref[SRC * i : SRC * i + SRC] = both.astype(jnp.bfloat16).reshape(SRC, 16, 128)
 
 
 def take_kernel(x_ref, o_hbm, turned, out, sems):
@@ -253,7 +246,6 @@
         copy.wait()
 
 
-SMEM = pl.BlockSpec(memory_space=pltpu.SMEM)
 VMEM = pl.BlockSpec(memory_space=pltpu.VMEM)
 HBM = pl.BlockSpec(memory_space=pltpu.HBM)
 
@@ -262,14 +254,14 @@
     return pltpu.with_memory_space_constraint(x, pltpu.HBM)
 
 
-def send_call(base, doc_bounds, q, k, v, q_gain, k_gain):
+def send_call(doc_bounds, q, k, v, q_gain, k_gain):
     return pl.pallas_call(
         send_kernel,
         out_shape=jax.ShapeDtypeStruct((HEADS, 48, 128), jnp.bfloat16),
-        in_specs=[SMEM] + [HBM] * 6,
+        in_specs=[HBM] * 6,
         out_specs=VMEM,
         scratch_shapes=[
-            pltpu.SMEM((DOCS + 1,), jnp.int32),
+            pltpu.VMEM((1, DOCS + 1), jnp.int32),
             pltpu.VMEM((3, TOK, HD, HEADS), jnp.bfloat16),
             pltpu.VMEM((2, 1, HD), jnp.float32),
             pltpu.VMEM((2, ROWS, 128, HEADS), jnp.bfloat16),
@@ -278,14 +270,14 @@
         ],
         compiler_params=pltpu.CompilerParams(vmem_limit_bytes=32 << 20),
         name="send_side",
-    )(base, *(in_hbm(x) for x in (doc_bounds, q, k, v, q_gain.reshape(1, HD), k_gain.reshape(1, HD))))
+    )(*(in_hbm(x) for x in (doc_bounds, q, k, v, q_gain.reshape(1, HD), k_gain.reshape(1, HD))))
 
 
 def attend_call(doc_bounds, mine):
     return pl.pallas_call(
         attend_kernel,
         out_shape=jax.ShapeDtypeStruct((SEQ // TOK, ROWS, 128), jnp.bfloat16),
-        in_specs=[SMEM, VMEM],
+        in_specs=[VMEM, VMEM],
         out_specs=VMEM,
         scratch_shapes=[
             pltpu.VMEM((NBLK + 1, HD, BLK), jnp.bfloat16),
@@ -296,7 +288,8 @@
             pltpu.VMEM((NBLK + 1, 8, BLK), jnp.float32),
             pltpu.VMEM((NBLK + 1, HD, BLK), jnp.float32),
             pltpu.SMEM((FAR,), jnp.int32),
-            pltpu.SMEM((FAR,), jnp.int32),
+            pltpu.SMEM((1, DOCS + 1), jnp.int32),
+            pltpu.SemaphoreType.DMA(()),
         ],
         compiler_params=pltpu.CompilerParams(vmem_limit_bytes=44 << 20),
         name="attend",
@@ -320,10 +313,9 @@
 
 
 def body(queries, keys, values, doc_bounds, q_gain, k_gain):
-    index = lax.axis_index("seqa") * lax.axis_size("seqb") + lax.axis_index("seqb")
-    base = (index * TOK).astype(jnp.int32).reshape(1)
+    doc_bounds = doc_bounds.reshape(1, DOCS + 1)
     inputs = [jnp.transpose(x, (0, 2, 1)) for x in (queries, keys, values)]
-    packed = send_call(base, doc_bounds, *inputs, q_gain, k_gain)
+    packed = send_call(doc_bounds, *inputs, q_gain, k_gain)
     mine = lax.all_to_all(packed, AXES, split_axis=0, concat_axis=0, tiled=True)
     result = attend_call(doc_bounds, mine)
     back = lax.all_to_all(result, AXES, split_axis=0, concat_axis=0, tiled=True)

time: 151 us -> 150 us (level)
  Pallas kernels: 11.7 us -> 9.23 us
    pallas_call x1, Pallas kernels: 7.28 us -> 4.82 us  [attend_call(): pl.pallas_call(attend_kernel, out_shape=jax.ShapeDtypeStruct((SEQ // TOK,...]
where the time goes in v4:
time: 150 us; the launch traced here: 149 us
  blocking collectives  140 us (93%)
  Pallas kernels  9.23 us (6%)
    all_to_all x1, blocking collectives, body(): mine = lax.all_to_all(packed, AXES, split_axis=0, concat_axis=0, tiled=True)  95.4 us
    all_to_all x1, blocking collectives, body(): back = lax.all_to_all(result, AXES, split_axis=0, concat_axis=0, tiled=True)  44.4 us
    pallas_call x1, Pallas kernels, attend_call(): pl.pallas_call(attend_kernel, out_shape=jax.ShapeDtypeStruct((SEQ // TOK,...  4.82 us
    pallas_call x1, Pallas kernels, send_call(): pl.pallas_call(send_kernel, out_shape=jax.ShapeDtypeStruct((HEADS, 48, 12...  3.11 us

profile of v4, /device:TPU:1, one launch (start us, length us, event | category | flops | bytes accessed | tf_op | source)
XLA Modules:
  0.0 149.0 jit_solution(3168026337301860782)
XLA Ops:
  0.0 3.1 %send_side.1 = bf16[128,48,128]{2,1,0:T(8,128)(2,1)S(1)} custom-call(s32[1,9]{1,0:T(1,128)} %bitcast.7, bf16[32,64,128]{2,1,0:T(8,128)(2,1)} %bitcast.9, bf16[32,64,128]{2,1,0:T(8,128)(2,1)} %bitcast.10, bf16[32,64,128]{2,1,0:T(8,128)(2,1)} %bitcast.11, f32[1,64]{1,0:T(1,128)} %bitcast.12, f32[1,64]{1,0:T(1,128)} %bitcast.13), custom_call_target="tpu_custom_call" | custom-call | tf_op jit(solution)/shard_map/send_side/pallas_call | solution.py:258
  3.1 0.0 copy-start
  3.1 95.4 %all_to_all.10.x_ref = bf16[128,48,128]{2,1,0:T(8,128)(2,1)S(1)} all-to-all(bf16[128,48,128]{2,1,0:T(8,128)(2,1)S(1)} %send_side.1), channel_id=1, replica_groups=mesh['seqa'=16,'seqb'=8,'dp'=4] {'seqa','seqb'}, dimensions={0} | all-to-all | bytes 3145728 | tf_op jit(solution)/shard_map/all_to_all | solution.py:319
  98.5 0.0 copy-done
  98.5 4.8 %attend.1 = bf16[128,16,128]{2,1,0:T(8,128)(2,1)S(1)} custom-call(s32[1,9]{1,0:T(1,128)S(1)} %bitcast.8, bf16[128,48,128]{2,1,0:T(8,128)(2,1)S(1)} %all_to_all.10.x_ref), custom_call_target="tpu_custom_call" | custom-call | tf_op jit(solution)/shard_map/attend/pallas_call | solution.py:277
  103.3 44.4 %all_to_all.11.x_ref = bf16[128,16,128]{2,1,0:T(8,128)(2,1)S(1)} all-to-all(bf16[128,16,128]{2,1,0:T(8,128)(2,1)S(1)} %attend.1), channel_id=1, replica_groups=mesh['seqa'=16,'seqb'=8,'dp'=4] {'seqa','seqb'}, dimensions={0} | all-to-all | bytes 1048576 | tf_op jit(solution)/shard_map/all_to_all | solution.py:321
  147.7 1.3 take_side.1
Async XLA Ops:
  3.1 95.4 %copy-start = (s32[9]{0:T(128)S(1)}, s32[9]{0:T(128)}, u32[]{:S(2)}) copy-start(s32[9]{0:T(128)} %param.9) | copy-start | bytes 112

commit v5 on v4

--- a/solution.py
+++ b/solution.py
@@ -16,9 +16,8 @@
 PAIRS = BLK // 2
 NBLK = SEQ // BLK
 SRC = BLK // TOK
-UNROLL = 8
-GROUP = 16
-FAR = (NBLK - 2) * (NBLK - 1) // 2 + UNROLL
+LONG, MIDDLE, SHORT = 16, 8, 4
+FAR = (NBLK - 2) * (NBLK - 1) // 2 + LONG
 NT = (((1,), (1,)), ((), ()))
 NN = (((1,), (0,)), ((), ()))
 BIG = 32768.0
@@ -108,21 +107,22 @@
                 heads = slice(h + 16 * m, h + 16 * m + 16)
                 o_ref[heads, 16 * n : 16 * n + 16, :] = both[:, 128 * m : 128 * m + 128].reshape(16, 16, 128)
 
-    arriving[3].wait()
-    arriving[4].wait()
-    for r in range(0, ROWS, 2):
-        turn(2, r, jnp.concatenate([x_ref[2, t] for t in (r, r + ROWS, r + 1, r + 1 + ROWS)], axis=0))
+    for c in arriving[3:]:
+        c.wait()
+
+    def turn_values():
+        for r in range(0, ROWS, 2):
+            turn(2, r, jnp.concatenate([x_ref[2, t] for t in (r, r + ROWS, r + 1, r + 1 + ROWS)], axis=0))
+
+    turn_values()
+    rotate(0)
     spread(2)
-    rotate(0)
-    arriving[5].wait()
+    rotate(1)
     spread(0)
-    rotate(1)
     spread(1)
 
 
-def attend_kernel(bounds_ref, x_ref, o_ref, qt, kf, vt, near, far, total, summed, items, scalars, sem):
-    copy = pltpu.make_async_copy(bounds_ref, scalars, sem)
-    copy.start()
+def attend_kernel(bounds_ref, x_ref, o_ref, qt, kf, vt, near, far, total, summed, items):
 
     def offsets(shape, axis):
         n = lax.broadcasted_iota(jnp.int32, shape, axis)
@@ -176,43 +176,50 @@
             near[i, 1] = e1
             total[i] = partial_sum(e0) + partial_sum(e1)
 
-    near_scores(range(3))
-    copy.wait()
+    scalars = [jnp.max(bounds_ref[:, d : d + 1]) for d in range(DOCS)]
     n_far = jnp.int32(0)
     for i in range(2, NBLK):
-        start = starts_of(jnp.int32(BLK * i), lambda d: scalars[0, d])
+        start = starts_of(jnp.int32(BLK * i), lambda d: scalars[d])
         for j in range(i - 2, -1, -1):
             items[n_far] = NBLK * i + j
             n_far += (start < BLK * (j + 1)).astype(jnp.int32)
-    near_scores(range(3, NBLK))
-    for u in range(UNROLL - 1):
+    near_scores(range(NBLK))
+    for u in range(LONG - 1):
         items[n_far + u] = NBLK * NBLK
-    trips = (n_far + UNROLL - 1) // UNROLL
-
-    def far_scores(w, _):
-        for u in range(UNROLL):
-            n = UNROLL * w + u
-            i, j = items[n] >> 4, items[n] & 15
-            e = scores(j, qt[i], flags_of(i))
-            far[n] = e
-            total[i] += partial_sum(e)
-        return 0
-
-    lax.fori_loop(0, trips, far_scores, 0)
-
+    trips = (n_far + LONG - MIDDLE - 1) // LONG
+    left = n_far - LONG * trips
+    passes = (
+        (0, trips, LONG),
+        (LONG * trips, (left > SHORT).astype(jnp.int32), MIDDLE),
+        (LONG * trips, ((left > 0) & (left <= SHORT)).astype(jnp.int32), SHORT),
+    )
+
+    def far_blocks(work):
+        for begin, trips, length in passes:
+
+            def trip(w, _, begin=begin, length=length):
+                for u in range(length):
+                    n = begin + length * w + u
+                    work(n, items[n] >> 4, items[n] & 15)
+                return 0
+
+            lax.fori_loop(0, trips, trip, 0)
+
+    def far_scores(n, i, j):
+        e = scores(j, qt[i], flags_of(i))
+        far[n] = e
+        total[i] += partial_sum(e)
+
+    far_blocks(far_scores)
     for i in range(NBLK):
         inverse = 1.0 / jnp.sum(total[i], axis=0, keepdims=True)
         total[i] = jnp.broadcast_to(inverse, (8, BLK))
         summed[i] = jnp.zeros((HD, BLK), jnp.float32)
 
-    def far_values(w, _):
-        for u in range(UNROLL):
-            n = UNROLL * w + u
-            i, j = items[n] >> 4, items[n] & 15
-            summed[i] += dot(vt[j], (far[n] * total[i][0:1]).astype(jnp.bfloat16))
-        return 0
-
-    lax.fori_loop(0, trips, far_values, 0)
+    def far_values(n, i, j):
+        summed[i] += dot(vt[j], (far[n] * total[i][0:1]).astype(jnp.bfloat16))
+
+    far_blocks(far_values)
 
     for i in range(NBLK):
         w = jnp.concatenate([(near[i, n] * total[i][0:1]).astype(jnp.bfloat16) for n in range(2)], axis=0)
@@ -288,8 +295,6 @@
             pltpu.VMEM((NBLK + 1, 8, BLK), jnp.float32),
             pltpu.VMEM((NBLK + 1, HD, BLK), jnp.float32),
             pltpu.SMEM((FAR,), jnp.int32),
-            pltpu.SMEM((1, DOCS + 1), jnp.int32),
-            pltpu.SemaphoreType.DMA(()),
         ],
         compiler_params=pltpu.CompilerParams(vmem_limit_bytes=44 << 20),
         name="attend",

time: 150 us -> 149 us (level)
  no operation moved by 1% of the time
where the time goes in v5:
time: 149 us; the launch traced here: 148 us
  blocking collectives  140 us (94%)
  Pallas kernels  8.47 us (6%)
    all_to_all x1, blocking collectives, body(): mine = lax.all_to_all(packed, AXES, split_axis=0, concat_axis=0, tiled=True)  95.4 us
    all_to_all x1, blocking collectives, body(): back = lax.all_to_all(result, AXES, split_axis=0, concat_axis=0, tiled=True)  44.4 us
    pallas_call x1, Pallas kernels, attend_call(): pl.pallas_call(attend_kernel, out_shape=jax.ShapeDtypeStruct((SEQ // TOK,...  4.16 us
    pallas_call x1, Pallas kernels, send_call(): pl.pallas_call(send_kernel, out_shape=jax.ShapeDtypeStruct((HEADS, 48, 12...  3 us

profile of v5, /device:TPU:1, one launch (start us, length us, event | category | flops | bytes accessed | tf_op | source)
XLA Modules:
  0.0 148.3 jit_solution(14184014856254229355)
XLA Ops:
  0.0 3.0 %send_side.1 = bf16[128,48,128]{2,1,0:T(8,128)(2,1)S(1)} custom-call(s32[1,9]{1,0:T(1,128)} %bitcast.7, bf16[32,64,128]{2,1,0:T(8,128)(2,1)} %bitcast.9, bf16[32,64,128]{2,1,0:T(8,128)(2,1)} %bitcast.10, bf16[32,64,128]{2,1,0:T(8,128)(2,1)} %bitcast.11, f32[1,64]{1,0:T(1,128)} %bitcast.12, f32[1,64]{1,0:T(1,128)} %bitcast.13), custom_call_target="tpu_custom_call" | custom-call | tf_op jit(solution)/shard_map/send_side/pallas_call | solution.py:265
  3.0 0.0 copy-start
  3.0 95.4 %all_to_all.10.x_ref = bf16[128,48,128]{2,1,0:T(8,128)(2,1)S(1)} all-to-all(bf16[128,48,128]{2,1,0:T(8,128)(2,1)S(1)} %send_side.1), channel_id=1, replica_groups=mesh['seqa'=16,'seqb'=8,'dp'=4] {'seqa','seqb'}, dimensions={0} | all-to-all | bytes 3145728 | tf_op jit(solution)/shard_map/all_to_all | solution.py:324
  98.4 0.0 copy-done
  98.4 4.2 %attend.1 = bf16[128,16,128]{2,1,0:T(8,128)(2,1)S(1)} custom-call(s32[1,9]{1,0:T(1,128)S(1)} %bitcast.8, bf16[128,48,128]{2,1,0:T(8,128)(2,1)S(1)} %all_to_all.10.x_ref), custom_call_target="tpu_custom_call" | custom-call | tf_op jit(solution)/shard_map/attend/pallas_call | solution.py:284
  102.6 44.4 %all_to_all.11.x_ref = bf16[128,16,128]{2,1,0:T(8,128)(2,1)S(1)} all-to-all(bf16[128,16,128]{2,1,0:T(8,128)(2,1)S(1)} %attend.1), channel_id=1, replica_groups=mesh['seqa'=16,'seqb'=8,'dp'=4] {'seqa','seqb'}, dimensions={0} | all-to-all | bytes 1048576 | tf_op jit(solution)/shard_map/all_to_all | solution.py:326
  147.0 1.3 take_side.1
Async XLA Ops:
  3.0 95.4 %copy-start = (s32[9]{0:T(128)S(1)}, s32[9]{0:T(128)}, u32[]{:S(2)}) copy-start(s32[9]{0:T(128)} %param.9) | copy-start | bytes 112

commit v6 on v5

--- a/solution.py
+++ b/solution.py
@@ -5,7 +5,7 @@
 from jax.experimental.pallas import tpu as pltpu
 from jax.sharding import PartitionSpec as P
 
-AXES = ("seqa", "seqb")
+ORDER = ("zh", "zl", "x", "c")
 TOK = 32
 ROWS = 16
 HD = 64
@@ -69,7 +69,9 @@
     for c in arriving[:3]:
         c.wait()
     lane = lax.broadcasted_iota(jnp.int32, (HD // 2, 128), 1)
-    index = lax.axis_index("seqa") * lax.axis_size("seqb") + lax.axis_index("seqb")
+    seqa = lax.axis_index("zl") * 2 + lax.axis_index("c")
+    seqb = lax.axis_index("x") * 2 + lax.axis_index("zh")
+    index = seqa * SRC + seqb
     token = index * TOK + lane
     start = starts_of(token, lambda d: bounds_ref[:, d : d + 1])
     place = (token - start).astype(jnp.float32)
@@ -126,7 +128,8 @@
 
     def offsets(shape, axis):
         n = lax.broadcasted_iota(jnp.int32, shape, axis)
-        return ((n % PAIRS) // 16) * 32 + n % 16 + (n // PAIRS) * 16
+        run = (n % PAIRS) // 16
+        return (run % 4 * 2 + run // 4) * 32 + n % 16 + (n // PAIRS) * 16
 
     below = offsets((BLK, BLK), 0) <= offsets((BLK, BLK), 1)
     q_off = offsets((16, BLK), 1)
@@ -150,7 +153,7 @@
         return jnp.concatenate([t[:HD], t[HD:]], axis=1)
 
     def scores(j, q, flags):
-        k2 = x_ref[pl.ds(SRC * j, SRC), 16:32, :].reshape(PAIRS, 128)
+        k2 = x_ref[:, j >> 1, :, j & 1, 16:32, :].reshape(PAIRS, 128)
         low = dot(jnp.concatenate([k2, kf[j, :PAIRS]], axis=1), jnp.concatenate([q, zero, flags, rest], axis=0))
         high = dot(jnp.concatenate([k2, kf[j, PAIRS:]], axis=1), jnp.concatenate([zero, q, flags, rest], axis=0))
         return jnp.exp2(jnp.concatenate([low, high], axis=0) * jnp.float32(SCALE))
@@ -163,9 +166,9 @@
 
     def near_scores(blocks):
         for i in blocks:
-            q = wide(x_ref[pl.ds(SRC * i, SRC), 0:16, :].reshape(PAIRS, 128))
+            q = wide(x_ref[:, i >> 1, :, i & 1, 0:16, :].reshape(PAIRS, 128))
             qt[i] = q
-            vt[i] = wide(x_ref[pl.ds(SRC * i, SRC), 32:48, :].reshape(PAIRS, 128))
+            vt[i] = wide(x_ref[:, i >> 1, :, i & 1, 32:48, :].reshape(PAIRS, 128))
             flags = flags_of(i)
             kf[i] = jnp.where(BLK * i + k_off < k_bounds, jnp.float32(1.0), jnp.float32(0.0)).astype(jnp.bfloat16)
             e1 = jnp.where(below, scores(i, q, flags), jnp.float32(0.0))
@@ -225,7 +228,7 @@
         w = jnp.concatenate([(near[i, n] * total[i][0:1]).astype(jnp.bfloat16) for n in range(2)], axis=0)
         out = dot(jnp.concatenate([vt[max(i - 1, 0)], vt[i]], axis=1), w) + summed[i]
         both = jnp.transpose(jnp.concatenate([out[:, :PAIRS], out[:, PAIRS:]], axis=0))
-        o_ref[SRC * i : SRC * i + SRC] = both.astype(jnp.bfloat16).reshape(SRC, 16, 128)
+        o_ref[:, i >> 1, :, i & 1] = both.astype(jnp.bfloat16).reshape(2, 4, 16, 128)
 
 
 def take_kernel(x_ref, o_hbm, turned, out, sems):
@@ -283,7 +286,7 @@
 def attend_call(doc_bounds, mine):
     return pl.pallas_call(
         attend_kernel,
-        out_shape=jax.ShapeDtypeStruct((SEQ // TOK, ROWS, 128), jnp.bfloat16),
+        out_shape=jax.ShapeDtypeStruct((2, 8, 4, 2, ROWS, 128), jnp.bfloat16),
         in_specs=[VMEM, VMEM],
         out_specs=VMEM,
         scratch_shapes=[
@@ -321,17 +324,18 @@
     doc_bounds = doc_bounds.reshape(1, DOCS + 1)
     inputs = [jnp.transpose(x, (0, 2, 1)) for x in (queries, keys, values)]
     packed = send_call(doc_bounds, *inputs, q_gain, k_gain)
-    mine = lax.all_to_all(packed, AXES, split_axis=0, concat_axis=0, tiled=True)
-    result = attend_call(doc_bounds, mine)
-    back = lax.all_to_all(result, AXES, split_axis=0, concat_axis=0, tiled=True)
+    mine = lax.all_to_all(packed, ORDER, split_axis=0, concat_axis=0, tiled=True)
+    result = attend_call(doc_bounds, mine.reshape(2, 8, 4, 2, 48, 128)).reshape(HEADS, ROWS, 128)
+    back = lax.all_to_all(result, ORDER, split_axis=0, concat_axis=0, tiled=True)
     return jnp.transpose(take_call(back), (0, 2, 1))
 
 
 def solution(mesh):
-    tokens = P(("dp", "seqa", "seqb"), None, None)
+    fine = jax.sharding.Mesh(mesh.devices.reshape(8, 2, 4, 2, -1), ("zl", "c", "x", "zh", "dp"))
+    tokens = P(("dp", "zl", "c", "x", "zh"), None, None)
     return jax.shard_map(
         body,
-        mesh=mesh,
+        mesh=fine,
         in_specs=(tokens, tokens, tokens, P("dp"), P(), P()),
         out_specs=tokens,
         check_vma=False,

time: 149 us -> 149 us (level); the launches traced: 148 us -> 147 us
  blocking collectives: 140 us -> 138 us
    all_to_all x2, blocking collectives: 140 us -> 138 us  [the longest x1 94.9 us: body(): lax.all_to_all(packed, ORDER, split_axis=0, concat_axis=0, tiled=True)]
where the time goes in v6:
time: 149 us; the launch traced here: 147 us
  blocking collectives  138 us (93%)
  Pallas kernels  8.53 us (6%)
    all_to_all x1, blocking collectives, body(): lax.all_to_all(packed, ORDER, split_axis=0, concat_axis=0, tiled=True)  94.9 us
    all_to_all x1, blocking collectives, body(): lax.all_to_all(result, ORDER, split_axis=0, concat_axis=0, tiled=True)  43.3 us
    pallas_call x1, Pallas kernels, attend_call(): pl.pallas_call(attend_kernel, out_shape=jax.ShapeDtypeStruct((2, 8, 4, 2,...  4.22 us
    pallas_call x1, Pallas kernels, send_call(): pl.pallas_call(send_kernel, out_shape=jax.ShapeDtypeStruct((HEADS, 48, 12...  3 us

profile of v6, /device:TPU:1, one launch (start us, length us, event | category | flops | bytes accessed | tf_op | source)
XLA Modules:
  0.0 146.8 jit_solution(7293609661327886416)
XLA Ops:
  0.0 3.0 %send_side.1 = bf16[128,48,128]{2,1,0:T(8,128)(2,1)S(1)} custom-call(s32[1,9]{1,0:T(1,128)} %bitcast.11, bf16[32,64,128]{2,1,0:T(8,128)(2,1)} %bitcast.13, bf16[32,64,128]{2,1,0:T(8,128)(2,1)} %bitcast.14, bf16[32,64,128]{2,1,0:T(8,128)(2,1)} %bitcast.15, f32[1,64]{1,0:T(1,128)} %bitcast.16, f32[1,64]{1,0:T(1,128)} %bitcast.17), custom_call_target="tpu_custom_call" | custom-call | tf_op jit(solution)/shard_map/send_side/pallas_call | solution.py:268
  3.0 0.0 copy-start
  3.0 94.9 %all_to_all.10 = bf16[128,48,128]{2,1,0:T(8,128)(2,1)S(1)} all-to-all(bf16[128,48,128]{2,1,0:T(8,128)(2,1)S(1)} %send_side.1), channel_id=1, replica_groups=mesh['zl'=8,'c'=2,'x'=4,'zh'=2,'dp'=4] {'zh','zl','x','c'}, dimensions={0} | all-to-all | bytes 3145728 | tf_op jit(solution)/shard_map/all_to_all | solution.py:327
  97.9 0.0 copy-done
  98.0 4.2 %attend.1 = bf16[2,8,4,2,16,128]{5,4,3,2,1,0:T(8,128)(2,1)S(1)} custom-call(s32[1,9]{1,0:T(1,128)S(1)} %bitcast.12, bf16[2,8,4,2,48,128]{5,4,3,2,1,0:T(8,128)(2,1)S(1)} %bitcast.9), custom_call_target="tpu_custom_call" | custom-call | tf_op jit(solution)/shard_map/attend/pallas_call | solution.py:287
  102.2 43.3 %all_to_all.11.x_ref = bf16[128,16,128]{2,1,0:T(8,128)(2,1)S(1)} all-to-all(bf16[128,16,128]{2,1,0:T(8,128)(2,1)S(1)} %bitcast.10), channel_id=1, replica_groups=mesh['zl'=8,'c'=2,'x'=4,'zh'=2,'dp'=4] {'zh','zl','x','c'}, dimensions={0} | all-to-all | bytes 1048576 | tf_op jit(solution)/shard_map/all_to_all | solution.py:329
  145.5 1.3 take_side.1
Async XLA Ops:
  3.0 94.9 %copy-start = (s32[9]{0:T(128)S(1)}, s32[9]{0:T(128)}, u32[]{:S(2)}) copy-start(s32[9]{0:T(128)} %param.9) | copy-start | bytes 112

commit v7 on v5

--- a/solution.py
+++ b/solution.py
@@ -5,7 +5,6 @@
 from jax.experimental.pallas import tpu as pltpu
 from jax.sharding import PartitionSpec as P
 
-AXES = ("seqa", "seqb")
 TOK = 32
 ROWS = 16
 HD = 64
@@ -23,6 +22,14 @@
 BIG = 32768.0
 SCALE = 1.4426950408889634 / 8.0
 FIRST = -9.210340371976184
+
+
+def run_of(z, x, c):
+    return ((z % 8 * 2 + c) * 4 + x) * 2 + z // 8
+
+
+ORDER = [run_of(7 * z % 16, x, c) for z in range(16) for x in range(4) for c in range(2)]
+PLACE = [ORDER.index(s) for s in range(len(ORDER))]
 
 
 def dot(a, b, dims=NN):
@@ -69,8 +76,7 @@
     for c in arriving[:3]:
         c.wait()
     lane = lax.broadcasted_iota(jnp.int32, (HD // 2, 128), 1)
-    index = lax.axis_index("seqa") * lax.axis_size("seqb") + lax.axis_index("seqb")
-    token = index * TOK + lane
+    token = lax.axis_index("run") * TOK + lane
     start = starts_of(token, lambda d: bounds_ref[:, d : d + 1])
     place = (token - start).astype(jnp.float32)
     index = lax.broadcasted_iota(jnp.int32, (HD // 2, 128), 0).astype(jnp.float32)
@@ -122,7 +128,7 @@
     spread(1)
 
 
-def attend_kernel(bounds_ref, x_ref, o_ref, qt, kf, vt, near, far, total, summed, items):
+def attend_kernel(bounds_ref, x_ref, o_ref, qt, kt, kf, vt, near, far, total, summed, items):
 
     def offsets(shape, axis):
         n = lax.broadcasted_iota(jnp.int32, shape, axis)
@@ -150,7 +156,7 @@
         return jnp.concatenate([t[:HD], t[HD:]], axis=1)
 
     def scores(j, q, flags):
-        k2 = x_ref[pl.ds(SRC * j, SRC), 16:32, :].reshape(PAIRS, 128)
+        k2 = kt[j]
         low = dot(jnp.concatenate([k2, kf[j, :PAIRS]], axis=1), jnp.concatenate([q, zero, flags, rest], axis=0))
         high = dot(jnp.concatenate([k2, kf[j, PAIRS:]], axis=1), jnp.concatenate([zero, q, flags, rest], axis=0))
         return jnp.exp2(jnp.concatenate([low, high], axis=0) * jnp.float32(SCALE))
@@ -161,11 +167,16 @@
     def partial_sum(e):
         return jnp.sum(e.reshape(BLK // 8, 8, BLK), axis=0)
 
+    def tiles(i, row):
+        runs = range(SRC * i, SRC * i + SRC)
+        return jnp.concatenate([x_ref[PLACE[s], row : row + 16, :] for s in runs], axis=0)
+
     def near_scores(blocks):
         for i in blocks:
-            q = wide(x_ref[pl.ds(SRC * i, SRC), 0:16, :].reshape(PAIRS, 128))
+            q = wide(tiles(i, 0))
+            kt[i] = tiles(i, 16)
             qt[i] = q
-            vt[i] = wide(x_ref[pl.ds(SRC * i, SRC), 32:48, :].reshape(PAIRS, 128))
+            vt[i] = wide(tiles(i, 32))
             flags = flags_of(i)
             kf[i] = jnp.where(BLK * i + k_off < k_bounds, jnp.float32(1.0), jnp.float32(0.0)).astype(jnp.bfloat16)
             e1 = jnp.where(below, scores(i, q, flags), jnp.float32(0.0))
@@ -225,7 +236,9 @@
         w = jnp.concatenate([(near[i, n] * total[i][0:1]).astype(jnp.bfloat16) for n in range(2)], axis=0)
         out = dot(jnp.concatenate([vt[max(i - 1, 0)], vt[i]], axis=1), w) + summed[i]
         both = jnp.transpose(jnp.concatenate([out[:, :PAIRS], out[:, PAIRS:]], axis=0))
-        o_ref[SRC * i : SRC * i + SRC] = both.astype(jnp.bfloat16).reshape(SRC, 16, 128)
+        both = both.astype(jnp.bfloat16)
+        for n in range(SRC):
+            o_ref[PLACE[SRC * i + n]] = both[16 * n : 16 * n + 16]
 
 
 def take_kernel(x_ref, o_hbm, turned, out, sems):
@@ -288,6 +301,7 @@
         out_specs=VMEM,
         scratch_shapes=[
             pltpu.VMEM((NBLK + 1, HD, BLK), jnp.bfloat16),
+            pltpu.VMEM((NBLK, PAIRS, 128), jnp.bfloat16),
             pltpu.VMEM((NBLK, BLK, 128), jnp.bfloat16),
             pltpu.VMEM((NBLK, HD, BLK), jnp.bfloat16),
             pltpu.VMEM((NBLK, 2, BLK, BLK), jnp.float32),
@@ -317,21 +331,26 @@
     )(back)
 
 
+def exchange(x):
+    return lax.all_to_all(x, "run", split_axis=0, concat_axis=0, axis_index_groups=[ORDER], tiled=True)
+
+
 def body(queries, keys, values, doc_bounds, q_gain, k_gain):
     doc_bounds = doc_bounds.reshape(1, DOCS + 1)
     inputs = [jnp.transpose(x, (0, 2, 1)) for x in (queries, keys, values)]
     packed = send_call(doc_bounds, *inputs, q_gain, k_gain)
-    mine = lax.all_to_all(packed, AXES, split_axis=0, concat_axis=0, tiled=True)
+    mine = exchange(packed)
     result = attend_call(doc_bounds, mine)
-    back = lax.all_to_all(result, AXES, split_axis=0, concat_axis=0, tiled=True)
+    back = exchange(result)
     return jnp.transpose(take_call(back), (0, 2, 1))
 
 
 def solution(mesh):
-    tokens = P(("dp", "seqa", "seqb"), None, None)
+    runs = jax.sharding.Mesh(mesh.devices.reshape(len(PLACE), -1), ("run", "dp"))
+    tokens = P(("dp", "run"), None, None)
     return jax.shard_map(
         body,
-        mesh=mesh,
+        mesh=runs,
         in_specs=(tokens, tokens, tokens, P("dp"), P(), P()),
         out_specs=tokens,
         check_vma=False,

time: 149 us -> 150 us (level)
  no operation moved by 1% of the time
where the time goes in v7:
time: 150 us; the launch traced here: 148 us
  blocking collectives  139 us (93%)
  Pallas kernels  9.11 us (6%)
    all_to_all x2, blocking collectives, exchange(): lax.all_to_all(x, 'run', split_axis=0, concat_axis=0, axis_index_groups=[...  139 us
    pallas_call x1, Pallas kernels, attend_call(): pl.pallas_call(attend_kernel, out_shape=jax.ShapeDtypeStruct((SEQ // TOK,...  4.8 us

profile of v7, /device:TPU:1, one launch (start us, length us, event | category | flops | bytes accessed | tf_op | source)
XLA Modules:
  0.0 148.4 jit_solution(1829837279257399408)
XLA Ops:
  0.0 3.0 %send_side.1 = bf16[128,48,128]{2,1,0:T(8,128)(2,1)S(1)} custom-call(s32[1,9]{1,0:T(1,128)} %bitcast.7, bf16[32,64,128]{2,1,0:T(8,128)(2,1)} %bitcast.9, bf16[32,64,128]{2,1,0:T(8,128)(2,1)} %bitcast.10, bf16[32,64,128]{2,1,0:T(8,128)(2,1)} %bitcast.11, f32[1,64]{1,0:T(1,128)} %bitcast.12, f32[1,64]{1,0:T(1,128)} %bitcast.13), custom_call_target="tpu_custom_call" | custom-call | tf_op jit(solution)/shard_map/send_side/pallas_call | solution.py:278
  3.0 0.0 copy-start
  3.0 96.3 %all_to_all.10.x_ref = bf16[128,48,128]{2,1,0:T(8,128)(2,1)S(1)} all-to-all(bf16[128,48,128]{2,1,0:T(8,128)(2,1)S(1)} %send_side.1), channel_id=1, replica_groups={{0,32,8,40,16,48,24,56,448,480,456,488,464,496,472,504,388,420,396,428,..., dimensions={0} | all-to-all | bytes 3145728 | tf_op jit(solution)/shard_map/all_to_all | solution.py:335
  99.3 0.0 copy-done
  99.3 4.8 %attend.1 = bf16[128,16,128]{2,1,0:T(8,128)(2,1)S(1)} custom-call(s32[1,9]{1,0:T(1,128)S(1)} %bitcast.8, bf16[128,48,128]{2,1,0:T(8,128)(2,1)S(1)} %all_to_all.10.x_ref), custom_call_target="tpu_custom_call" | custom-call | tf_op jit(solution)/shard_map/attend/pallas_call | solution.py:297
  104.1 43.0 %all_to_all.11.x_ref = bf16[128,16,128]{2,1,0:T(8,128)(2,1)S(1)} all-to-all(bf16[128,16,128]{2,1,0:T(8,128)(2,1)S(1)} %attend.1), channel_id=1, replica_groups={{0,32,8,40,16,48,24,56,448,480,456,488,464,496,472,504,388,420,396,428,..., dimensions={0} | all-to-all | bytes 1048576 | tf_op jit(solution)/shard_map/all_to_all | solution.py:335
  147.1 1.3 take_side.1
Async XLA Ops:
  3.0 96.3 %copy-start = (s32[9]{0:T(128)S(1)}, s32[9]{0:T(128)}, u32[]{:S(2)}) copy-start(s32[9]{0:T(128)} %param.9) | copy-start | bytes 112

commit v8 on v7

--- a/solution.py
+++ b/solution.py
@@ -28,7 +28,7 @@
     return ((z % 8 * 2 + c) * 4 + x) * 2 + z // 8
 
 
-ORDER = [run_of(7 * z % 16, x, c) for z in range(16) for x in range(4) for c in range(2)]
+ORDER = [run_of(z, x, c) for x in range(4) for c in range(2) for z in range(16)]
 PLACE = [ORDER.index(s) for s in range(len(ORDER))]
 
 

time: 150 us -> 150 us (level)
  blocking collectives: 139 us -> 141 us
    all_to_all x2, blocking collectives: 139 us -> 141 us  [exchange(): lax.all_to_all(x, 'run', split_axis=0, concat_axis=0, axis_index_groups=[...]
where the time goes in v8:
time: 150 us
  blocking collectives  141 us (94%)
  Pallas kernels  8.59 us (6%)
    all_to_all x2, blocking collectives, exchange(): lax.all_to_all(x, 'run', split_axis=0, concat_axis=0, axis_index_groups=[...  141 us
    pallas_call x1, Pallas kernels, attend_call(): pl.pallas_call(attend_kernel, out_shape=jax.ShapeDtypeStruct((SEQ // TOK,...  4.28 us

profile of v8, /device:TPU:1, one launch (start us, length us, event | category | flops | bytes accessed | tf_op | source)
XLA Modules:
  0.0 149.7 jit_solution(7033086416119390533)
XLA Ops:
  0.0 3.0 %send_side.1 = bf16[128,48,128]{2,1,0:T(8,128)(2,1)S(1)} custom-call(s32[1,9]{1,0:T(1,128)} %bitcast.7, bf16[32,64,128]{2,1,0:T(8,128)(2,1)} %bitcast.9, bf16[32,64,128]{2,1,0:T(8,128)(2,1)} %bitcast.10, bf16[32,64,128]{2,1,0:T(8,128)(2,1)} %bitcast.11, f32[1,64]{1,0:T(1,128)} %bitcast.12, f32[1,64]{1,0:T(1,128)} %bitcast.13), custom_call_target="tpu_custom_call" | custom-call | tf_op jit(solution)/shard_map/send_side/pallas_call | solution.py:278
  3.0 0.0 copy-start
  3.0 95.0 %all_to_all.10.x_ref = bf16[128,48,128]{2,1,0:T(8,128)(2,1)S(1)} all-to-all(bf16[128,48,128]{2,1,0:T(8,128)(2,1)S(1)} %send_side.1), channel_id=1, replica_groups={{0,64,128,192,256,320,384,448,4,68,132,196,260,324,388,452,32,96,160,22..., dimensions={0} | all-to-all | bytes 3145728 | tf_op jit(solution)/shard_map/all_to_all | solution.py:335
  98.0 0.0 copy-done
  98.0 4.3 %attend.1 = bf16[128,16,128]{2,1,0:T(8,128)(2,1)S(1)} custom-call(s32[1,9]{1,0:T(1,128)S(1)} %bitcast.8, bf16[128,48,128]{2,1,0:T(8,128)(2,1)S(1)} %all_to_all.10.x_ref), custom_call_target="tpu_custom_call" | custom-call | tf_op jit(solution)/shard_map/attend/pallas_call | solution.py:297
  102.3 46.1 %all_to_all.11.x_ref = bf16[128,16,128]{2,1,0:T(8,128)(2,1)S(1)} all-to-all(bf16[128,16,128]{2,1,0:T(8,128)(2,1)S(1)} %attend.1), channel_id=1, replica_groups={{0,64,128,192,256,320,384,448,4,68,132,196,260,324,388,452,32,96,160,22..., dimensions={0} | all-to-all | bytes 1048576 | tf_op jit(solution)/shard_map/all_to_all | solution.py:335
  148.4 1.3 take_side.1
Async XLA Ops:
  3.0 95.0 %copy-start = (s32[9]{0:T(128)S(1)}, s32[9]{0:T(128)}, u32[]{:S(2)}) copy-start(s32[9]{0:T(128)} %param.9) | copy-start | bytes 112

commit v9 on v8

--- a/solution.py
+++ b/solution.py
@@ -28,7 +28,7 @@
     return ((z % 8 * 2 + c) * 4 + x) * 2 + z // 8
 
 
-ORDER = [run_of(z, x, c) for x in range(4) for c in range(2) for z in range(16)]
+ORDER = [run_of((8 + (n + 1) // 2 * (-1) ** n) % 16, x, c) for n in range(16) for x in range(4) for c in range(2)]
 PLACE = [ORDER.index(s) for s in range(len(ORDER))]
 
 

time: 150 us -> 144 us (0.960)
  blocking collectives: 141 us -> 135 us
    all_to_all x2, blocking collectives: 141 us -> 135 us  [exchange(): lax.all_to_all(x, 'run', split_axis=0, concat_axis=0, axis_index_groups=[...]
where the time goes in v9:
time: 144 us
  blocking collectives  135 us (94%)
  Pallas kernels  9.12 us (6%)
    all_to_all x2, blocking collectives, exchange(): lax.all_to_all(x, 'run', split_axis=0, concat_axis=0, axis_index_groups=[...  135 us
    pallas_call x1, Pallas kernels, attend_call(): pl.pallas_call(attend_kernel, out_shape=jax.ShapeDtypeStruct((SEQ // TOK,...  4.81 us
    pallas_call x1, Pallas kernels, send_call(): pl.pallas_call(send_kernel, out_shape=jax.ShapeDtypeStruct((HEADS, 48, 12...  3 us

profile of v9, /device:TPU:1, one launch (start us, length us, event | category | flops | bytes accessed | tf_op | source)
XLA Modules:
  0.0 144.0 jit_solution(114155808369187566)
XLA Ops:
  0.0 3.0 %send_side.1 = bf16[128,48,128]{2,1,0:T(8,128)(2,1)S(1)} custom-call(s32[1,9]{1,0:T(1,128)} %bitcast.7, bf16[32,64,128]{2,1,0:T(8,128)(2,1)} %bitcast.9, bf16[32,64,128]{2,1,0:T(8,128)(2,1)} %bitcast.10, bf16[32,64,128]{2,1,0:T(8,128)(2,1)} %bitcast.11, f32[1,64]{1,0:T(1,128)} %bitcast.12, f32[1,64]{1,0:T(1,128)} %bitcast.13), custom_call_target="tpu_custom_call" | custom-call | tf_op jit(solution)/shard_map/send_side/pallas_call | solution.py:278
  3.0 0.0 copy-start
  3.0 94.2 %all_to_all.10.x_ref = bf16[128,48,128]{2,1,0:T(8,128)(2,1)S(1)} all-to-all(bf16[128,48,128]{2,1,0:T(8,128)(2,1)S(1)} %send_side.1), channel_id=1, replica_groups={{4,36,12,44,20,52,28,60,448,480,456,488,464,496,472,504,68,100,76,108,8..., dimensions={0} | all-to-all | bytes 3145728 | tf_op jit(solution)/shard_map/all_to_all | solution.py:335
  97.2 0.0 copy-done
  97.2 4.8 %attend.1 = bf16[128,16,128]{2,1,0:T(8,128)(2,1)S(1)} custom-call(s32[1,9]{1,0:T(1,128)S(1)} %bitcast.8, bf16[128,48,128]{2,1,0:T(8,128)(2,1)S(1)} %all_to_all.10.x_ref), custom_call_target="tpu_custom_call" | custom-call | tf_op jit(solution)/shard_map/attend/pallas_call | solution.py:297
  102.0 40.7 %all_to_all.11.x_ref = bf16[128,16,128]{2,1,0:T(8,128)(2,1)S(1)} all-to-all(bf16[128,16,128]{2,1,0:T(8,128)(2,1)S(1)} %attend.1), channel_id=1, replica_groups={{4,36,12,44,20,52,28,60,448,480,456,488,464,496,472,504,68,100,76,108,8..., dimensions={0} | all-to-all | bytes 1048576 | tf_op jit(solution)/shard_map/all_to_all | solution.py:335
  142.7 1.3 take_side.1
Async XLA Ops:
  3.0 94.2 %copy-start = (s32[9]{0:T(128)S(1)}, s32[9]{0:T(128)}, u32[]{:S(2)}) copy-start(s32[9]{0:T(128)} %param.9) | copy-start | bytes 112

commit v10 on v9

--- a/solution.py
+++ b/solution.py
@@ -28,7 +28,7 @@
     return ((z % 8 * 2 + c) * 4 + x) * 2 + z // 8
 
 
-ORDER = [run_of((8 + (n + 1) // 2 * (-1) ** n) % 16, x, c) for n in range(16) for x in range(4) for c in range(2)]
+ORDER = [run_of((n + 1) // 2 * (-1) ** n % 16, x, c) for n in range(16) for x in range(4) for c in range(2)]
 PLACE = [ORDER.index(s) for s in range(len(ORDER))]
 
 

time: 144 us -> 150 us (1.042)
  blocking collectives: 135 us -> 141 us
    all_to_all x2, blocking collectives: 135 us -> 141 us  [exchange(): lax.all_to_all(x, 'run', split_axis=0, concat_axis=0, axis_index_groups=[...]
where the time goes in v10:
time: 150 us
  blocking collectives  141 us (94%)
  Pallas kernels  8.57 us (6%)
    all_to_all x2, blocking collectives, exchange(): lax.all_to_all(x, 'run', split_axis=0, concat_axis=0, axis_index_groups=[...  141 us
    pallas_call x1, Pallas kernels, attend_call(): pl.pallas_call(attend_kernel, out_shape=jax.ShapeDtypeStruct((SEQ // TOK,...  4.26 us

profile of v10, /device:TPU:1, one launch (start us, length us, event | category | flops | bytes accessed | tf_op | source)
XLA Modules:
  0.0 149.8 jit_solution(16208647056193649188)
XLA Ops:
  0.0 3.0 %send_side.1 = bf16[128,48,128]{2,1,0:T(8,128)(2,1)S(1)} custom-call(s32[1,9]{1,0:T(1,128)} %bitcast.7, bf16[32,64,128]{2,1,0:T(8,128)(2,1)} %bitcast.9, bf16[32,64,128]{2,1,0:T(8,128)(2,1)} %bitcast.10, bf16[32,64,128]{2,1,0:T(8,128)(2,1)} %bitcast.11, f32[1,64]{1,0:T(1,128)} %bitcast.12, f32[1,64]{1,0:T(1,128)} %bitcast.13), custom_call_target="tpu_custom_call" | custom-call | tf_op jit(solution)/shard_map/send_side/pallas_call | solution.py:278
  3.0 0.0 copy-start
  3.0 101.3 %all_to_all.10.x_ref = bf16[128,48,128]{2,1,0:T(8,128)(2,1)S(1)} all-to-all(bf16[128,48,128]{2,1,0:T(8,128)(2,1)S(1)} %send_side.1), channel_id=1, replica_groups={{0,32,8,40,16,48,24,56,452,484,460,492,468,500,476,508,64,96,72,104,80,..., dimensions={0} | all-to-all | bytes 3145728 | tf_op jit(solution)/shard_map/all_to_all | solution.py:335
  104.4 0.0 copy-done
  104.4 4.3 %attend.1 = bf16[128,16,128]{2,1,0:T(8,128)(2,1)S(1)} custom-call(s32[1,9]{1,0:T(1,128)S(1)} %bitcast.8, bf16[128,48,128]{2,1,0:T(8,128)(2,1)S(1)} %all_to_all.10.x_ref), custom_call_target="tpu_custom_call" | custom-call | tf_op jit(solution)/shard_map/attend/pallas_call | solution.py:297
  108.6 39.8 %all_to_all.11.x_ref = bf16[128,16,128]{2,1,0:T(8,128)(2,1)S(1)} all-to-all(bf16[128,16,128]{2,1,0:T(8,128)(2,1)S(1)} %attend.1), channel_id=1, replica_groups={{0,32,8,40,16,48,24,56,452,484,460,492,468,500,476,508,64,96,72,104,80,..., dimensions={0} | all-to-all | bytes 1048576 | tf_op jit(solution)/shard_map/all_to_all | solution.py:335
  148.4 1.3 take_side.1
Async XLA Ops:
  3.0 101.4 %copy-start = (s32[9]{0:T(128)S(1)}, s32[9]{0:T(128)}, u32[]{:S(2)}) copy-start(s32[9]{0:T(128)} %param.9) | copy-start | bytes 112

commit v11 on v10

--- a/solution.py
+++ b/solution.py
@@ -28,8 +28,12 @@
     return ((z % 8 * 2 + c) * 4 + x) * 2 + z // 8
 
 
-ORDER = [run_of((n + 1) // 2 * (-1) ** n % 16, x, c) for n in range(16) for x in range(4) for c in range(2)]
-PLACE = [ORDER.index(s) for s in range(len(ORDER))]
+FIRST_Z = [8, 7, 9, 6, 10, 5, 11, 4, 12, 3, 13, 2, 14, 1, 15, 0]
+THEN_Z = [0, 1, 2, 3, 4, 5, 6, 7, 8, 9, 10, 11, 12, 13, 14, 15]
+ORDER_IN = [run_of(z, x, c) for z in FIRST_Z for x in range(4) for c in range(2)]
+ORDER_OUT = [run_of(z, x, c) for z in THEN_Z for x in range(4) for c in range(2)]
+PLACE_IN = [ORDER_IN.index(s) for s in range(len(ORDER_IN))]
+PLACE_OUT = [ORDER_OUT.index(s) for s in range(len(ORDER_OUT))]
 
 
 def dot(a, b, dims=NN):
@@ -169,7 +173,7 @@
 
     def tiles(i, row):
         runs = range(SRC * i, SRC * i + SRC)
-        return jnp.concatenate([x_ref[PLACE[s], row : row + 16, :] for s in runs], axis=0)
+        return jnp.concatenate([x_ref[PLACE_IN[s], row : row + 16, :] for s in runs], axis=0)
 
     def near_scores(blocks):
         for i in blocks:
@@ -238,14 +242,15 @@
         both = jnp.transpose(jnp.concatenate([out[:, :PAIRS], out[:, PAIRS:]], axis=0))
         both = both.astype(jnp.bfloat16)
         for n in range(SRC):
-            o_ref[PLACE[SRC * i + n]] = both[16 * n : 16 * n + 16]
+            o_ref[PLACE_OUT[SRC * i + n]] = both[16 * n : 16 * n + 16]
 
 
 def take_kernel(x_ref, o_hbm, turned, out, sems):
     mix = interleave()
     eye = identity(128)
     for h in range(0, HEADS, 32):
-        part = jnp.concatenate([x_ref[h + m : h + m + 16].reshape(256, 128) for m in (0, 16)], axis=1)
+        tiles = [x_ref[PLACE_OUT[s]] for s in ORDER_IN[h : h + 32]]
+        part = jnp.concatenate([jnp.concatenate(tiles[m : m + 16], axis=0) for m in (0, 16)], axis=1)
         both = dot(mix, part).astype(jnp.bfloat16)
         for m in range(2):
             turned[:, h + 16 * m : h + 16 * m + 16, :] = both[:, 128 * m : 128 * m + 128].reshape(16, 16, 128)
@@ -331,22 +336,22 @@
     )(back)
 
 
-def exchange(x):
-    return lax.all_to_all(x, "run", split_axis=0, concat_axis=0, axis_index_groups=[ORDER], tiled=True)
+def exchange(x, order):
+    return lax.all_to_all(x, "run", split_axis=0, concat_axis=0, axis_index_groups=[order], tiled=True)
 
 
 def body(queries, keys, values, doc_bounds, q_gain, k_gain):
     doc_bounds = doc_bounds.reshape(1, DOCS + 1)
     inputs = [jnp.transpose(x, (0, 2, 1)) for x in (queries, keys, values)]
     packed = send_call(doc_bounds, *inputs, q_gain, k_gain)
-    mine = exchange(packed)
+    mine = exchange(packed, ORDER_IN)
     result = attend_call(doc_bounds, mine)
-    back = exchange(result)
+    back = exchange(result, ORDER_OUT)
     return jnp.transpose(take_call(back), (0, 2, 1))
 
 
 def solution(mesh):
-    runs = jax.sharding.Mesh(mesh.devices.reshape(len(PLACE), -1), ("run", "dp"))
+    runs = jax.sharding.Mesh(mesh.devices.reshape(len(ORDER_IN), -1), ("run", "dp"))
     tokens = P(("dp", "run"), None, None)
     return jax.shard_map(
         body,

time: 150 us -> 151 us (level)
  no operation moved by 1% of the time
where the time goes in v11:
time: 151 us; the launch traced here: 150 us
  blocking collectives  140 us (93%)
  Pallas kernels  9.83 us (7%)
    all_to_all x2, blocking collectives, exchange(): lax.all_to_all(x, 'run', split_axis=0, concat_axis=0, axis_index_groups=[...  140 us
    pallas_call x1, Pallas kernels, attend_call(): pl.pallas_call(attend_kernel, out_shape=jax.ShapeDtypeStruct((SEQ // TOK,...  5.51 us

profile of v11, /device:TPU:1, one launch (start us, length us, event | category | flops | bytes accessed | tf_op | source)
XLA Modules:
  0.0 149.7 jit_solution(6864052531304009211)
XLA Ops:
  0.0 3.0 %send_side.1 = bf16[128,48,128]{2,1,0:T(8,128)(2,1)S(1)} custom-call(s32[1,9]{1,0:T(1,128)} %bitcast.7, bf16[32,64,128]{2,1,0:T(8,128)(2,1)} %bitcast.9, bf16[32,64,128]{2,1,0:T(8,128)(2,1)} %bitcast.10, bf16[32,64,128]{2,1,0:T(8,128)(2,1)} %bitcast.11, f32[1,64]{1,0:T(1,128)} %bitcast.12, f32[1,64]{1,0:T(1,128)} %bitcast.13), custom_call_target="tpu_custom_call" | custom-call | tf_op jit(solution)/shard_map/send_side/pallas_call | solution.py:283
  3.0 0.0 copy-start
  3.0 94.2 %all_to_all.10.x_ref = bf16[128,48,128]{2,1,0:T(8,128)(2,1)S(1)} all-to-all(bf16[128,48,128]{2,1,0:T(8,128)(2,1)S(1)} %send_side.1), channel_id=1, replica_groups={{4,36,12,44,20,52,28,60,448,480,456,488,464,496,472,504,68,100,76,108,8..., dimensions={0} | all-to-all | bytes 3145728 | tf_op jit(solution)/shard_map/all_to_all | solution.py:340
  97.2 0.0 copy-done
  97.2 5.5 %attend.1 = bf16[128,16,128]{2,1,0:T(8,128)(2,1)S(1)} custom-call(s32[1,9]{1,0:T(1,128)S(1)} %bitcast.8, bf16[128,48,128]{2,1,0:T(8,128)(2,1)S(1)} %all_to_all.10.x_ref), custom_call_target="tpu_custom_call" | custom-call | tf_op jit(solution)/shard_map/attend/pallas_call | solution.py:302
  102.7 45.7 %all_to_all.11.x_ref = bf16[128,16,128]{2,1,0:T(8,128)(2,1)S(1)} all-to-all(bf16[128,16,128]{2,1,0:T(8,128)(2,1)S(1)} %attend.1), channel_id=1, replica_groups={{0,32,8,40,16,48,24,56,64,96,72,104,80,112,88,120,128,160,136,168,144,1..., dimensions={0} | all-to-all | bytes 1048576 | tf_op jit(solution)/shard_map/all_to_all | solution.py:340
  148.4 1.3 take_side.1
Async XLA Ops:
  3.0 94.2 %copy-start = (s32[9]{0:T(128)S(1)}, s32[9]{0:T(128)}, u32[]{:S(2)}) copy-start(s32[9]{0:T(128)} %param.9) | copy-start | bytes 112

commit v12 on v11

--- a/solution.py
+++ b/solution.py
@@ -29,7 +29,7 @@
 
 
 FIRST_Z = [8, 7, 9, 6, 10, 5, 11, 4, 12, 3, 13, 2, 14, 1, 15, 0]
-THEN_Z = [0, 1, 2, 3, 4, 5, 6, 7, 8, 9, 10, 11, 12, 13, 14, 15]
+THEN_Z = [0, 15, 1, 14, 2, 13, 3, 12, 4, 11, 5, 10, 6, 9, 7, 8]
 ORDER_IN = [run_of(z, x, c) for z in FIRST_Z for x in range(4) for c in range(2)]
 ORDER_OUT = [run_of(z, x, c) for z in THEN_Z for x in range(4) for c in range(2)]
 PLACE_IN = [ORDER_IN.index(s) for s in range(len(ORDER_IN))]

time: 151 us -> 153 us (1.013)
  blocking collectives: 140 us -> 143 us
    all_to_all x2, blocking collectives: 140 us -> 143 us  [exchange(): lax.all_to_all(x, 'run', split_axis=0, concat_axis=0, axis_index_groups=[...]
where the time goes in v12:
time: 153 us; the launch traced here: 152 us
  blocking collectives  143 us (93%)
  Pallas kernels  9.12 us (6%)
    all_to_all x2, blocking collectives, exchange(): lax.all_to_all(x, 'run', split_axis=0, concat_axis=0, axis_index_groups=[...  143 us
    pallas_call x1, Pallas kernels, attend_call(): pl.pallas_call(attend_kernel, out_shape=jax.ShapeDtypeStruct((SEQ // TOK,...  4.81 us

profile of v12, /device:TPU:1, one launch (start us, length us, event | category | flops | bytes accessed | tf_op | source)
XLA Modules:
  0.0 152.1 jit_solution(6413906632273813603)
XLA Ops:
  0.0 3.0 %send_side.1 = bf16[128,48,128]{2,1,0:T(8,128)(2,1)S(1)} custom-call(s32[1,9]{1,0:T(1,128)} %bitcast.7, bf16[32,64,128]{2,1,0:T(8,128)(2,1)} %bitcast.9, bf16[32,64,128]{2,1,0:T(8,128)(2,1)} %bitcast.10, bf16[32,64,128]{2,1,0:T(8,128)(2,1)} %bitcast.11, f32[1,64]{1,0:T(1,128)} %bitcast.12, f32[1,64]{1,0:T(1,128)} %bitcast.13), custom_call_target="tpu_custom_call" | custom-call | tf_op jit(solution)/shard_map/send_side/pallas_call | solution.py:283
  3.0 0.0 copy-start
  3.0 94.2 %all_to_all.10.x_ref = bf16[128,48,128]{2,1,0:T(8,128)(2,1)S(1)} all-to-all(bf16[128,48,128]{2,1,0:T(8,128)(2,1)S(1)} %send_side.1), channel_id=1, replica_groups={{4,36,12,44,20,52,28,60,448,480,456,488,464,496,472,504,68,100,76,108,8..., dimensions={0} | all-to-all | bytes 3145728 | tf_op jit(solution)/shard_map/all_to_all | solution.py:340
  97.2 0.0 copy-done
  97.2 4.8 %attend.1 = bf16[128,16,128]{2,1,0:T(8,128)(2,1)S(1)} custom-call(s32[1,9]{1,0:T(1,128)S(1)} %bitcast.8, bf16[128,48,128]{2,1,0:T(8,128)(2,1)S(1)} %all_to_all.10.x_ref), custom_call_target="tpu_custom_call" | custom-call | tf_op jit(solution)/shard_map/attend/pallas_call | solution.py:302
  102.0 48.8 %all_to_all.11.x_ref = bf16[128,16,128]{2,1,0:T(8,128)(2,1)S(1)} all-to-all(bf16[128,16,128]{2,1,0:T(8,128)(2,1)S(1)} %attend.1), channel_id=1, replica_groups={{0,32,8,40,16,48,24,56,452,484,460,492,468,500,476,508,64,96,72,104,80,..., dimensions={0} | all-to-all | bytes 1048576 | tf_op jit(solution)/shard_map/all_to_all | solution.py:340
  150.7 1.3 take_side.1
Async XLA Ops:
  3.0 94.2 %copy-start = (s32[9]{0:T(128)S(1)}, s32[9]{0:T(128)}, u32[]{:S(2)}) copy-start(s32[9]{0:T(128)} %param.9) | copy-start | bytes 112

commit v13 on v12

--- a/solution.py
+++ b/solution.py
@@ -28,8 +28,8 @@
     return ((z % 8 * 2 + c) * 4 + x) * 2 + z // 8
 
 
-FIRST_Z = [8, 7, 9, 6, 10, 5, 11, 4, 12, 3, 13, 2, 14, 1, 15, 0]
-THEN_Z = [0, 15, 1, 14, 2, 13, 3, 12, 4, 11, 5, 10, 6, 9, 7, 8]
+FIRST_Z = [11, 8, 5, 4, 1, 3, 9, 0, 12, 2, 13, 7, 15, 10, 6, 14]
+THEN_Z = [1, 3, 0, 8, 9, 15, 13, 10, 5, 7, 11, 2, 6, 4, 12, 14]
 ORDER_IN = [run_of(z, x, c) for z in FIRST_Z for x in range(4) for c in range(2)]
 ORDER_OUT = [run_of(z, x, c) for z in THEN_Z for x in range(4) for c in range(2)]
 PLACE_IN = [ORDER_IN.index(s) for s in range(len(ORDER_IN))]

time: 153 us -> 149 us (0.974)
  blocking collectives: 143 us -> 139 us
    all_to_all x2, blocking collectives: 143 us -> 139 us  [exchange(): lax.all_to_all(x, 'run', split_axis=0, concat_axis=0, axis_index_groups=[...]
where the time goes in v13:
time: 149 us
  blocking collectives  139 us (93%)
  Pallas kernels  9.34 us (6%)
    all_to_all x2, blocking collectives, exchange(): lax.all_to_all(x, 'run', split_axis=0, concat_axis=0, axis_index_groups=[...  139 us
    pallas_call x1, Pallas kernels, attend_call(): pl.pallas_call(attend_kernel, out_shape=jax.ShapeDtypeStruct((SEQ // TOK,...  5.03 us
    pallas_call x1, Pallas kernels, send_call(): pl.pallas_call(send_kernel, out_shape=jax.ShapeDtypeStruct((HEADS, 48, 12...  3 us

profile of v13, /device:TPU:1, one launch (start us, length us, event | category | flops | bytes accessed | tf_op | source)
XLA Modules:
  0.0 148.7 jit_solution(17326457778032168861)
XLA Ops:
  0.0 3.0 %send_side.1 = bf16[128,48,128]{2,1,0:T(8,128)(2,1)S(1)} custom-call(s32[1,9]{1,0:T(1,128)} %bitcast.7, bf16[32,64,128]{2,1,0:T(8,128)(2,1)} %bitcast.9, bf16[32,64,128]{2,1,0:T(8,128)(2,1)} %bitcast.10, bf16[32,64,128]{2,1,0:T(8,128)(2,1)} %bitcast.11, f32[1,64]{1,0:T(1,128)} %bitcast.12, f32[1,64]{1,0:T(1,128)} %bitcast.13), custom_call_target="tpu_custom_call" | custom-call | tf_op jit(solution)/shard_map/send_side/pallas_call | solution.py:283
  3.0 0.0 copy-start
  3.0 93.6 %all_to_all.10.x_ref = bf16[128,48,128]{2,1,0:T(8,128)(2,1)S(1)} all-to-all(bf16[128,48,128]{2,1,0:T(8,128)(2,1)S(1)} %send_side.1), channel_id=1, replica_groups={{196,228,204,236,212,244,220,252,4,36,12,44,20,52,28,60,320,352,328,360..., dimensions={0} | all-to-all | bytes 3145728 | tf_op jit(solution)/shard_map/all_to_all | solution.py:340
  96.7 0.0 copy-done
  96.7 5.0 %attend.1 = bf16[128,16,128]{2,1,0:T(8,128)(2,1)S(1)} custom-call(s32[1,9]{1,0:T(1,128)S(1)} %bitcast.8, bf16[128,48,128]{2,1,0:T(8,128)(2,1)S(1)} %all_to_all.10.x_ref), custom_call_target="tpu_custom_call" | custom-call | tf_op jit(solution)/shard_map/attend/pallas_call | solution.py:302
  101.7 45.7 %all_to_all.11.x_ref = bf16[128,16,128]{2,1,0:T(8,128)(2,1)S(1)} all-to-all(bf16[128,16,128]{2,1,0:T(8,128)(2,1)S(1)} %attend.1), channel_id=1, replica_groups={{64,96,72,104,80,112,88,120,192,224,200,232,208,240,216,248,0,32,8,40,1..., dimensions={0} | all-to-all | bytes 1048576 | tf_op jit(solution)/shard_map/all_to_all | solution.py:340
  147.4 1.3 take_side.1
Async XLA Ops:
  3.0 93.7 %copy-start = (s32[9]{0:T(128)S(1)}, s32[9]{0:T(128)}, u32[]{:S(2)}) copy-start(s32[9]{0:T(128)} %param.9) | copy-start | bytes 112

commit v14 on v12

--- a/solution.py
+++ b/solution.py
@@ -29,7 +29,7 @@
 
 
 FIRST_Z = [8, 7, 9, 6, 10, 5, 11, 4, 12, 3, 13, 2, 14, 1, 15, 0]
-THEN_Z = [0, 15, 1, 14, 2, 13, 3, 12, 4, 11, 5, 10, 6, 9, 7, 8]
+THEN_Z = [11, 10, 12, 9, 13, 8, 14, 7, 15, 6, 0, 5, 1, 4, 2, 3]
 ORDER_IN = [run_of(z, x, c) for z in FIRST_Z for x in range(4) for c in range(2)]
 ORDER_OUT = [run_of(z, x, c) for z in THEN_Z for x in range(4) for c in range(2)]
 PLACE_IN = [ORDER_IN.index(s) for s in range(len(ORDER_IN))]

time: 153 us -> 145 us (0.948)
  blocking collectives: 143 us -> 136 us
    all_to_all x2, blocking collectives: 143 us -> 136 us  [exchange(): lax.all_to_all(x, 'run', split_axis=0, concat_axis=0, axis_index_groups=[...]
where the time goes in v14:
time: 145 us
  blocking collectives  136 us (94%)
  Pallas kernels  8.58 us (6%)
    all_to_all x2, blocking collectives, exchange(): lax.all_to_all(x, 'run', split_axis=0, concat_axis=0, axis_index_groups=[...  136 us
    pallas_call x1, Pallas kernels, attend_call(): pl.pallas_call(attend_kernel, out_shape=jax.ShapeDtypeStruct((SEQ // TOK,...  4.27 us
    pallas_call x1, Pallas kernels, send_call(): pl.pallas_call(send_kernel, out_shape=jax.ShapeDtypeStruct((HEADS, 48, 12...  3 us

profile of v14, /device:TPU:1, one launch (start us, length us, event | category | flops | bytes accessed | tf_op | source)
XLA Modules:
  0.0 144.5 jit_solution(17619608909395270238)
XLA Ops:
  0.0 3.0 %send_side.1 = bf16[128,48,128]{2,1,0:T(8,128)(2,1)S(1)} custom-call(s32[1,9]{1,0:T(1,128)} %bitcast.7, bf16[32,64,128]{2,1,0:T(8,128)(2,1)} %bitcast.9, bf16[32,64,128]{2,1,0:T(8,128)(2,1)} %bitcast.10, bf16[32,64,128]{2,1,0:T(8,128)(2,1)} %bitcast.11, f32[1,64]{1,0:T(1,128)} %bitcast.12, f32[1,64]{1,0:T(1,128)} %bitcast.13), custom_call_target="tpu_custom_call" | custom-call | tf_op jit(solution)/shard_map/send_side/pallas_call | solution.py:283
  3.0 0.0 copy-start
  3.0 94.2 %all_to_all.10.x_ref = bf16[128,48,128]{2,1,0:T(8,128)(2,1)S(1)} all-to-all(bf16[128,48,128]{2,1,0:T(8,128)(2,1)S(1)} %send_side.1), channel_id=1, replica_groups={{4,36,12,44,20,52,28,60,448,480,456,488,464,496,472,504,68,100,76,108,8..., dimensions={0} | all-to-all | bytes 3145728 | tf_op jit(solution)/shard_map/all_to_all | solution.py:340
  97.2 0.0 copy-done
  97.2 4.3 %attend.1 = bf16[128,16,128]{2,1,0:T(8,128)(2,1)S(1)} custom-call(s32[1,9]{1,0:T(1,128)S(1)} %bitcast.8, bf16[128,48,128]{2,1,0:T(8,128)(2,1)S(1)} %all_to_all.10.x_ref), custom_call_target="tpu_custom_call" | custom-call | tf_op jit(solution)/shard_map/attend/pallas_call | solution.py:302
  101.4 41.7 %all_to_all.11.x_ref = bf16[128,16,128]{2,1,0:T(8,128)(2,1)S(1)} all-to-all(bf16[128,16,128]{2,1,0:T(8,128)(2,1)S(1)} %attend.1), channel_id=1, replica_groups={{196,228,204,236,212,244,220,252,132,164,140,172,148,180,156,188,260,29..., dimensions={0} | all-to-all | bytes 1048576 | tf_op jit(solution)/shard_map/all_to_all | solution.py:340
  143.2 1.3 take_side.1
Async XLA Ops:
  3.0 94.2 %copy-start = (s32[9]{0:T(128)S(1)}, s32[9]{0:T(128)}, u32[]{:S(2)}) copy-start(s32[9]{0:T(128)} %param.9) | copy-start | bytes 112

commit v15 on v14

--- a/solution.py
+++ b/solution.py
@@ -28,8 +28,8 @@
     return ((z % 8 * 2 + c) * 4 + x) * 2 + z // 8
 
 
-FIRST_Z = [8, 7, 9, 6, 10, 5, 11, 4, 12, 3, 13, 2, 14, 1, 15, 0]
-THEN_Z = [11, 10, 12, 9, 13, 8, 14, 7, 15, 6, 0, 5, 1, 4, 2, 3]
+FIRST_Z = [10, 9, 11, 8, 12, 7, 13, 6, 14, 5, 15, 4, 0, 3, 1, 2]
+THEN_Z = [6, 5, 7, 4, 8, 3, 9, 2, 10, 1, 11, 0, 12, 15, 13, 14]
 ORDER_IN = [run_of(z, x, c) for z in FIRST_Z for x in range(4) for c in range(2)]
 ORDER_OUT = [run_of(z, x, c) for z in THEN_Z for x in range(4) for c in range(2)]
 PLACE_IN = [ORDER_IN.index(s) for s in range(len(ORDER_IN))]

time: 145 us -> 147 us (1.014)
  no operation moved by 1% of the time
where the time goes in v15:
time: 147 us; the launch traced here: 146 us
  blocking collectives  137 us (93%)
  Pallas kernels  9.33 us (6%)
    all_to_all x2, blocking collectives, exchange(): lax.all_to_all(x, 'run', split_axis=0, concat_axis=0, axis_index_groups=[...  137 us
    pallas_call x1, Pallas kernels, attend_call(): pl.pallas_call(attend_kernel, out_shape=jax.ShapeDtypeStruct((SEQ // TOK,...  5.02 us
    pallas_call x1, Pallas kernels, send_call(): pl.pallas_call(send_kernel, out_shape=jax.ShapeDtypeStruct((HEADS, 48, 12...  3 us

profile of v15, /device:TPU:1, one launch (start us, length us, event | category | flops | bytes accessed | tf_op | source)
XLA Modules:
  0.0 146.3 jit_solution(15058255406669368894)
XLA Ops:
  0.0 3.0 %send_side.1 = bf16[128,48,128]{2,1,0:T(8,128)(2,1)S(1)} custom-call(s32[1,9]{1,0:T(1,128)} %bitcast.7, bf16[32,64,128]{2,1,0:T(8,128)(2,1)} %bitcast.9, bf16[32,64,128]{2,1,0:T(8,128)(2,1)} %bitcast.10, bf16[32,64,128]{2,1,0:T(8,128)(2,1)} %bitcast.11, f32[1,64]{1,0:T(1,128)} %bitcast.12, f32[1,64]{1,0:T(1,128)} %bitcast.13), custom_call_target="tpu_custom_call" | custom-call | tf_op jit(solution)/shard_map/send_side/pallas_call | solution.py:283
  3.0 0.0 copy-start
  3.0 91.9 %all_to_all.10.x_ref = bf16[128,48,128]{2,1,0:T(8,128)(2,1)S(1)} all-to-all(bf16[128,48,128]{2,1,0:T(8,128)(2,1)S(1)} %send_side.1), channel_id=1, replica_groups={{132,164,140,172,148,180,156,188,68,100,76,108,84,116,92,124,196,228,20..., dimensions={0} | all-to-all | bytes 3145728 | tf_op jit(solution)/shard_map/all_to_all | solution.py:340
  94.9 0.0 copy-done
  94.9 5.0 %attend.1 = bf16[128,16,128]{2,1,0:T(8,128)(2,1)S(1)} custom-call(s32[1,9]{1,0:T(1,128)S(1)} %bitcast.8, bf16[128,48,128]{2,1,0:T(8,128)(2,1)S(1)} %all_to_all.10.x_ref), custom_call_target="tpu_custom_call" | custom-call | tf_op jit(solution)/shard_map/attend/pallas_call | solution.py:302
  99.9 45.0 %all_to_all.11.x_ref = bf16[128,16,128]{2,1,0:T(8,128)(2,1)S(1)} all-to-all(bf16[128,16,128]{2,1,0:T(8,128)(2,1)S(1)} %attend.1), channel_id=1, replica_groups={{384,416,392,424,400,432,408,440,320,352,328,360,336,368,344,376,448,48..., dimensions={0} | all-to-all | bytes 1048576 | tf_op jit(solution)/shard_map/all_to_all | solution.py:340
  144.9 1.3 take_side.1
Async XLA Ops:
  3.0 91.9 %copy-start = (s32[9]{0:T(128)S(1)}, s32[9]{0:T(128)}, u32[]{:S(2)}) copy-start(s32[9]{0:T(128)} %param.9) | copy-start | bytes 112

commit v16 on v14

--- a/solution.py
+++ b/solution.py
@@ -29,7 +29,7 @@
 
 
 FIRST_Z = [8, 7, 9, 6, 10, 5, 11, 4, 12, 3, 13, 2, 14, 1, 15, 0]
-THEN_Z = [11, 10, 12, 9, 13, 8, 14, 7, 15, 6, 0, 5, 1, 4, 2, 3]
+THEN_Z = [8, 15, 6, 13, 4, 11, 2, 9, 0, 7, 14, 5, 12, 3, 10, 1]
 ORDER_IN = [run_of(z, x, c) for z in FIRST_Z for x in range(4) for c in range(2)]
 ORDER_OUT = [run_of(z, x, c) for z in THEN_Z for x in range(4) for c in range(2)]
 PLACE_IN = [ORDER_IN.index(s) for s in range(len(ORDER_IN))]

time: 145 us -> 144 us (level)
  no operation moved by 1% of the time
where the time goes in v16:
time: 144 us
  blocking collectives  135 us (94%)
  Pallas kernels  9.12 us (6%)
    all_to_all x2, blocking collectives, exchange(): lax.all_to_all(x, 'run', split_axis=0, concat_axis=0, axis_index_groups=[...  135 us
    pallas_call x1, Pallas kernels, attend_call(): pl.pallas_call(attend_kernel, out_shape=jax.ShapeDtypeStruct((SEQ // TOK,...  4.81 us
    pallas_call x1, Pallas kernels, send_call(): pl.pallas_call(send_kernel, out_shape=jax.ShapeDtypeStruct((HEADS, 48, 12...  3 us

profile of v16, /device:TPU:1, one launch (start us, length us, event | category | flops | bytes accessed | tf_op | source)
XLA Modules:
  0.0 144.0 jit_solution(16678821951692638002)
XLA Ops:
  0.0 3.0 %send_side.1 = bf16[128,48,128]{2,1,0:T(8,128)(2,1)S(1)} custom-call(s32[1,9]{1,0:T(1,128)} %bitcast.7, bf16[32,64,128]{2,1,0:T(8,128)(2,1)} %bitcast.9, bf16[32,64,128]{2,1,0:T(8,128)(2,1)} %bitcast.10, bf16[32,64,128]{2,1,0:T(8,128)(2,1)} %bitcast.11, f32[1,64]{1,0:T(1,128)} %bitcast.12, f32[1,64]{1,0:T(1,128)} %bitcast.13), custom_call_target="tpu_custom_call" | custom-call | tf_op jit(solution)/shard_map/send_side/pallas_call | solution.py:283
  3.0 0.0 copy-start
  3.0 94.2 %all_to_all.10.x_ref = bf16[128,48,128]{2,1,0:T(8,128)(2,1)S(1)} all-to-all(bf16[128,48,128]{2,1,0:T(8,128)(2,1)S(1)} %send_side.1), channel_id=1, replica_groups={{4,36,12,44,20,52,28,60,448,480,456,488,464,496,472,504,68,100,76,108,8..., dimensions={0} | all-to-all | bytes 3145728 | tf_op jit(solution)/shard_map/all_to_all | solution.py:340
  97.2 0.0 copy-done
  97.2 4.8 %attend.1 = bf16[128,16,128]{2,1,0:T(8,128)(2,1)S(1)} custom-call(s32[1,9]{1,0:T(1,128)S(1)} %bitcast.8, bf16[128,48,128]{2,1,0:T(8,128)(2,1)S(1)} %all_to_all.10.x_ref), custom_call_target="tpu_custom_call" | custom-call | tf_op jit(solution)/shard_map/attend/pallas_call | solution.py:302
  102.0 40.6 %all_to_all.11.x_ref = bf16[128,16,128]{2,1,0:T(8,128)(2,1)S(1)} all-to-all(bf16[128,16,128]{2,1,0:T(8,128)(2,1)S(1)} %attend.1), channel_id=1, replica_groups={{4,36,12,44,20,52,28,60,452,484,460,492,468,500,476,508,384,416,392,424..., dimensions={0} | all-to-all | bytes 1048576 | tf_op jit(solution)/shard_map/all_to_all | solution.py:340
  142.6 1.3 take_side.1
Async XLA Ops:
  3.0 94.2 %copy-start = (s32[9]{0:T(128)S(1)}, s32[9]{0:T(128)}, u32[]{:S(2)}) copy-start(s32[9]{0:T(128)} %param.9) | copy-start | bytes 112

commit v17 on v16

--- a/solution.py
+++ b/solution.py
@@ -30,8 +30,8 @@
 
 FIRST_Z = [8, 7, 9, 6, 10, 5, 11, 4, 12, 3, 13, 2, 14, 1, 15, 0]
 THEN_Z = [8, 15, 6, 13, 4, 11, 2, 9, 0, 7, 14, 5, 12, 3, 10, 1]
-ORDER_IN = [run_of(z, x, c) for z in FIRST_Z for x in range(4) for c in range(2)]
-ORDER_OUT = [run_of(z, x, c) for z in THEN_Z for x in range(4) for c in range(2)]
+ORDER_IN = [run_of(z, x, c) for z in FIRST_Z for x in range(4) for c in (1, 0)]
+ORDER_OUT = [run_of(z, x, c) for z in THEN_Z for x in range(4) for c in (1, 0)]
 PLACE_IN = [ORDER_IN.index(s) for s in range(len(ORDER_IN))]
 PLACE_OUT = [ORDER_OUT.index(s) for s in range(len(ORDER_OUT))]
 

time: 144 us -> 144 us (level)
  no operation moved by 1% of the time
where the time goes in v17:
time: 144 us
  blocking collectives  135 us (94%)
  Pallas kernels  8.55 us (6%)
    all_to_all x2, blocking collectives, exchange(): lax.all_to_all(x, 'run', split_axis=0, concat_axis=0, axis_index_groups=[...  135 us
    pallas_call x1, Pallas kernels, attend_call(): pl.pallas_call(attend_kernel, out_shape=jax.ShapeDtypeStruct((SEQ // TOK,...  4.24 us
    pallas_call x1, Pallas kernels, send_call(): pl.pallas_call(send_kernel, out_shape=jax.ShapeDtypeStruct((HEADS, 48, 12...  3 us

profile of v17, /device:TPU:1, one launch (start us, length us, event | category | flops | bytes accessed | tf_op | source)
XLA Modules:
  0.0 143.6 jit_solution(3659483467439513410)
XLA Ops:
  0.0 3.0 %send_side.1 = bf16[128,48,128]{2,1,0:T(8,128)(2,1)S(1)} custom-call(s32[1,9]{1,0:T(1,128)} %bitcast.7, bf16[32,64,128]{2,1,0:T(8,128)(2,1)} %bitcast.9, bf16[32,64,128]{2,1,0:T(8,128)(2,1)} %bitcast.10, bf16[32,64,128]{2,1,0:T(8,128)(2,1)} %bitcast.11, f32[1,64]{1,0:T(1,128)} %bitcast.12, f32[1,64]{1,0:T(1,128)} %bitcast.13), custom_call_target="tpu_custom_call" | custom-call | tf_op jit(solution)/shard_map/send_side/pallas_call | solution.py:283
  3.0 0.0 copy-start
  3.0 94.1 %all_to_all.10.x_ref = bf16[128,48,128]{2,1,0:T(8,128)(2,1)S(1)} all-to-all(bf16[128,48,128]{2,1,0:T(8,128)(2,1)S(1)} %send_side.1), channel_id=1, replica_groups={{36,4,44,12,52,20,60,28,480,448,488,456,496,464,504,472,100,68,108,76,1..., dimensions={0} | all-to-all | bytes 3145728 | tf_op jit(solution)/shard_map/all_to_all | solution.py:340
  97.1 0.0 copy-done
  97.1 4.2 %attend.1 = bf16[128,16,128]{2,1,0:T(8,128)(2,1)S(1)} custom-call(s32[1,9]{1,0:T(1,128)S(1)} %bitcast.8, bf16[128,48,128]{2,1,0:T(8,128)(2,1)S(1)} %all_to_all.10.x_ref), custom_call_target="tpu_custom_call" | custom-call | tf_op jit(solution)/shard_map/attend/pallas_call | solution.py:302
  101.3 41.0 %all_to_all.11.x_ref = bf16[128,16,128]{2,1,0:T(8,128)(2,1)S(1)} all-to-all(bf16[128,16,128]{2,1,0:T(8,128)(2,1)S(1)} %attend.1), channel_id=1, replica_groups={{36,4,44,12,52,20,60,28,484,452,492,460,500,468,508,476,416,384,424,392..., dimensions={0} | all-to-all | bytes 1048576 | tf_op jit(solution)/shard_map/all_to_all | solution.py:340
  142.3 1.3 take_side.1
Async XLA Ops:
  3.0 94.1 %copy-start = (s32[9]{0:T(128)S(1)}, s32[9]{0:T(128)}, u32[]{:S(2)}) copy-start(s32[9]{0:T(128)} %param.9) | copy-start | bytes 112

commit v18 on v17

--- a/solution.py
+++ b/solution.py
@@ -30,8 +30,8 @@
 
 FIRST_Z = [8, 7, 9, 6, 10, 5, 11, 4, 12, 3, 13, 2, 14, 1, 15, 0]
 THEN_Z = [8, 15, 6, 13, 4, 11, 2, 9, 0, 7, 14, 5, 12, 3, 10, 1]
-ORDER_IN = [run_of(z, x, c) for z in FIRST_Z for x in range(4) for c in (1, 0)]
-ORDER_OUT = [run_of(z, x, c) for z in THEN_Z for x in range(4) for c in (1, 0)]
+ORDER_IN = [run_of(z, x, c) for z in FIRST_Z for x in (2, 1, 3, 0) for c in range(2)]
+ORDER_OUT = [run_of(z, x, c) for z in THEN_Z for x in (2, 1, 3, 0) for c in range(2)]
 PLACE_IN = [ORDER_IN.index(s) for s in range(len(ORDER_IN))]
 PLACE_OUT = [ORDER_OUT.index(s) for s in range(len(ORDER_OUT))]
 

time: 144 us -> 141 us (0.979)
  blocking collectives: 135 us -> 132 us
    all_to_all x2, blocking collectives: 135 us -> 132 us  [exchange(): lax.all_to_all(x, 'run', split_axis=0, concat_axis=0, axis_index_groups=[...]
where the time goes in v18:
time: 141 us
  blocking collectives  132 us (94%)
  Pallas kernels  8.58 us (6%)
    all_to_all x2, blocking collectives, exchange(): lax.all_to_all(x, 'run', split_axis=0, concat_axis=0, axis_index_groups=[...  132 us
    pallas_call x1, Pallas kernels, attend_call(): pl.pallas_call(attend_kernel, out_shape=jax.ShapeDtypeStruct((SEQ // TOK,...  4.27 us
    pallas_call x1, Pallas kernels, send_call(): pl.pallas_call(send_kernel, out_shape=jax.ShapeDtypeStruct((HEADS, 48, 12...  3 us

profile of v18, /device:TPU:1, one launch (start us, length us, event | category | flops | bytes accessed | tf_op | source)
XLA Modules:
  0.0 140.5 jit_solution(7883417346956888461)
XLA Ops:
  0.0 3.0 %send_side.1 = bf16[128,48,128]{2,1,0:T(8,128)(2,1)S(1)} custom-call(s32[1,9]{1,0:T(1,128)} %bitcast.7, bf16[32,64,128]{2,1,0:T(8,128)(2,1)} %bitcast.9, bf16[32,64,128]{2,1,0:T(8,128)(2,1)} %bitcast.10, bf16[32,64,128]{2,1,0:T(8,128)(2,1)} %bitcast.11, f32[1,64]{1,0:T(1,128)} %bitcast.12, f32[1,64]{1,0:T(1,128)} %bitcast.13), custom_call_target="tpu_custom_call" | custom-call | tf_op jit(solution)/shard_map/send_side/pallas_call | solution.py:283
  3.0 0.0 copy-start
  3.0 92.9 %all_to_all.10.x_ref = bf16[128,48,128]{2,1,0:T(8,128)(2,1)S(1)} all-to-all(bf16[128,48,128]{2,1,0:T(8,128)(2,1)S(1)} %send_side.1), channel_id=1, replica_groups={{20,52,12,44,28,60,4,36,464,496,456,488,472,504,448,480,84,116,76,108,9..., dimensions={0} | all-to-all | bytes 3145728 | tf_op jit(solution)/shard_map/all_to_all | solution.py:340
  95.9 0.0 copy-done
  95.9 4.3 %attend.1 = bf16[128,16,128]{2,1,0:T(8,128)(2,1)S(1)} custom-call(s32[1,9]{1,0:T(1,128)S(1)} %bitcast.8, bf16[128,48,128]{2,1,0:T(8,128)(2,1)S(1)} %all_to_all.10.x_ref), custom_call_target="tpu_custom_call" | custom-call | tf_op jit(solution)/shard_map/attend/pallas_call | solution.py:302
  100.2 39.1 %all_to_all.11.x_ref = bf16[128,16,128]{2,1,0:T(8,128)(2,1)S(1)} all-to-all(bf16[128,16,128]{2,1,0:T(8,128)(2,1)S(1)} %attend.1), channel_id=1, replica_groups={{20,52,12,44,28,60,4,36,468,500,460,492,476,508,452,484,400,432,392,424..., dimensions={0} | all-to-all | bytes 1048576 | tf_op jit(solution)/shard_map/all_to_all | solution.py:340
  139.2 1.3 take_side.1
Async XLA Ops:
  3.0 92.9 %copy-start = (s32[9]{0:T(128)S(1)}, s32[9]{0:T(128)}, u32[]{:S(2)}) copy-start(s32[9]{0:T(128)} %param.9) | copy-start | bytes 112

commit v19 on v18

--- a/solution.py
+++ b/solution.py
@@ -28,8 +28,8 @@
     return ((z % 8 * 2 + c) * 4 + x) * 2 + z // 8
 
 
-FIRST_Z = [8, 7, 9, 6, 10, 5, 11, 4, 12, 3, 13, 2, 14, 1, 15, 0]
-THEN_Z = [8, 15, 6, 13, 4, 11, 2, 9, 0, 7, 14, 5, 12, 3, 10, 1]
+FIRST_Z = [9, 8, 10, 7, 11, 6, 12, 5, 13, 4, 14, 3, 15, 2, 0, 1]
+THEN_Z = [8, 7, 9, 6, 10, 5, 11, 4, 12, 3, 13, 2, 14, 1, 15, 0]
 ORDER_IN = [run_of(z, x, c) for z in FIRST_Z for x in (2, 1, 3, 0) for c in range(2)]
 ORDER_OUT = [run_of(z, x, c) for z in THEN_Z for x in (2, 1, 3, 0) for c in range(2)]
 PLACE_IN = [ORDER_IN.index(s) for s in range(len(ORDER_IN))]

time: 141 us -> 142 us (level)
  no operation moved by 1% of the time
where the time goes in v19:
time: 142 us
  blocking collectives  132 us (93%)
  Pallas kernels  9.35 us (7%)
    all_to_all x2, blocking collectives, exchange(): lax.all_to_all(x, 'run', split_axis=0, concat_axis=0, axis_index_groups=[...  132 us
    pallas_call x1, Pallas kernels, attend_call(): pl.pallas_call(attend_kernel, out_shape=jax.ShapeDtypeStruct((SEQ // TOK,...  5.04 us
    pallas_call x1, Pallas kernels, send_call(): pl.pallas_call(send_kernel, out_shape=jax.ShapeDtypeStruct((HEADS, 48, 12...  3 us

profile of v19, /device:TPU:1, one launch (start us, length us, event | category | flops | bytes accessed | tf_op | source)
XLA Modules:
  0.0 141.6 jit_solution(9153801080254109772)
XLA Ops:
  0.0 3.0 %send_side.1 = bf16[128,48,128]{2,1,0:T(8,128)(2,1)S(1)} custom-call(s32[1,9]{1,0:T(1,128)} %bitcast.7, bf16[32,64,128]{2,1,0:T(8,128)(2,1)} %bitcast.9, bf16[32,64,128]{2,1,0:T(8,128)(2,1)} %bitcast.10, bf16[32,64,128]{2,1,0:T(8,128)(2,1)} %bitcast.11, f32[1,64]{1,0:T(1,128)} %bitcast.12, f32[1,64]{1,0:T(1,128)} %bitcast.13), custom_call_target="tpu_custom_call" | custom-call | tf_op jit(solution)/shard_map/send_side/pallas_call | solution.py:283
  3.0 0.0 copy-start
  3.0 92.0 %all_to_all.10.x_ref = bf16[128,48,128]{2,1,0:T(8,128)(2,1)S(1)} all-to-all(bf16[128,48,128]{2,1,0:T(8,128)(2,1)S(1)} %send_side.1), channel_id=1, replica_groups={{84,116,76,108,92,124,68,100,20,52,12,44,28,60,4,36,148,180,140,172,156..., dimensions={0} | all-to-all | bytes 3145728 | tf_op jit(solution)/shard_map/all_to_all | solution.py:340
  95.0 0.0 copy-done
  95.0 5.0 %attend.1 = bf16[128,16,128]{2,1,0:T(8,128)(2,1)S(1)} custom-call(s32[1,9]{1,0:T(1,128)S(1)} %bitcast.8, bf16[128,48,128]{2,1,0:T(8,128)(2,1)S(1)} %all_to_all.10.x_ref), custom_call_target="tpu_custom_call" | custom-call | tf_op jit(solution)/shard_map/attend/pallas_call | solution.py:302
  100.1 40.2 %all_to_all.11.x_ref = bf16[128,16,128]{2,1,0:T(8,128)(2,1)S(1)} all-to-all(bf16[128,16,128]{2,1,0:T(8,128)(2,1)S(1)} %attend.1), channel_id=1, replica_groups={{20,52,12,44,28,60,4,36,464,496,456,488,472,504,448,480,84,116,76,108,9..., dimensions={0} | all-to-all | bytes 1048576 | tf_op jit(solution)/shard_map/all_to_all | solution.py:340
  140.3 1.3 take_side.1
Async XLA Ops:
  3.0 92.0 %copy-start = (s32[9]{0:T(128)S(1)}, s32[9]{0:T(128)}, u32[]{:S(2)}) copy-start(s32[9]{0:T(128)} %param.9) | copy-start | bytes 112

commit v20 on v19

--- a/solution.py
+++ b/solution.py
@@ -28,8 +28,8 @@
     return ((z % 8 * 2 + c) * 4 + x) * 2 + z // 8
 
 
-FIRST_Z = [9, 8, 10, 7, 11, 6, 12, 5, 13, 4, 14, 3, 15, 2, 0, 1]
-THEN_Z = [8, 7, 9, 6, 10, 5, 11, 4, 12, 3, 13, 2, 14, 1, 15, 0]
+FIRST_Z = [8, 15, 6, 13, 4, 11, 2, 9, 0, 7, 14, 5, 12, 3, 10, 1]
+THEN_Z = [8, 1, 10, 3, 12, 5, 14, 7, 0, 9, 2, 11, 4, 13, 6, 15]
 ORDER_IN = [run_of(z, x, c) for z in FIRST_Z for x in (2, 1, 3, 0) for c in range(2)]
 ORDER_OUT = [run_of(z, x, c) for z in THEN_Z for x in (2, 1, 3, 0) for c in range(2)]
 PLACE_IN = [ORDER_IN.index(s) for s in range(len(ORDER_IN))]

time: 142 us -> 142 us (level)
  no operation moved by 1% of the time
where the time goes in v20:
time: 142 us
  blocking collectives  132 us (93%)
  Pallas kernels  9.84 us (7%)
    all_to_all x2, blocking collectives, exchange(): lax.all_to_all(x, 'run', split_axis=0, concat_axis=0, axis_index_groups=[...  132 us
    pallas_call x1, Pallas kernels, attend_call(): pl.pallas_call(attend_kernel, out_shape=jax.ShapeDtypeStruct((SEQ // TOK,...  5.53 us
    pallas_call x1, Pallas kernels, send_call(): pl.pallas_call(send_kernel, out_shape=jax.ShapeDtypeStruct((HEADS, 48, 12...  3 us

profile of v20, /device:TPU:1, one launch (start us, length us, event | category | flops | bytes accessed | tf_op | source)
XLA Modules:
  0.0 142.2 jit_solution(11777732788834786112)
XLA Ops:
  0.0 3.0 %send_side.1 = bf16[128,48,128]{2,1,0:T(8,128)(2,1)S(1)} custom-call(s32[1,9]{1,0:T(1,128)} %bitcast.7, bf16[32,64,128]{2,1,0:T(8,128)(2,1)} %bitcast.9, bf16[32,64,128]{2,1,0:T(8,128)(2,1)} %bitcast.10, bf16[32,64,128]{2,1,0:T(8,128)(2,1)} %bitcast.11, f32[1,64]{1,0:T(1,128)} %bitcast.12, f32[1,64]{1,0:T(1,128)} %bitcast.13), custom_call_target="tpu_custom_call" | custom-call | tf_op jit(solution)/shard_map/send_side/pallas_call | solution.py:283
  3.0 0.0 copy-start
  3.0 92.3 %all_to_all.10.x_ref = bf16[128,48,128]{2,1,0:T(8,128)(2,1)S(1)} all-to-all(bf16[128,48,128]{2,1,0:T(8,128)(2,1)S(1)} %send_side.1), channel_id=1, replica_groups={{20,52,12,44,28,60,4,36,468,500,460,492,476,508,452,484,400,432,392,424..., dimensions={0} | all-to-all | bytes 3145728 | tf_op jit(solution)/shard_map/all_to_all | solution.py:340
  95.3 0.0 copy-done
  95.3 5.5 %attend.1 = bf16[128,16,128]{2,1,0:T(8,128)(2,1)S(1)} custom-call(s32[1,9]{1,0:T(1,128)S(1)} %bitcast.8, bf16[128,48,128]{2,1,0:T(8,128)(2,1)S(1)} %all_to_all.10.x_ref), custom_call_target="tpu_custom_call" | custom-call | tf_op jit(solution)/shard_map/attend/pallas_call | solution.py:302
  100.9 40.0 %all_to_all.11.x_ref = bf16[128,16,128]{2,1,0:T(8,128)(2,1)S(1)} all-to-all(bf16[128,16,128]{2,1,0:T(8,128)(2,1)S(1)} %attend.1), channel_id=1, replica_groups={{20,52,12,44,28,60,4,36,80,112,72,104,88,120,64,96,148,180,140,172,156,..., dimensions={0} | all-to-all | bytes 1048576 | tf_op jit(solution)/shard_map/all_to_all | solution.py:340
  140.8 1.3 take_side.1
Async XLA Ops:
  3.0 92.3 %copy-start = (s32[9]{0:T(128)S(1)}, s32[9]{0:T(128)}, u32[]{:S(2)}) copy-start(s32[9]{0:T(128)} %param.9) | copy-start | bytes 112

commit v21 on v19

--- a/solution.py
+++ b/solution.py
@@ -29,7 +29,7 @@
 
 
 FIRST_Z = [9, 8, 10, 7, 11, 6, 12, 5, 13, 4, 14, 3, 15, 2, 0, 1]
-THEN_Z = [8, 7, 9, 6, 10, 5, 11, 4, 12, 3, 13, 2, 14, 1, 15, 0]
+THEN_Z = [8, 15, 6, 13, 4, 11, 2, 9, 0, 7, 14, 5, 12, 3, 10, 1]
 ORDER_IN = [run_of(z, x, c) for z in FIRST_Z for x in (2, 1, 3, 0) for c in range(2)]
 ORDER_OUT = [run_of(z, x, c) for z in THEN_Z for x in (2, 1, 3, 0) for c in range(2)]
 PLACE_IN = [ORDER_IN.index(s) for s in range(len(ORDER_IN))]

time: 142 us -> 142 us (level)
  no operation moved by 1% of the time
where the time goes in v21:
time: 142 us
  blocking collectives  133 us (94%)
  Pallas kernels  9.35 us (7%)
    all_to_all x2, blocking collectives, exchange(): lax.all_to_all(x, 'run', split_axis=0, concat_axis=0, axis_index_groups=[...  133 us
    pallas_call x1, Pallas kernels, attend_call(): pl.pallas_call(attend_kernel, out_shape=jax.ShapeDtypeStruct((SEQ // TOK,...  5.04 us
    pallas_call x1, Pallas kernels, send_call(): pl.pallas_call(send_kernel, out_shape=jax.ShapeDtypeStruct((HEADS, 48, 12...  3 us

profile of v21, /device:TPU:1, one launch (start us, length us, event | category | flops | bytes accessed | tf_op | source)
XLA Modules:
  0.0 142.1 jit_solution(7236859996350757659)
XLA Ops:
  0.0 3.0 %send_side.1 = bf16[128,48,128]{2,1,0:T(8,128)(2,1)S(1)} custom-call(s32[1,9]{1,0:T(1,128)} %bitcast.7, bf16[32,64,128]{2,1,0:T(8,128)(2,1)} %bitcast.9, bf16[32,64,128]{2,1,0:T(8,128)(2,1)} %bitcast.10, bf16[32,64,128]{2,1,0:T(8,128)(2,1)} %bitcast.11, f32[1,64]{1,0:T(1,128)} %bitcast.12, f32[1,64]{1,0:T(1,128)} %bitcast.13), custom_call_target="tpu_custom_call" | custom-call | tf_op jit(solution)/shard_map/send_side/pallas_call | solution.py:283
  3.0 0.0 copy-start
  3.0 92.0 %all_to_all.10.x_ref = bf16[128,48,128]{2,1,0:T(8,128)(2,1)S(1)} all-to-all(bf16[128,48,128]{2,1,0:T(8,128)(2,1)S(1)} %send_side.1), channel_id=1, replica_groups={{84,116,76,108,92,124,68,100,20,52,12,44,28,60,4,36,148,180,140,172,156..., dimensions={0} | all-to-all | bytes 3145728 | tf_op jit(solution)/shard_map/all_to_all | solution.py:340
  95.0 0.0 copy-done
  95.0 5.0 %attend.1 = bf16[128,16,128]{2,1,0:T(8,128)(2,1)S(1)} custom-call(s32[1,9]{1,0:T(1,128)S(1)} %bitcast.8, bf16[128,48,128]{2,1,0:T(8,128)(2,1)S(1)} %all_to_all.10.x_ref), custom_call_target="tpu_custom_call" | custom-call | tf_op jit(solution)/shard_map/attend/pallas_call | solution.py:302
  100.1 40.7 %all_to_all.11.x_ref = bf16[128,16,128]{2,1,0:T(8,128)(2,1)S(1)} all-to-all(bf16[128,16,128]{2,1,0:T(8,128)(2,1)S(1)} %attend.1), channel_id=1, replica_groups={{20,52,12,44,28,60,4,36,468,500,460,492,476,508,452,484,400,432,392,424..., dimensions={0} | all-to-all | bytes 1048576 | tf_op jit(solution)/shard_map/all_to_all | solution.py:340
  140.8 1.3 take_side.1
Async XLA Ops:
  3.0 92.0 %copy-start = (s32[9]{0:T(128)S(1)}, s32[9]{0:T(128)}, u32[]{:S(2)}) copy-start(s32[9]{0:T(128)} %param.9) | copy-start | bytes 112

commit v22 on v18

--- a/solution.py
+++ b/solution.py
@@ -30,8 +30,8 @@
 
 FIRST_Z = [8, 7, 9, 6, 10, 5, 11, 4, 12, 3, 13, 2, 14, 1, 15, 0]
 THEN_Z = [8, 15, 6, 13, 4, 11, 2, 9, 0, 7, 14, 5, 12, 3, 10, 1]
-ORDER_IN = [run_of(z, x, c) for z in FIRST_Z for x in (2, 1, 3, 0) for c in range(2)]
-ORDER_OUT = [run_of(z, x, c) for z in THEN_Z for x in (2, 1, 3, 0) for c in range(2)]
+ORDER_IN = [run_of(z, x, c) for x in (2, 1, 3, 0) for z in FIRST_Z for c in range(2)]
+ORDER_OUT = [run_of(z, x, c) for c in range(2) for z in THEN_Z for x in (2, 1, 3, 0)]
 PLACE_IN = [ORDER_IN.index(s) for s in range(len(ORDER_IN))]
 PLACE_OUT = [ORDER_OUT.index(s) for s in range(len(ORDER_OUT))]
 

time: 141 us -> 143 us (1.014)
  no operation moved by 1% of the time
where the time goes in v22:
time: 143 us; the launch traced here: 142 us
  blocking collectives  133 us (93%)
  Pallas kernels  9.32 us (7%)
    all_to_all x2, blocking collectives, exchange(): lax.all_to_all(x, 'run', split_axis=0, concat_axis=0, axis_index_groups=[...  133 us
    pallas_call x1, Pallas kernels, attend_call(): pl.pallas_call(attend_kernel, out_shape=jax.ShapeDtypeStruct((SEQ // TOK,...  5.02 us
    pallas_call x1, Pallas kernels, send_call(): pl.pallas_call(send_kernel, out_shape=jax.ShapeDtypeStruct((HEADS, 48, 12...  3 us

profile of v22, /device:TPU:1, one launch (start us, length us, event | category | flops | bytes accessed | tf_op | source)
XLA Modules:
  0.0 142.1 jit_solution(13026666265066013454)
XLA Ops:
  0.0 3.0 %send_side.1 = bf16[128,48,128]{2,1,0:T(8,128)(2,1)S(1)} custom-call(s32[1,9]{1,0:T(1,128)} %bitcast.7, bf16[32,64,128]{2,1,0:T(8,128)(2,1)} %bitcast.9, bf16[32,64,128]{2,1,0:T(8,128)(2,1)} %bitcast.10, bf16[32,64,128]{2,1,0:T(8,128)(2,1)} %bitcast.11, f32[1,64]{1,0:T(1,128)} %bitcast.12, f32[1,64]{1,0:T(1,128)} %bitcast.13), custom_call_target="tpu_custom_call" | custom-call | tf_op jit(solution)/shard_map/send_side/pallas_call | solution.py:283
  3.0 0.0 copy-start
  3.0 92.3 %all_to_all.10.x_ref = bf16[128,48,128]{2,1,0:T(8,128)(2,1)S(1)} all-to-all(bf16[128,48,128]{2,1,0:T(8,128)(2,1)S(1)} %send_side.1), channel_id=1, replica_groups={{20,52,464,496,84,116,400,432,148,180,336,368,212,244,272,304,276,308,2..., dimensions={0} | all-to-all | bytes 3145728 | tf_op jit(solution)/shard_map/all_to_all | solution.py:340
  95.4 0.0 copy-done
  95.4 5.0 %attend.1 = bf16[128,16,128]{2,1,0:T(8,128)(2,1)S(1)} custom-call(s32[1,9]{1,0:T(1,128)S(1)} %bitcast.8, bf16[128,48,128]{2,1,0:T(8,128)(2,1)S(1)} %all_to_all.10.x_ref), custom_call_target="tpu_custom_call" | custom-call | tf_op jit(solution)/shard_map/attend/pallas_call | solution.py:302
  100.4 40.5 %all_to_all.11.x_ref = bf16[128,16,128]{2,1,0:T(8,128)(2,1)S(1)} all-to-all(bf16[128,16,128]{2,1,0:T(8,128)(2,1)S(1)} %attend.1), channel_id=1, replica_groups={{20,12,28,4,468,460,476,452,400,392,408,384,340,332,348,324,272,264,280..., dimensions={0} | all-to-all | bytes 1048576 | tf_op jit(solution)/shard_map/all_to_all | solution.py:340
  140.8 1.3 take_side.1
Async XLA Ops:
  3.0 92.4 %copy-start = (s32[9]{0:T(128)S(1)}, s32[9]{0:T(128)}, u32[]{:S(2)}) copy-start(s32[9]{0:T(128)} %param.9) | copy-start | bytes 112

commit v23 on v21

--- a/solution.py
+++ b/solution.py
@@ -28,7 +28,7 @@
     return ((z % 8 * 2 + c) * 4 + x) * 2 + z // 8
 
 
-FIRST_Z = [9, 8, 10, 7, 11, 6, 12, 5, 13, 4, 14, 3, 15, 2, 0, 1]
+FIRST_Z = [8, 15, 6, 13, 4, 11, 2, 9, 0, 7, 14, 5, 12, 3, 10, 1]
 THEN_Z = [8, 15, 6, 13, 4, 11, 2, 9, 0, 7, 14, 5, 12, 3, 10, 1]
 ORDER_IN = [run_of(z, x, c) for z in FIRST_Z for x in (2, 1, 3, 0) for c in range(2)]
 ORDER_OUT = [run_of(z, x, c) for z in THEN_Z for x in (2, 1, 3, 0) for c in range(2)]

time: 142 us -> 142 us (level)
  no operation moved by 1% of the time
where the time goes in v23:
time: 142 us
  blocking collectives  133 us (94%)
  Pallas kernels  9.35 us (7%)
    all_to_all x2, blocking collectives, exchange(): lax.all_to_all(x, 'run', split_axis=0, concat_axis=0, axis_index_groups=[...  133 us
    pallas_call x1, Pallas kernels, attend_call(): pl.pallas_call(attend_kernel, out_shape=jax.ShapeDtypeStruct((SEQ // TOK,...  5.04 us
    pallas_call x1, Pallas kernels, send_call(): pl.pallas_call(send_kernel, out_shape=jax.ShapeDtypeStruct((HEADS, 48, 12...  3 us

profile of v23, /device:TPU:1, one launch (start us, length us, event | category | flops | bytes accessed | tf_op | source)
XLA Modules:
  0.0 142.1 jit_solution(4789394243504991465)
XLA Ops:
  0.0 3.0 %send_side.1 = bf16[128,48,128]{2,1,0:T(8,128)(2,1)S(1)} custom-call(s32[1,9]{1,0:T(1,128)} %bitcast.7, bf16[32,64,128]{2,1,0:T(8,128)(2,1)} %bitcast.9, bf16[32,64,128]{2,1,0:T(8,128)(2,1)} %bitcast.10, bf16[32,64,128]{2,1,0:T(8,128)(2,1)} %bitcast.11, f32[1,64]{1,0:T(1,128)} %bitcast.12, f32[1,64]{1,0:T(1,128)} %bitcast.13), custom_call_target="tpu_custom_call" | custom-call | tf_op jit(solution)/shard_map/send_side/pallas_call | solution.py:283
  3.0 0.0 copy-start
  3.0 92.3 %all_to_all.10.x_ref = bf16[128,48,128]{2,1,0:T(8,128)(2,1)S(1)} all-to-all(bf16[128,48,128]{2,1,0:T(8,128)(2,1)S(1)} %send_side.1), channel_id=1, replica_groups={{20,52,12,44,28,60,4,36,468,500,460,492,476,508,452,484,400,432,392,424..., dimensions={0} | all-to-all | bytes 3145728 | tf_op jit(solution)/shard_map/all_to_all | solution.py:340
  95.3 0.0 copy-done
  95.3 5.0 %attend.1 = bf16[128,16,128]{2,1,0:T(8,128)(2,1)S(1)} custom-call(s32[1,9]{1,0:T(1,128)S(1)} %bitcast.8, bf16[128,48,128]{2,1,0:T(8,128)(2,1)S(1)} %all_to_all.10.x_ref), custom_call_target="tpu_custom_call" | custom-call | tf_op jit(solution)/shard_map/attend/pallas_call | solution.py:302
  100.4 40.4 %all_to_all.11.x_ref = bf16[128,16,128]{2,1,0:T(8,128)(2,1)S(1)} all-to-all(bf16[128,16,128]{2,1,0:T(8,128)(2,1)S(1)} %attend.1), channel_id=1, replica_groups={{20,52,12,44,28,60,4,36,468,500,460,492,476,508,452,484,400,432,392,424..., dimensions={0} | all-to-all | bytes 1048576 | tf_op jit(solution)/shard_map/all_to_all | solution.py:340
  140.8 1.3 take_side.1
Async XLA Ops:
  3.0 92.3 %copy-start = (s32[9]{0:T(128)S(1)}, s32[9]{0:T(128)}, u32[]{:S(2)}) copy-start(s32[9]{0:T(128)} %param.9) | copy-start | bytes 112

commit v24 on v23

--- a/solution.py
+++ b/solution.py
@@ -28,8 +28,8 @@
     return ((z % 8 * 2 + c) * 4 + x) * 2 + z // 8
 
 
-FIRST_Z = [8, 15, 6, 13, 4, 11, 2, 9, 0, 7, 14, 5, 12, 3, 10, 1]
-THEN_Z = [8, 15, 6, 13, 4, 11, 2, 9, 0, 7, 14, 5, 12, 3, 10, 1]
+FIRST_Z = [10, 5, 11, 4, 12, 3, 13, 2, 14, 1, 15, 0, 8, 7, 9, 6]
+THEN_Z = [10, 1, 8, 15, 6, 13, 4, 11, 2, 9, 0, 7, 14, 5, 12, 3]
 ORDER_IN = [run_of(z, x, c) for z in FIRST_Z for x in (2, 1, 3, 0) for c in range(2)]
 ORDER_OUT = [run_of(z, x, c) for z in THEN_Z for x in (2, 1, 3, 0) for c in range(2)]
 PLACE_IN = [ORDER_IN.index(s) for s in range(len(ORDER_IN))]

time: 142 us -> 142 us (level)
  no operation moved by 1% of the time
where the time goes in v24:
time: 142 us
  blocking collectives  132 us (93%)
  Pallas kernels  9.1 us (6%)
    all_to_all x2, blocking collectives, exchange(): lax.all_to_all(x, 'run', split_axis=0, concat_axis=0, axis_index_groups=[...  132 us
    pallas_call x1, Pallas kernels, attend_call(): pl.pallas_call(attend_kernel, out_shape=jax.ShapeDtypeStruct((SEQ // TOK,...  4.79 us
    pallas_call x1, Pallas kernels, send_call(): pl.pallas_call(send_kernel, out_shape=jax.ShapeDtypeStruct((HEADS, 48, 12...  3 us

profile of v24, /device:TPU:1, one launch (start us, length us, event | category | flops | bytes accessed | tf_op | source)
XLA Modules:
  0.0 141.6 jit_solution(5381372044250240613)
XLA Ops:
  0.0 3.0 %send_side.1 = bf16[128,48,128]{2,1,0:T(8,128)(2,1)S(1)} custom-call(s32[1,9]{1,0:T(1,128)} %bitcast.7, bf16[32,64,128]{2,1,0:T(8,128)(2,1)} %bitcast.9, bf16[32,64,128]{2,1,0:T(8,128)(2,1)} %bitcast.10, bf16[32,64,128]{2,1,0:T(8,128)(2,1)} %bitcast.11, f32[1,64]{1,0:T(1,128)} %bitcast.12, f32[1,64]{1,0:T(1,128)} %bitcast.13), custom_call_target="tpu_custom_call" | custom-call | tf_op jit(solution)/shard_map/send_side/pallas_call | solution.py:283
  3.0 0.0 copy-start
  3.0 91.6 %all_to_all.10.x_ref = bf16[128,48,128]{2,1,0:T(8,128)(2,1)S(1)} all-to-all(bf16[128,48,128]{2,1,0:T(8,128)(2,1)S(1)} %send_side.1), channel_id=1, replica_groups={{148,180,140,172,156,188,132,164,336,368,328,360,344,376,320,352,212,24..., dimensions={0} | all-to-all | bytes 3145728 | tf_op jit(solution)/shard_map/all_to_all | solution.py:340
  94.7 0.0 copy-done
  94.7 4.8 %attend.1 = bf16[128,16,128]{2,1,0:T(8,128)(2,1)S(1)} custom-call(s32[1,9]{1,0:T(1,128)S(1)} %bitcast.8, bf16[128,48,128]{2,1,0:T(8,128)(2,1)S(1)} %all_to_all.10.x_ref), custom_call_target="tpu_custom_call" | custom-call | tf_op jit(solution)/shard_map/attend/pallas_call | solution.py:302
  99.5 40.8 %all_to_all.11.x_ref = bf16[128,16,128]{2,1,0:T(8,128)(2,1)S(1)} all-to-all(bf16[128,16,128]{2,1,0:T(8,128)(2,1)S(1)} %attend.1), channel_id=1, replica_groups={{148,180,140,172,156,188,132,164,80,112,72,104,88,120,64,96,20,52,12,44..., dimensions={0} | all-to-all | bytes 1048576 | tf_op jit(solution)/shard_map/all_to_all | solution.py:340
  140.2 1.3 take_side.1
Async XLA Ops:
  3.0 91.7 %copy-start = (s32[9]{0:T(128)S(1)}, s32[9]{0:T(128)}, u32[]{:S(2)}) copy-start(s32[9]{0:T(128)} %param.9) | copy-start | bytes 112

commit v25 on v18

--- a/solution.py
+++ b/solution.py
@@ -32,6 +32,7 @@
 THEN_Z = [8, 15, 6, 13, 4, 11, 2, 9, 0, 7, 14, 5, 12, 3, 10, 1]
 ORDER_IN = [run_of(z, x, c) for z in FIRST_Z for x in (2, 1, 3, 0) for c in range(2)]
 ORDER_OUT = [run_of(z, x, c) for z in THEN_Z for x in (2, 1, 3, 0) for c in range(2)]
+ORDER_IN, ORDER_OUT = ORDER_IN[1:] + ORDER_IN[:1], ORDER_OUT[1:] + ORDER_OUT[:1]
 PLACE_IN = [ORDER_IN.index(s) for s in range(len(ORDER_IN))]
 PLACE_OUT = [ORDER_OUT.index(s) for s in range(len(ORDER_OUT))]
 

time: 141 us -> 142 us (level)
  no operation moved by 1% of the time
where the time goes in v25:
time: 142 us; the launch traced here: 141 us
  blocking collectives  132 us (93%)
  Pallas kernels  8.56 us (6%)
    all_to_all x2, blocking collectives, exchange(): lax.all_to_all(x, 'run', split_axis=0, concat_axis=0, axis_index_groups=[...  132 us
    pallas_call x1, Pallas kernels, attend_call(): pl.pallas_call(attend_kernel, out_shape=jax.ShapeDtypeStruct((SEQ // TOK,...  4.26 us
    pallas_call x1, Pallas kernels, send_call(): pl.pallas_call(send_kernel, out_shape=jax.ShapeDtypeStruct((HEADS, 48, 12...  3 us

profile of v25, /device:TPU:1, one launch (start us, length us, event | category | flops | bytes accessed | tf_op | source)
XLA Modules:
  0.0 141.0 jit_solution(7701307325279841997)
XLA Ops:
  0.0 3.0 %send_side.1 = bf16[128,48,128]{2,1,0:T(8,128)(2,1)S(1)} custom-call(s32[1,9]{1,0:T(1,128)} %bitcast.7, bf16[32,64,128]{2,1,0:T(8,128)(2,1)} %bitcast.9, bf16[32,64,128]{2,1,0:T(8,128)(2,1)} %bitcast.10, bf16[32,64,128]{2,1,0:T(8,128)(2,1)} %bitcast.11, f32[1,64]{1,0:T(1,128)} %bitcast.12, f32[1,64]{1,0:T(1,128)} %bitcast.13), custom_call_target="tpu_custom_call" | custom-call | tf_op jit(solution)/shard_map/send_side/pallas_call | solution.py:284
  3.0 0.0 copy-start
  3.0 91.8 %all_to_all.10.x_ref = bf16[128,48,128]{2,1,0:T(8,128)(2,1)S(1)} all-to-all(bf16[128,48,128]{2,1,0:T(8,128)(2,1)S(1)} %send_side.1), channel_id=1, replica_groups={{52,12,44,28,60,4,36,464,496,456,488,472,504,448,480,84,116,76,108,92,1..., dimensions={0} | all-to-all | bytes 3145728 | tf_op jit(solution)/shard_map/all_to_all | solution.py:341
  94.8 0.0 copy-done
  94.8 4.3 %attend.1 = bf16[128,16,128]{2,1,0:T(8,128)(2,1)S(1)} custom-call(s32[1,9]{1,0:T(1,128)S(1)} %bitcast.8, bf16[128,48,128]{2,1,0:T(8,128)(2,1)S(1)} %all_to_all.10.x_ref), custom_call_target="tpu_custom_call" | custom-call | tf_op jit(solution)/shard_map/attend/pallas_call | solution.py:303
  99.1 40.6 %all_to_all.11.x_ref = bf16[128,16,128]{2,1,0:T(8,128)(2,1)S(1)} all-to-all(bf16[128,16,128]{2,1,0:T(8,128)(2,1)S(1)} %attend.1), channel_id=1, replica_groups={{52,12,44,28,60,4,36,468,500,460,492,476,508,452,484,400,432,392,424,40..., dimensions={0} | all-to-all | bytes 1048576 | tf_op jit(solution)/shard_map/all_to_all | solution.py:341
  139.7 1.3 take_side.1
Async XLA Ops:
  3.0 91.8 %copy-start = (s32[9]{0:T(128)S(1)}, s32[9]{0:T(128)}, u32[]{:S(2)}) copy-start(s32[9]{0:T(128)} %param.9) | copy-start | bytes 112

commit v26 on v18

--- a/solution.py
+++ b/solution.py
@@ -15,7 +15,7 @@
 PAIRS = BLK // 2
 NBLK = SEQ // BLK
 SRC = BLK // TOK
-LONG, MIDDLE, SHORT = 16, 8, 4
+LONG, MIDDLE, SHORT = 20, 12, 6
 FAR = (NBLK - 2) * (NBLK - 1) // 2 + LONG
 NT = (((1,), (1,)), ((), ()))
 NN = (((1,), (0,)), ((), ()))

time: 141 us -> 141 us (level)
  no operation moved by 1% of the time
where the time goes in v26:
time: 141 us
  blocking collectives  132 us (94%)
  Pallas kernels  9.44 us (7%)
    all_to_all x2, blocking collectives, exchange(): lax.all_to_all(x, 'run', split_axis=0, concat_axis=0, axis_index_groups=[...  132 us
    pallas_call x1, Pallas kernels, attend_call(): pl.pallas_call(attend_kernel, out_shape=jax.ShapeDtypeStruct((SEQ // TOK,...  5.13 us
    pallas_call x1, Pallas kernels, send_call(): pl.pallas_call(send_kernel, out_shape=jax.ShapeDtypeStruct((HEADS, 48, 12...  3 us

profile of v26, /device:TPU:1, one launch (start us, length us, event | category | flops | bytes accessed | tf_op | source)
XLA Modules:
  0.0 141.4 jit_solution(5257927691579918358)
XLA Ops:
  0.0 3.0 %send_side.1 = bf16[128,48,128]{2,1,0:T(8,128)(2,1)S(1)} custom-call(s32[1,9]{1,0:T(1,128)} %bitcast.7, bf16[32,64,128]{2,1,0:T(8,128)(2,1)} %bitcast.9, bf16[32,64,128]{2,1,0:T(8,128)(2,1)} %bitcast.10, bf16[32,64,128]{2,1,0:T(8,128)(2,1)} %bitcast.11, f32[1,64]{1,0:T(1,128)} %bitcast.12, f32[1,64]{1,0:T(1,128)} %bitcast.13), custom_call_target="tpu_custom_call" | custom-call | tf_op jit(solution)/shard_map/send_side/pallas_call | solution.py:283
  3.0 0.0 copy-start
  3.0 92.9 %all_to_all.10.x_ref = bf16[128,48,128]{2,1,0:T(8,128)(2,1)S(1)} all-to-all(bf16[128,48,128]{2,1,0:T(8,128)(2,1)S(1)} %send_side.1), channel_id=1, replica_groups={{20,52,12,44,28,60,4,36,464,496,456,488,472,504,448,480,84,116,76,108,9..., dimensions={0} | all-to-all | bytes 3145728 | tf_op jit(solution)/shard_map/all_to_all | solution.py:340
  95.9 0.0 copy-done
  95.9 5.1 %attend.1 = bf16[128,16,128]{2,1,0:T(8,128)(2,1)S(1)} custom-call(s32[1,9]{1,0:T(1,128)S(1)} %bitcast.8, bf16[128,48,128]{2,1,0:T(8,128)(2,1)S(1)} %all_to_all.10.x_ref), custom_call_target="tpu_custom_call" | custom-call | tf_op jit(solution)/shard_map/attend/pallas_call | solution.py:302
  101.0 39.1 %all_to_all.11.x_ref = bf16[128,16,128]{2,1,0:T(8,128)(2,1)S(1)} all-to-all(bf16[128,16,128]{2,1,0:T(8,128)(2,1)S(1)} %attend.1), channel_id=1, replica_groups={{20,52,12,44,28,60,4,36,468,500,460,492,476,508,452,484,400,432,392,424..., dimensions={0} | all-to-all | bytes 1048576 | tf_op jit(solution)/shard_map/all_to_all | solution.py:340
  140.1 1.3 take_side.1
Async XLA Ops:
  3.0 92.9 %copy-start = (s32[9]{0:T(128)S(1)}, s32[9]{0:T(128)}, u32[]{:S(2)}) copy-start(s32[9]{0:T(128)} %param.9) | copy-start | bytes 112

commit v27 on v26

--- a/solution.py
+++ b/solution.py
@@ -30,8 +30,8 @@
 
 FIRST_Z = [8, 7, 9, 6, 10, 5, 11, 4, 12, 3, 13, 2, 14, 1, 15, 0]
 THEN_Z = [8, 15, 6, 13, 4, 11, 2, 9, 0, 7, 14, 5, 12, 3, 10, 1]
-ORDER_IN = [run_of(z, x, c) for z in FIRST_Z for x in (2, 1, 3, 0) for c in range(2)]
-ORDER_OUT = [run_of(z, x, c) for z in THEN_Z for x in (2, 1, 3, 0) for c in range(2)]
+ORDER_IN = [run_of(z, x, c) for z in FIRST_Z for x in (2, 3, 1, 0) for c in range(2)]
+ORDER_OUT = [run_of(z, x, c) for z in THEN_Z for x in (2, 3, 1, 0) for c in range(2)]
 PLACE_IN = [ORDER_IN.index(s) for s in range(len(ORDER_IN))]
 PLACE_OUT = [ORDER_OUT.index(s) for s in range(len(ORDER_OUT))]
 

time: 141 us -> 141 us (level)
  no operation moved by 1% of the time
where the time goes in v27:
time: 141 us; the launch traced here: 142 us
  blocking collectives  133 us (94%)
  Pallas kernels  8.77 us (6%)
    all_to_all x2, blocking collectives, exchange(): lax.all_to_all(x, 'run', split_axis=0, concat_axis=0, axis_index_groups=[...  133 us
    pallas_call x1, Pallas kernels, attend_call(): pl.pallas_call(attend_kernel, out_shape=jax.ShapeDtypeStruct((SEQ // TOK,...  4.46 us
    pallas_call x1, Pallas kernels, send_call(): pl.pallas_call(send_kernel, out_shape=jax.ShapeDtypeStruct((HEADS, 48, 12...  3 us

profile of v27, /device:TPU:1, one launch (start us, length us, event | category | flops | bytes accessed | tf_op | source)
XLA Modules:
  0.0 141.5 jit_solution(8000268913124318688)
XLA Ops:
  0.0 3.0 %send_side.1 = bf16[128,48,128]{2,1,0:T(8,128)(2,1)S(1)} custom-call(s32[1,9]{1,0:T(1,128)} %bitcast.7, bf16[32,64,128]{2,1,0:T(8,128)(2,1)} %bitcast.9, bf16[32,64,128]{2,1,0:T(8,128)(2,1)} %bitcast.10, bf16[32,64,128]{2,1,0:T(8,128)(2,1)} %bitcast.11, f32[1,64]{1,0:T(1,128)} %bitcast.12, f32[1,64]{1,0:T(1,128)} %bitcast.13), custom_call_target="tpu_custom_call" | custom-call | tf_op jit(solution)/shard_map/send_side/pallas_call | solution.py:283
  3.0 0.0 copy-start
  3.0 93.7 %all_to_all.10.x_ref = bf16[128,48,128]{2,1,0:T(8,128)(2,1)S(1)} all-to-all(bf16[128,48,128]{2,1,0:T(8,128)(2,1)S(1)} %send_side.1), channel_id=1, replica_groups={{20,52,28,60,12,44,4,36,464,496,472,504,456,488,448,480,84,116,92,124,7..., dimensions={0} | all-to-all | bytes 3145728 | tf_op jit(solution)/shard_map/all_to_all | solution.py:340
  96.7 0.0 copy-done
  96.7 4.5 %attend.1 = bf16[128,16,128]{2,1,0:T(8,128)(2,1)S(1)} custom-call(s32[1,9]{1,0:T(1,128)S(1)} %bitcast.8, bf16[128,48,128]{2,1,0:T(8,128)(2,1)S(1)} %all_to_all.10.x_ref), custom_call_target="tpu_custom_call" | custom-call | tf_op jit(solution)/shard_map/attend/pallas_call | solution.py:302
  101.1 39.1 %all_to_all.11.x_ref = bf16[128,16,128]{2,1,0:T(8,128)(2,1)S(1)} all-to-all(bf16[128,16,128]{2,1,0:T(8,128)(2,1)S(1)} %attend.1), channel_id=1, replica_groups={{20,52,28,60,12,44,4,36,468,500,476,508,460,492,452,484,400,432,408,440..., dimensions={0} | all-to-all | bytes 1048576 | tf_op jit(solution)/shard_map/all_to_all | solution.py:340
  140.2 1.3 take_side.1
Async XLA Ops:
  3.0 93.7 %copy-start = (s32[9]{0:T(128)S(1)}, s32[9]{0:T(128)}, u32[]{:S(2)}) copy-start(s32[9]{0:T(128)} %param.9) | copy-start | bytes 112

commit v28 on v26

--- a/solution.py
+++ b/solution.py
@@ -28,7 +28,7 @@
     return ((z % 8 * 2 + c) * 4 + x) * 2 + z // 8
 
 
-FIRST_Z = [8, 7, 9, 6, 10, 5, 11, 4, 12, 3, 13, 2, 14, 1, 15, 0]
+FIRST_Z = [8, 9, 7, 10, 6, 11, 5, 12, 4, 13, 3, 14, 2, 15, 1, 0]
 THEN_Z = [8, 15, 6, 13, 4, 11, 2, 9, 0, 7, 14, 5, 12, 3, 10, 1]
 ORDER_IN = [run_of(z, x, c) for z in FIRST_Z for x in (2, 1, 3, 0) for c in range(2)]
 ORDER_OUT = [run_of(z, x, c) for z in THEN_Z for x in (2, 1, 3, 0) for c in range(2)]

time: 141 us -> 141 us (level)
  no operation moved by 1% of the time
where the time goes in v28:
time: 141 us
  blocking collectives  132 us (94%)
  Pallas kernels  8.77 us (6%)
    all_to_all x2, blocking collectives, exchange(): lax.all_to_all(x, 'run', split_axis=0, concat_axis=0, axis_index_groups=[...  132 us
    pallas_call x1, Pallas kernels, attend_call(): pl.pallas_call(attend_kernel, out_shape=jax.ShapeDtypeStruct((SEQ // TOK,...  4.46 us
    pallas_call x1, Pallas kernels, send_call(): pl.pallas_call(send_kernel, out_shape=jax.ShapeDtypeStruct((HEADS, 48, 12...  3 us

profile of v28, /device:TPU:1, one launch (start us, length us, event | category | flops | bytes accessed | tf_op | source)
XLA Modules:
  0.0 141.2 jit_solution(1344822151357682998)
XLA Ops:
  0.0 3.0 %send_side.1 = bf16[128,48,128]{2,1,0:T(8,128)(2,1)S(1)} custom-call(s32[1,9]{1,0:T(1,128)} %bitcast.7, bf16[32,64,128]{2,1,0:T(8,128)(2,1)} %bitcast.9, bf16[32,64,128]{2,1,0:T(8,128)(2,1)} %bitcast.10, bf16[32,64,128]{2,1,0:T(8,128)(2,1)} %bitcast.11, f32[1,64]{1,0:T(1,128)} %bitcast.12, f32[1,64]{1,0:T(1,128)} %bitcast.13), custom_call_target="tpu_custom_call" | custom-call | tf_op jit(solution)/shard_map/send_side/pallas_call | solution.py:283
  3.0 0.0 copy-start
  3.0 92.9 %all_to_all.10.x_ref = bf16[128,48,128]{2,1,0:T(8,128)(2,1)S(1)} all-to-all(bf16[128,48,128]{2,1,0:T(8,128)(2,1)S(1)} %send_side.1), channel_id=1, replica_groups={{20,52,12,44,28,60,4,36,84,116,76,108,92,124,68,100,464,496,456,488,472..., dimensions={0} | all-to-all | bytes 3145728 | tf_op jit(solution)/shard_map/all_to_all | solution.py:340
  96.0 0.0 copy-done
  96.0 4.5 %attend.1 = bf16[128,16,128]{2,1,0:T(8,128)(2,1)S(1)} custom-call(s32[1,9]{1,0:T(1,128)S(1)} %bitcast.8, bf16[128,48,128]{2,1,0:T(8,128)(2,1)S(1)} %all_to_all.10.x_ref), custom_call_target="tpu_custom_call" | custom-call | tf_op jit(solution)/shard_map/attend/pallas_call | solution.py:302
  100.4 39.5 %all_to_all.11.x_ref = bf16[128,16,128]{2,1,0:T(8,128)(2,1)S(1)} all-to-all(bf16[128,16,128]{2,1,0:T(8,128)(2,1)S(1)} %attend.1), channel_id=1, replica_groups={{20,52,12,44,28,60,4,36,468,500,460,492,476,508,452,484,400,432,392,424..., dimensions={0} | all-to-all | bytes 1048576 | tf_op jit(solution)/shard_map/all_to_all | solution.py:340
  139.9 1.3 take_side.1
Async XLA Ops:
  3.0 93.0 %copy-start = (s32[9]{0:T(128)S(1)}, s32[9]{0:T(128)}, u32[]{:S(2)}) copy-start(s32[9]{0:T(128)} %param.9) | copy-start | bytes 112

commit v29 on v26

--- a/solution.py
+++ b/solution.py
@@ -31,7 +31,7 @@
 FIRST_Z = [8, 7, 9, 6, 10, 5, 11, 4, 12, 3, 13, 2, 14, 1, 15, 0]
 THEN_Z = [8, 15, 6, 13, 4, 11, 2, 9, 0, 7, 14, 5, 12, 3, 10, 1]
 ORDER_IN = [run_of(z, x, c) for z in FIRST_Z for x in (2, 1, 3, 0) for c in range(2)]
-ORDER_OUT = [run_of(z, x, c) for z in THEN_Z for x in (2, 1, 3, 0) for c in range(2)]
+ORDER_OUT = [run_of(z, x, c) for z in THEN_Z for x in (2, 1, 3, 0) for c in (1, 0)]
 PLACE_IN = [ORDER_IN.index(s) for s in range(len(ORDER_IN))]
 PLACE_OUT = [ORDER_OUT.index(s) for s in range(len(ORDER_OUT))]
 

time: 141 us -> 141 us (level)
  no operation moved by 1% of the time
where the time goes in v29:
time: 141 us
  blocking collectives  131 us (93%)
  Pallas kernels  9.44 us (7%)
    all_to_all x2, blocking collectives, exchange(): lax.all_to_all(x, 'run', split_axis=0, concat_axis=0, axis_index_groups=[...  131 us
    pallas_call x1, Pallas kernels, attend_call(): pl.pallas_call(attend_kernel, out_shape=jax.ShapeDtypeStruct((SEQ // TOK,...  5.12 us
    pallas_call x1, Pallas kernels, send_call(): pl.pallas_call(send_kernel, out_shape=jax.ShapeDtypeStruct((HEADS, 48, 12...  3 us

profile of v29, /device:TPU:1, one launch (start us, length us, event | category | flops | bytes accessed | tf_op | source)
XLA Modules:
  0.0 140.8 jit_solution(16405916746918562638)
XLA Ops:
  0.0 3.0 %send_side.1 = bf16[128,48,128]{2,1,0:T(8,128)(2,1)S(1)} custom-call(s32[1,9]{1,0:T(1,128)} %bitcast.7, bf16[32,64,128]{2,1,0:T(8,128)(2,1)} %bitcast.9, bf16[32,64,128]{2,1,0:T(8,128)(2,1)} %bitcast.10, bf16[32,64,128]{2,1,0:T(8,128)(2,1)} %bitcast.11, f32[1,64]{1,0:T(1,128)} %bitcast.12, f32[1,64]{1,0:T(1,128)} %bitcast.13), custom_call_target="tpu_custom_call" | custom-call | tf_op jit(solution)/shard_map/send_side/pallas_call | solution.py:283
  3.0 0.0 copy-start
  3.0 92.9 %all_to_all.10.x_ref = bf16[128,48,128]{2,1,0:T(8,128)(2,1)S(1)} all-to-all(bf16[128,48,128]{2,1,0:T(8,128)(2,1)S(1)} %send_side.1), channel_id=1, replica_groups={{20,52,12,44,28,60,4,36,464,496,456,488,472,504,448,480,84,116,76,108,9..., dimensions={0} | all-to-all | bytes 3145728 | tf_op jit(solution)/shard_map/all_to_all | solution.py:340
  95.9 0.0 copy-done
  95.9 5.1 %attend.1 = bf16[128,16,128]{2,1,0:T(8,128)(2,1)S(1)} custom-call(s32[1,9]{1,0:T(1,128)S(1)} %bitcast.8, bf16[128,48,128]{2,1,0:T(8,128)(2,1)S(1)} %all_to_all.10.x_ref), custom_call_target="tpu_custom_call" | custom-call | tf_op jit(solution)/shard_map/attend/pallas_call | solution.py:302
  101.0 38.5 %all_to_all.11.x_ref = bf16[128,16,128]{2,1,0:T(8,128)(2,1)S(1)} all-to-all(bf16[128,16,128]{2,1,0:T(8,128)(2,1)S(1)} %attend.1), channel_id=1, replica_groups={{52,20,44,12,60,28,36,4,500,468,492,460,508,476,484,452,432,400,424,392..., dimensions={0} | all-to-all | bytes 1048576 | tf_op jit(solution)/shard_map/all_to_all | solution.py:340
  139.5 1.3 take_side.1
Async XLA Ops:
  3.0 92.9 %copy-start = (s32[9]{0:T(128)S(1)}, s32[9]{0:T(128)}, u32[]{:S(2)}) copy-start(s32[9]{0:T(128)} %param.9) | copy-start | bytes 112
